TPU v7x, 32 devices: a whole 2x2x4 slice. The times are simulated.
32 devices in a mesh: dp: 2 (over core), row: 4 (over y, x), col: 4 (over z).
Axes of the slice: x: 2, y: 2, z: 4, core: 2. Of those that a mesh axis runs over, the one named last changes fastest.
Arguments:
- tokens: bfloat16 [4, 768, 2048], P('dp', 'row', 'col'), may hold values from -6 to 6
- segments: int32 [4, 2048], P('dp'), may hold values from 0 to 5, never falling along the last dimension, each value on 1 to 800 neighbouring positions
- labels: int32 [4, 6], P('dp'), may hold values from 0 to 13
- cotangent: bfloat16 [4, 768, 2048], P('dp', 'row', 'col'), may hold values from -6 to 6
- w_qkv: bfloat16 [768, 2304], P('row', 'col'), may hold values from -0.21875 to 0.21875
- b_qkv: float32 [2, 768], P(None, 'col'), may hold values from -0.75 to 0.75
- w_out: bfloat16 [768, 768], P('col', 'row'), may hold values from -2.5 to 2.5
- b_out: float32 [768], P('row'), may hold values from -4 to 4
- ln1_gain: float32 [768], P('row'), may hold values from 0.5 to 1.5
- ln1_bias: float32 [768], P('row'), may hold values from -4 to 4
- w_in: bfloat16 [768, 3072], P('row', 'col'), may hold values from -0.21875 to 0.21875
- b_in: float32 [3072], P('col'), may hold values from -4 to 4
- w_back: bfloat16 [768, 3072], P('row', 'col'), may hold values from -0.109375 to 0.109375
- b_back: float32 [768], P('row'), may hold values from -4 to 4
- ln2_gain: float32 [768], P('row'), may hold values from 0.5 to 1.5
- ln2_bias: float32 [768], P('row'), may hold values from -4 to 4
- s_proj: bfloat16 [768, 128], P('row'), may hold values from -0.21875 to 0.21875
- s_bias: float32 [128], replicated, may hold values from -4 to 4
- s_query: float32 [128], replicated, may hold values from -4 to 4
- s_mid: float32 [128, 128], replicated, may hold values from -0.5 to 0.5
- s_mid_bias: float32 [128], replicated, may hold values from -4 to 4
- s_cls: float32 [128, 14], replicated, may hold values from -0.5 to 0.5
- s_cls_bias: float32 [14], replicated, may hold values from -6 to 6
Outputs:
- out: bfloat16 [4, 768, 2048], P('dp', 'row', 'col')
- logits: float32 [4, 6, 14], P('dp')
- tokens_grad: float32 [4, 768, 2048], P('dp', 'row', 'col')
- w_qkv_grad: float32 [768, 2304], P('row', 'col')
- b_qkv_grad: float32 [2, 768], P(None, 'col')
- w_out_grad: float32 [768, 768], P('col', 'row')
- b_out_grad: float32 [768], P('row')
- ln1_gain_grad: float32 [768], P('row')
- ln1_bias_grad: float32 [768], P('row')
- w_in_grad: float32 [768, 3072], P('row', 'col')
- b_in_grad: float32 [3072], P('col')
- w_back_grad: float32 [768, 3072], P('row', 'col')
- b_back_grad: float32 [768], P('row')
- ln2_gain_grad: float32 [768], P('row')
- ln2_bias_grad: float32 [768], P('row')
- s_proj_grad: float32 [768, 128], P('row')
- s_bias_grad: float32 [128], replicated
- s_query_grad: float32 [128], replicated
- s_mid_grad: float32 [128, 128], replicated
- s_mid_bias_grad: float32 [128], replicated
- s_cls_grad: float32 [128, 14], replicated
- s_cls_bias_grad: float32 [14], replicated
Inputs may be any that keep to these rules, and one draw needn't show every extreme that they name: `segments`: in each sequence the ids never fall, every id from 0 to 5 is present, every document has 1 to 800 tokens, and some document has exactly 800.
All inputs are finite; a program needn't handle non-finite values.
Results may differ from a plain program's by a relative error of at most 0.015.
Values may be sent and summed in bfloat16 or wider, within the bound.
A program may use at most 192 MiB of HBM per device.

v0:
```python
import jax
import jax.numpy as jnp
from jax import lax
from jax.sharding import PartitionSpec as P

HD = 64
SH = 2
SHD = 64


norm_eps = 1e-06
masked_value = -1e30
highest = lax.Precision.HIGHEST


def as_sent(shard):

    def short(part):
        return part.astype(jnp.bfloat16) if part.dtype == jnp.float32 else part

    return jax.tree.map(short, shard)


def merged(part, axis, combine):
    gathered = jax.tree.map(lambda a: lax.all_gather(a, axis), part)

    def take(source):
        return jax.tree.map(lambda a: lax.dynamic_index_in_dim(a, source, 0, False), gathered)

    return lax.fori_loop(
        1, lax.axis_size(axis), lambda source, state: combine(state, take(source)), take(0)
    )


def gather_cols(values):
    return lax.all_gather(values, "col", axis=0, tiled=True)


def gather_rows(values):
    return lax.all_gather(values, "row", axis=0, tiled=True)


def reduce_rows(term_fn, rows_out):
    return lax.psum_scatter(
        term_fn(jnp.int32(0), lax.axis_size("row") * rows_out),
        "row",
        scatter_dimension=0,
        tiled=True,
    )


def reduce_cols(term_fn, rows_out):
    return lax.psum_scatter(
        term_fn(jnp.int32(0), lax.axis_size("col") * rows_out),
        "col",
        scatter_dimension=0,
        tiled=True,
    )


def sum_features(values):
    return lax.psum(values, "row")


def reduce_all(model_grads, token_grads):
    model_grads = jax.tree.map(
        lambda part: part.astype(jnp.float32), lax.psum(as_sent(model_grads), "dp")
    )
    token_grads = lax.psum(token_grads, ("dp", "col"))
    return (model_grads, token_grads)


def product_rows(gathered, matrix, contract):

    def term_fn(offset, amount):
        return lax.dot_general(
            gathered, matrix, (((1,), (contract,)), ((), ())), preferred_element_type=jnp.float32
        )

    return term_fn


def outer_grad(gathered, grads_all):
    return lax.dot_general(
        gathered, grads_all, (((0,), (0,)), ((), ())), preferred_element_type=jnp.float32
    )


def normalize(values, width):
    total_sum, total_sq = sum_features(
        (jnp.sum(values, axis=-1), jnp.sum(values * values, axis=-1))
    )
    mean_v = total_sum / width
    spread = total_sq / width - mean_v * mean_v
    inv_std = lax.rsqrt(spread + norm_eps)
    return ((values - mean_v[:, None]) * inv_std[:, None], inv_std)


def normalize_back(grad_hat, normed, inv_std, width):
    total_g, total_gn = sum_features(
        (jnp.sum(grad_hat, axis=-1), jnp.sum(grad_hat * normed, axis=-1))
    )
    return inv_std[:, None] * (
        grad_hat - total_g[:, None] / width - normed * (total_gn[:, None] / width)
    )


def gelu_exact(values):
    return jax.nn.gelu(values, approximate=False)


def masked_scores(queries, key_rows, query_segs, key_segs, score_scale):
    scores = (
        jnp.einsum("qhd,khd->hqk", queries, key_rows, preferred_element_type=jnp.float32)
        * score_scale
    )
    same_doc = query_segs[:, None] == key_segs[None, :]
    return jnp.where(same_doc[None], scores, masked_value)


def combine_pool(part_one, part_two):
    top_a, total_a, sum_a = part_one
    top_b, total_b, sum_b = part_two
    row_top = jnp.maximum(top_a, top_b)
    factor_a = jnp.exp(top_a - row_top)
    factor_b = jnp.exp(top_b - row_top)
    return (
        row_top,
        total_a * factor_a + total_b * factor_b,
        sum_a * factor_a[:, :, None] + sum_b * factor_b[:, :, None],
    )


def local(
    tokens,
    segments,
    labels,
    cotangent,
    w_qkv,
    b_qkv,
    w_out,
    b_out,
    ln1_gain,
    ln1_bias,
    w_in,
    b_in,
    w_back,
    b_back,
    ln2_gain,
    ln2_bias,
    s_proj,
    s_bias,
    s_query,
    s_mid,
    s_mid_bias,
    s_cls,
    s_cls_bias,
):
    micro_count, width_row, cols_local = tokens.shape
    rows_count = lax.axis_size("row")
    cols_count = lax.axis_size("col")
    seq_len = cols_local * cols_count
    rows_local = seq_len // rows_count
    width = width_row * rows_count
    row_index = lax.axis_index("row")
    col_index = lax.axis_index("col")
    width_col = b_qkv.shape[1]
    heads_dev = width_col // HD
    docs_count = labels.shape[1]
    class_count = s_cls.shape[1]
    student_width = s_proj.shape[1]
    score_scale = HD ** (-0.5)
    pool_scale = SHD ** (-0.5)
    query_heads = s_query.reshape(SH, SHD)
    doc_ids = jnp.arange(docs_count, dtype=jnp.int32)
    class_ids = jnp.arange(class_count, dtype=jnp.int32)
    qkv_offsets = (
        jnp.stack([b_qkv[0], jnp.zeros_like(b_qkv[0]), b_qkv[1]])
        .reshape(3, heads_dev, HD)
        .transpose(1, 0, 2)
    )
    model_acc = None
    token_acc = None
    out_list = []
    logit_list = []
    grad_list = []
    for micro_at in range(micro_count):
        tok_rows = tokens[micro_at].T
        seg_all = segments[micro_at]
        seg_rows = lax.dynamic_slice_in_dim(seg_all, row_index * rows_local, rows_local)
        seg_cols = lax.dynamic_slice_in_dim(seg_all, col_index * cols_local, cols_local)
        x_all = gather_cols(tok_rows)
        qkv_rows = reduce_rows(product_rows(x_all, w_qkv, 0), rows_local).reshape(
            rows_local, heads_dev, 3, HD
        )
        qkv_low = (qkv_rows + qkv_offsets[None]).astype(jnp.bfloat16)
        kv_all = gather_rows(qkv_low[:, :, 1:])
        queries = qkv_low[:, :, 0]
        key_rows = kv_all[:, :, 0]
        value_rows = kv_all[:, :, 1]
        scores = masked_scores(queries, key_rows, seg_rows, seg_all, score_scale)
        row_top = jnp.max(scores, axis=-1, keepdims=True)
        exp_scores = jnp.exp(scores - row_top)
        row_total = jnp.sum(exp_scores, axis=-1, keepdims=True)
        probs_low = (exp_scores / row_total).astype(jnp.bfloat16)
        context = jnp.einsum(
            "hqk,khd->qhd", probs_low, value_rows, preferred_element_type=jnp.float32
        )
        context = context.reshape(rows_local, width_col).astype(jnp.bfloat16)
        ctx_all = gather_rows(context)
        attn_out = reduce_cols(product_rows(ctx_all, w_out, 0), cols_local) + b_out
        normed_one, inv_one = normalize(tok_rows.astype(jnp.float32) + attn_out, width)
        hidden_one = normed_one * ln1_gain + ln1_bias
        hidden_low = hidden_one.astype(jnp.bfloat16)
        h1_all = gather_cols(hidden_low)
        pre_act = reduce_rows(product_rows(h1_all, w_in, 0), rows_local) + b_in
        act_all = gather_rows(gelu_exact(pre_act).astype(jnp.bfloat16))
        ffn_out = reduce_cols(product_rows(act_all, w_back, 1), cols_local) + b_back
        normed_two, inv_two = normalize(hidden_one + ffn_out, width)
        layer_out = (normed_two * ln2_gain + ln2_bias).astype(jnp.bfloat16)
        out_list.append(layer_out.T)
        proj_part = jnp.dot(layer_out, s_proj, preferred_element_type=jnp.float32)
        (proj_sum,) = sum_features((proj_part,))
        student_h = proj_sum + s_bias
        head_parts = student_h.reshape(cols_local, SH, SHD)
        pool_logit = jnp.sum(head_parts * query_heads, axis=-1) * pool_scale
        member = (seg_cols[:, None] == doc_ids[None, :])[:, :, None]
        masked = jnp.where(member, pool_logit[:, None, :], masked_value)
        local_top = jnp.max(masked, axis=0)
        local_exp = jnp.where(member, jnp.exp(masked - local_top[None]), 0.0)
        local_total = jnp.sum(local_exp, axis=0)
        local_sum = jnp.einsum("tdh,thk->dhk", local_exp, head_parts, precision=highest)
        doc_top, doc_total, doc_sum = merged(
            (local_top, local_total, local_sum), "col", combine_pool
        )
        pooled_heads = doc_sum / doc_total[:, :, None]
        pooled = pooled_heads.reshape(docs_count, student_width)
        middle = jnp.tanh(jnp.dot(pooled, s_mid, precision=highest) + s_mid_bias)
        logit_rows = jnp.dot(middle, s_cls, precision=highest) + s_cls_bias
        logit_list.append(logit_rows)
        logit_top = jnp.max(logit_rows, axis=-1, keepdims=True)
        logit_exp = jnp.exp(logit_rows - logit_top)
        one_hot = (labels[micro_at][:, None] == class_ids[None, :]).astype(jnp.float32)
        d_logits = logit_exp / jnp.sum(logit_exp, axis=-1, keepdims=True) - one_hot
        g_cls = jnp.dot(middle.T, d_logits, precision=highest)
        g_cls_bias = jnp.sum(d_logits, axis=0)
        d_middle = jnp.dot(d_logits, s_cls.T, precision=highest) * (1.0 - middle * middle)
        g_mid = jnp.dot(pooled.T, d_middle, precision=highest)
        g_mid_bias = jnp.sum(d_middle, axis=0)
        d_pooled = jnp.dot(d_middle, s_mid.T, precision=highest).reshape(docs_count, SH, SHD)
        shares = jnp.where(member, jnp.exp(masked - doc_top[None]), 0.0) / doc_total[None]
        d_share = jnp.einsum("dhk,thk->tdh", d_pooled, head_parts, precision=highest)
        base_term = jnp.sum(d_pooled * pooled_heads, axis=-1)
        d_pool_logit = jnp.sum(shares * (d_share - base_term[None]), axis=1)
        d_heads = jnp.einsum("tdh,dhk->thk", shares, d_pooled, precision=highest)
        d_heads = d_heads + d_pool_logit[:, :, None] * query_heads[None] * pool_scale
        g_query = (jnp.sum(d_pool_logit[:, :, None] * head_parts, axis=0) * pool_scale).reshape(
            student_width
        )
        d_student = d_heads.reshape(cols_local, student_width)
        g_sbias = jnp.sum(d_student, axis=0)
        g_sproj = jnp.dot(layer_out.astype(jnp.float32).T, d_student, precision=highest)
        d_out = cotangent[micro_at].astype(jnp.float32).T
        g_ln2_gain = jnp.sum(d_out * normed_two, axis=0)
        g_ln2_bias = jnp.sum(d_out, axis=0)
        d_resid_two = normalize_back(d_out * ln2_gain, normed_two, inv_two, width)
        d_ffn_low = d_resid_two.astype(jnp.bfloat16)
        g_back_bias = jnp.sum(d_ffn_low.astype(jnp.float32), axis=0)
        d_ffn = gather_cols(d_ffn_low)
        g_back = outer_grad(d_ffn, act_all)
        d_act = reduce_rows(product_rows(d_ffn, w_back, 0), rows_local)
        gelu_out, gelu_fn = jax.vjp(gelu_exact, pre_act)
        d_pre = gelu_fn(d_act)[0].astype(jnp.bfloat16)
        d_pre_all = gather_rows(d_pre)
        g_in_bias = jnp.sum(d_pre_all.astype(jnp.float32), axis=0)
        g_in = outer_grad(h1_all, d_pre_all)
        d_hidden_one = d_resid_two + reduce_cols(product_rows(d_pre_all, w_in, 1), cols_local)
        ffn_fresh = (g_in, g_in_bias, g_back)
        g_ln1_gain = jnp.sum(d_hidden_one * normed_one, axis=0)
        g_ln1_bias = jnp.sum(d_hidden_one, axis=0)
        d_resid_one = normalize_back(d_hidden_one * ln1_gain, normed_one, inv_one, width)
        d_attn_all = gather_cols(d_resid_one.astype(jnp.bfloat16))
        g_out_bias = jnp.sum(d_attn_all.astype(jnp.float32), axis=0)
        g_out = outer_grad(ctx_all, d_attn_all)
        d_context = reduce_rows(product_rows(d_attn_all, w_out, 1), rows_local)
        d_context = d_context.astype(jnp.bfloat16).reshape(rows_local, heads_dev, HD)
        scores_again = masked_scores(queries, key_rows, seg_rows, seg_all, score_scale)
        probs_f = jnp.exp(scores_again - row_top) / row_total
        probs_again = probs_f.astype(jnp.bfloat16)
        d_probs = jnp.einsum(
            "qhd,khd->hqk", d_context, value_rows, preferred_element_type=jnp.float32
        )
        delta_sum = jnp.sum(probs_f * d_probs, axis=-1, keepdims=True)
        d_scores = (probs_f * (d_probs - delta_sum)).astype(jnp.bfloat16)
        d_queries = (
            jnp.einsum("hqk,khd->qhd", d_scores, key_rows, preferred_element_type=jnp.float32)
            * score_scale
        )
        d_keys = (
            jnp.einsum("hqk,qhd->khd", d_scores, queries, preferred_element_type=jnp.float32)
            * score_scale
        )
        d_values = jnp.einsum(
            "hqk,qhd->khd", probs_again, d_context, preferred_element_type=jnp.float32
        )
        kv_terms = jnp.stack([d_keys, d_values], axis=2)
        kv_grads = lax.psum_scatter(
            kv_terms.astype(jnp.bfloat16), "row", scatter_dimension=0, tiled=True
        ).astype(jnp.float32)
        d_qkv = jnp.concatenate([d_queries[:, :, None], kv_grads], axis=2)
        d_qkv = d_qkv.astype(jnp.bfloat16).reshape(rows_local, 3 * width_col)
        d_qkv_all = gather_rows(d_qkv)
        slot_sums = jnp.sum(d_qkv_all.astype(jnp.float32), axis=0).reshape(heads_dev, 3, HD)
        g_qkv_bias = jnp.stack(
            [slot_sums[:, 0].reshape(width_col), slot_sums[:, 2].reshape(width_col)]
        )
        g_qkv = outer_grad(x_all, d_qkv_all)
        d_tokens = d_resid_one + reduce_cols(product_rows(d_qkv_all, w_qkv, 1), cols_local)
        grad_list.append(d_tokens.T)
        model_fresh = (
            g_qkv,
            g_qkv_bias,
            g_out,
            g_out_bias,
            g_mid,
            g_mid_bias,
            g_cls,
            g_cls_bias,
        ) + tuple(ffn_fresh)
        token_fresh = (
            g_ln1_gain,
            g_ln1_bias,
            g_ln2_gain,
            g_ln2_bias,
            g_sproj,
            g_sbias,
            g_query,
            g_back_bias,
        )
        if model_acc is None:
            model_acc, token_acc = (model_fresh, token_fresh)
        else:
            model_acc = jax.tree.map(jnp.add, model_acc, model_fresh)
            token_acc = jax.tree.map(jnp.add, token_acc, token_fresh)
    model_acc, token_acc = reduce_all(model_acc, token_acc)
    return (
        jnp.stack(out_list),
        jnp.stack(logit_list),
        jnp.stack(grad_list),
        model_acc[0],
        model_acc[1],
        model_acc[2],
        model_acc[3],
        token_acc[0],
        token_acc[1],
        model_acc[8],
        model_acc[9],
        model_acc[10],
        token_acc[7],
        token_acc[2],
        token_acc[3],
        token_acc[4],
        token_acc[5],
        token_acc[6],
        model_acc[4],
        model_acc[5],
        model_acc[6],
        model_acc[7],
    )


def solution(mesh):
    placed = (
        P("dp", "row", "col"),
        P("dp", None),
        P("dp", None),
        P("dp", "row", "col"),
        P("row", "col"),
        P(None, "col"),
        P("col", "row"),
        P("row"),
        P("row"),
        P("row"),
        P("row", "col"),
        P("col"),
        P("row", "col"),
        P("row"),
        P("row"),
        P("row"),
        P("row", None),
        P(),
        P(),
        P(),
        P(),
        P(),
        P(),
    )
    return jax.shard_map(
        local,
        mesh=mesh,
        in_specs=placed,
        out_specs=(
            P("dp", "row", "col"),
            P("dp", None, None),
            P("dp", "row", "col"),
            P("row", "col"),
            P(None, "col"),
            P("col", "row"),
            P("row"),
            P("row"),
            P("row"),
            P("row", "col"),
            P("col"),
            P("row", "col"),
            P("row"),
            P("row"),
            P("row"),
            P("row", None),
            P(),
            P(),
            P(),
            P(),
            P(),
            P(),
        ),
        check_vma=False,
    )
```

profile of v0, /device:TPU:0, one launch (start us, length us, event | category | flops | bytes accessed | tf_op | source)
XLA Modules:
  0.0 1450.3 jit_solution(8261347825728458767)
XLA Ops:
  8.4 21.3 %all_gather.95 = bf16[2048,192]{0,1:T(8,128)(2,1)S(1)} all-gather(bf16[512,192]{0,1:T(8,128)(2,1)S(1)} %get-tuple-element.604), channel_id=1, replica_groups=mesh['dp'=2,'row'=4,'col'=4] {'col'}, dimensions={0}, use_global_device_ids=true | all-gather | bytes 983040 | tf_op jit(solution)/shard_map/all_gather | solution.py:36
  33.7 17.7 %all_gather.90 = bf16[2048,192]{0,1:T(8,128)(2,1)S(1)} all-gather(bf16[512,192]{0,1:T(8,128)(2,1)S(1)} %get-tuple-element.603), channel_id=1, replica_groups=mesh['dp'=2,'row'=4,'col'=4] {'col'}, dimensions={0}, use_global_device_ids=true | all-gather | bytes 983040 | tf_op jit(solution)/shard_map/all_gather | solution.py:36
  56.2 34.0 %reduce-scatter.27.cloned.1.call-done = f32[512,576]{0,1:T(8,128)} async-done(((f32[2048,576]{0,1:T(8,128)}), f32[512,576]{0,1:T(8,128)}) %reduce-scatter.27.cloned.1.call-update) | async-done | bytes 1179664 | tf_op jit(solution)/shard_map/reduce_scatter | solution.py:44
  90.1 60.0 %reduce-scatter.19.cloned.1.call-done = f32[512,576]{0,1:T(8,128)} async-done(((f32[2048,576]{0,1:T(8,128)}), f32[512,576]{0,1:T(8,128)}) %reduce-scatter.19.cloned.1.call-update) | async-done | bytes 1179664 | tf_op jit(solution)/shard_map/reduce_scatter | solution.py:44
  155.6 28.1 %all-gather.23.cloned.1.call-done = bf16[2048,3,2,64]{0,3,1,2:T(8,128)(2,1)} async-done(((bf16[512,3,2,64]{0,3,1,2:T(8,128)(2,1)}), bf16[2048,3,2,64]{0,3,1,2:T(8,128)(2,1)}) %all-gather.23.cloned.1.call-update) | async-done | bytes 1572880 | tf_op jit(solution)/shard_map/all_gather | solution.py:40
  183.7 9.9 fusion.190
  193.6 7.1 fusion.64
  200.6 16.3 %all_gather.97 = bf16[2048,192]{0,1:T(8,128)(2,1)S(1)} all-gather(bf16[512,192]{0,1:T(8,128)(2,1)S(1)} %bitcast.396), channel_id=1, replica_groups=mesh['dp'=2,'row'=4,'col'=4] {'row'}, dimensions={0}, use_global_device_ids=true | all-gather | bytes 983040 | tf_op jit(solution)/shard_map/all_gather | solution.py:40
  220.4 9.9 fusion.189
  230.4 6.9 fusion.61
  237.3 10.9 all_gather.92
  250.7 7.3 reduce-scatter.29.cloned.1.call-done
  258.0 36.5 %reduce-scatter.21.cloned.1.call-done = f32[512,192]{0,1:T(8,128)} async-done(((f32[2048,192]{0,1:T(8,128)}), f32[512,192]{0,1:T(8,128)}) %reduce-scatter.21.cloned.1.call-update) | async-done | bytes 393232 | tf_op jit(solution)/shard_map/reduce_scatter | solution.py:53
  295.9 10.1 all-reduce.4
  306.2 17.4 %all_gather.98 = bf16[2048,192]{0,1:T(8,128)(2,1)S(1)} all-gather(bf16[512,192]{0,1:T(8,128)(2,1)S(1)} %get-tuple-element.625), channel_id=1, replica_groups=mesh['dp'=2,'row'=4,'col'=4] {'col'}, dimensions={0}, use_global_device_ids=true | all-gather | bytes 983040 | tf_op jit(solution)/shard_map/all_gather | solution.py:36
  328.4 17.3 %all_gather.93 = bf16[2048,192]{0,1:T(8,128)(2,1)S(1)} all-gather(bf16[512,192]{0,1:T(8,128)(2,1)S(1)} %get-tuple-element.624), channel_id=1, replica_groups=mesh['dp'=2,'row'=4,'col'=4] {'col'}, dimensions={0}, use_global_device_ids=true | all-gather | bytes 983040 | tf_op jit(solution)/shard_map/all_gather | solution.py:36
  346.6 3.8 fusion.199
  350.9 45.4 %reduce-scatter.31.cloned.1.call-done = f32[512,768]{1,0:T(8,128)} async-done(((f32[2048,768]{1,0:T(8,128)}), f32[512,768]{1,0:T(8,128)}) %reduce-scatter.31.cloned.1.call-update) | async-done | bytes 1572880 | tf_op jit(solution)/shard_map/reduce_scatter | solution.py:44
  396.3 73.0 %reduce-scatter.23.cloned.1.call-done = f32[512,768]{1,0:T(8,128)} async-done(((f32[2048,768]{1,0:T(8,128)}), f32[512,768]{1,0:T(8,128)}) %reduce-scatter.23.cloned.1.call-update) | async-done | bytes 1572880 | tf_op jit(solution)/shard_map/reduce_scatter | solution.py:44
  469.3 9.1 multiply_convert_fusion.3
  479.1 43.4 %all-gather.25.cloned.1.call-done = bf16[2048,768]{1,0:T(8,128)(2,1)} async-done(((bf16[512,768]{1,0:T(8,128)(2,1)}), bf16[2048,768]{1,0:T(8,128)(2,1)}) %all-gather.25.cloned.1.call-update) | async-done | bytes 3145744 | tf_op jit(solution)/shard_map/all_gather | solution.py:40
  522.5 4.2 fusion.204
  526.8 41.8 %all-gather.21.cloned.1.call-done = bf16[2048,768]{1,0:T(8,128)(2,1)} async-done(((bf16[512,768]{1,0:T(8,128)(2,1)}), bf16[2048,768]{1,0:T(8,128)(2,1)}) %all-gather.21.cloned.1.call-update) | async-done | bytes 3145744 | tf_op jit(solution)/shard_map/all_gather | solution.py:40
  568.6 4.2 fusion.200
  572.9 33.5 %reduce-scatter.33.cloned.1.call-done = f32[512,192]{0,1:T(8,128)} async-done(((f32[2048,192]{0,1:T(8,128)}), f32[512,192]{0,1:T(8,128)}) %reduce-scatter.33.cloned.1.call-update) | async-done | bytes 393232 | tf_op jit(solution)/shard_map/reduce_scatter | solution.py:53
  606.4 36.5 %reduce-scatter.25.cloned.1.call-done = f32[512,192]{0,1:T(8,128)} async-done(((f32[2048,192]{0,1:T(8,128)}), f32[512,192]{0,1:T(8,128)}) %reduce-scatter.25.cloned.1.call-update) | async-done | bytes 393232 | tf_op jit(solution)/shard_map/reduce_scatter | solution.py:53
  644.3 10.0 all-reduce.3
  655.3 8.0 all-reduce.2
  664.4 16.6 %all_gather.116 = bf16[2048,192]{0,1:T(8,128)(2,1)S(1)} all-gather(bf16[512,192]{0,1:T(8,128)(2,1)S(1)} %get-tuple-element.599), channel_id=1, replica_groups=mesh['dp'=2,'row'=4,'col'=4] {'col'}, dimensions={0}, use_global_device_ids=true | all-gather | bytes 983040 | tf_op jit(solution)/shard_map/all_gather | solution.py:36
  685.7 16.5 %all_gather.112 = bf16[2048,192]{0,1:T(8,128)(2,1)S(1)} all-gather(bf16[512,192]{0,1:T(8,128)(2,1)S(1)} %get-tuple-element.585), channel_id=1, replica_groups=mesh['dp'=2,'row'=4,'col'=4] {'col'}, dimensions={0}, use_global_device_ids=true | all-gather | bytes 983040 | tf_op jit(solution)/shard_map/all_gather | solution.py:36
  703.1 3.8 fusion.207
  707.0 47.5 %reduce-scatter.45.cloned.1.call-done = f32[512,768]{1,0:T(8,128)} async-done(((f32[2048,768]{1,0:T(8,128)}), f32[512,768]{1,0:T(8,128)}) %reduce-scatter.45.cloned.1.call-update) | async-done | bytes 1572880 | tf_op jit(solution)/shard_map/reduce_scatter | solution.py:44
  754.5 72.9 %reduce-scatter.35.cloned.1.call-done = f32[512,768]{1,0:T(8,128)} async-done(((f32[2048,768]{1,0:T(8,128)}), f32[512,768]{1,0:T(8,128)}) %reduce-scatter.35.cloned.1.call-update) | async-done | bytes 1572880 | tf_op jit(solution)/shard_map/reduce_scatter | solution.py:44
  827.4 5.9 add_convert_fusion.1
  833.9 43.4 %all-gather.31.cloned.1.call-done = bf16[2048,768]{1,0:T(8,128)(2,1)} async-done(((bf16[512,768]{1,0:T(8,128)(2,1)}), bf16[2048,768]{1,0:T(8,128)(2,1)}) %all-gather.31.cloned.1.call-update) | async-done | bytes 3145744 | tf_op jit(solution)/shard_map/all_gather | solution.py:40
  877.3 4.2 fusion.210
  881.6 41.9 %all-gather.27.cloned.1.call-done = bf16[2048,768]{1,0:T(8,128)(2,1)} async-done(((bf16[512,768]{1,0:T(8,128)(2,1)}), bf16[2048,768]{1,0:T(8,128)(2,1)}) %all-gather.27.cloned.1.call-update) | async-done | bytes 3145744 | tf_op jit(solution)/shard_map/all_gather | solution.py:40
  923.4 4.3 fusion.208
  927.8 33.2 %reduce-scatter.47.cloned.1.call-done = f32[512,192]{0,1:T(8,128)} async-done(((f32[2048,192]{0,1:T(8,128)}), f32[512,192]{0,1:T(8,128)}) %reduce-scatter.47.cloned.1.call-update) | async-done | bytes 393232 | tf_op jit(solution)/shard_map/reduce_scatter | solution.py:53
  962.5 35.0 %reduce-scatter.37.cloned.1.call-done = f32[512,192]{0,1:T(8,128)} async-done(((f32[2048,192]{0,1:T(8,128)}), f32[512,192]{0,1:T(8,128)}) %reduce-scatter.37.cloned.1.call-update) | async-done | bytes 393232 | tf_op jit(solution)/shard_map/reduce_scatter | solution.py:53
  999.0 10.0 all-reduce.1
  1009.3 17.6 %all_gather.114 = bf16[2048,192]{0,1:T(8,128)(2,1)S(1)} all-gather(bf16[512,192]{0,1:T(8,128)(2,1)S(1)} %get-tuple-element.636), channel_id=1, replica_groups=mesh['dp'=2,'row'=4,'col'=4] {'col'}, dimensions={0}, use_global_device_ids=true | all-gather | bytes 983040 | tf_op jit(solution)/shard_map/all_gather | solution.py:36
  1029.5 17.3 %all_gather.118 = bf16[2048,192]{0,1:T(8,128)(2,1)S(1)} all-gather(bf16[512,192]{0,1:T(8,128)(2,1)S(1)} %get-tuple-element.637), channel_id=1, replica_groups=mesh['dp'=2,'row'=4,'col'=4] {'col'}, dimensions={0}, use_global_device_ids=true | all-gather | bytes 983040 | tf_op jit(solution)/shard_map/all_gather | solution.py:36
  1049.3 9.2 reduce-scatter.39.cloned.1.call-done
  1059.6 10.3 multiply_reduce_fusion.1
  1072.2 6.2 multiply_convert_fusion.1
  1086.6 5.9 reduce-scatter.49.cloned.1.call-done
  1093.5 6.0 fusion.34
  1099.6 9.9 multiply_reduce_fusion
  1109.5 6.1 multiply_convert_fusion
  1125.8 4.4 fusion.57
  1146.5 29.2 %all-reduce.14.cloned.1.call-done = (f32[512,128]{1,0:T(8,128)}, f32[512,128]{1,0:T(8,128)}) async-done(((f32[512,128]{1,0:T(8,128)}, f32[512,128]{1,0:T(8,128)}), (f32[512,128]{1,0:T(8,128)}, f32[512,128]{1,0:T(8,128)})) %all-reduce.14.cloned.1.call-update) | async-done | bytes 524304 | tf_op jit(solution)/shard_map/psum | solution.py:62
  1178.2 4.8 fusion.72
  1183.1 26.7 %reduce-scatter.51.cloned.1.call-done = bf16[512,3,2,64]{0,3,1,2:T(8,128)(2,1)} async-done(((bf16[2048,3,2,64]{0,3,1,2:T(8,128)(2,1)}), bf16[512,3,2,64]{0,3,1,2:T(8,128)(2,1)}) %reduce-scatter.51.cloned.1.call-update) | async-done | bytes 393232 | tf_op jit(solution)/shard_map/reduce_scatter | solution.py:307
  1212.3 13.2 all-gather.2
  1225.7 10.9 all-gather.7
  1236.6 7.6 all-gather.6
  1252.8 36.2 %all-gather.33.cloned.1.call-done = bf16[2048,576]{0,1:T(8,128)(2,1)} async-done(((bf16[512,576]{0,1:T(8,128)(2,1)}), bf16[2048,576]{0,1:T(8,128)(2,1)}) %all-gather.33.cloned.1.call-update) | async-done | bytes 2359312 | tf_op jit(solution)/shard_map/all_gather | solution.py:40
  1297.0 13.2 all-gather.5
  1310.2 10.9 all-gather.9
  1321.1 7.9 all-gather.8
  1350.2 17.3 %all-reduce = (f32[192]{0:T(256)}, f32[192]{0:T(256)}, f32[192]{0:T(256)}, f32[192]{0:T(256)}, f32[192]{0:T(256)}, /*index=5*/f32[128]{0:T(128)}, f32[128]{0:T(128)}) all-reduce(f32[192]{0:T(256)S(1)} %copy-done.123, f32[192]{0:T(256)S(1)} %copy-done.122, ...), channel_id=1, replica_groups=mesh['dp'=2,'row'=4,'col'=4] {'dp','col'}, use_global_device_ids=true, to_apply=%region_78.79 | all-reduce | flops 1216 | bytes 9728 | tf_op jit(solution)/shard_map/psum | solution.py:69
  1370.6 4.2 all-reduce.6
  1390.5 51.3 %all-reduce.12.cloned.1.call-done = f32[192,128]{1,0:T(8,128)} async-done(((f32[192,128]{1,0:T(8,128)}), f32[192,128]{1,0:T(8,128)}) %all-reduce.12.cloned.1.call-update) | async-done | bytes 98320 | tf_op jit(solution)/shard_map/psum | solution.py:69
  (570 shorter events, 150.8 us)
Async XLA Ops:
  7.2 515.3 %copy-start = (bf16[192,768]{1,0:T(8,128)(2,1)S(1)}, bf16[192,768]{1,0:T(8,128)(2,1)}, u32[]{:S(2)}) copy-start(bf16[192,768]{1,0:T(8,128)(2,1)} %param.39) | copy-start | bytes 884740
  7.2 82.9 %reduce-scatter.27.cloned.1.call-start = ((), (), s32[]{:S(2)}) async-start(), calls=%async_computation.24 | async-start | bytes 5898240 | tf_op jit(solution)/shard_map/reduce_scatter | solution.py:44
  33.6 116.4 %reduce-scatter.19.cloned.1.call-start = ((), (), s32[]{:S(2)}) async-start(), calls=%async_computation.18 | async-start | bytes 5898240 | tf_op jit(solution)/shard_map/reduce_scatter | solution.py:44
  55.3 128.3 %all-gather.23.cloned.1.call-start = ((), (), s32[]{:S(2)}) async-start(), calls=%async_computation.25 | async-start | bytes 1966080 | tf_op jit(solution)/shard_map/all_gather | solution.py:40
  151.9 68.5 %copy-start.52 = (bf16[512,3,3,64]{0,3,1,2:T(8,128)(2,1)}, bf16[512,3,3,64]{0,3,1,2:T(8,128)(2,1)S(1)}, u32[]{:S(2)}) copy-start(bf16[512,3,3,64]{0,3,1,2:T(8,128)(2,1)S(1)} %get-tuple-element.611) | copy-start | bytes 1769476
  152.8 67.6 %all-gather.19.cloned.1.call-start = ((), (), s32[]{:S(2)}) async-start(), calls=%async_computation.19 | async-start | bytes 1966080 | tf_op jit(solution)/shard_map/all_gather | solution.py:40
  155.5 102.5 %reduce-scatter.29.cloned.1.call-start = ((), (), s32[]{:S(2)}) async-start(), calls=%async_computation.26 | async-start | bytes 1966080 | tf_op jit(solution)/shard_map/reduce_scatter | solution.py:53
  219.5 75.0 %reduce-scatter.21.cloned.1.call-start = ((), (), s32[]{:S(2)}) async-start(), calls=%async_computation.20 | async-start | bytes 1966080 | tf_op jit(solution)/shard_map/reduce_scatter | solution.py:53
  249.0 45.4 %copy-start.54 = (bf16[2,192,512]{2,1,0:T(8,128)(2,1)S(1)}, bf16[2,192,512]{2,1,0:T(8,128)(2,1)}, u32[]{:S(2)}) copy-start(bf16[2,192,512]{2,1,0:T(8,128)(2,1)} %param.27) | copy-start | bytes 1179652
  249.0 45.4 %copy-start.139 = (f32[192]{0:T(256)S(1)}, f32[192]{0:T(256)}, u32[]{:S(2)}) copy-start(f32[192]{0:T(256)} %param.34) | copy-start | bytes 2308
  250.6 55.4 %copy-start.66 = (f32[192]{0:T(256)S(1)}, f32[192]{0:T(256)}, u32[]{:S(2)}) copy-start(f32[192]{0:T(256)} %param.35) | copy-start | bytes 2308
  250.6 55.4 %copy-start.118 = (f32[192]{0:T(256)S(1)}, f32[192]{0:T(256)}, u32[]{:S(2)}) copy-start(f32[192]{0:T(256)} %param.36) | copy-start | bytes 2308
  250.6 145.7 %reduce-scatter.31.cloned.1.call-start = ((), (), s32[]{:S(2)}) async-start(), calls=%async_computation.27 | async-start | bytes 7864320 | tf_op jit(solution)/shard_map/reduce_scatter | solution.py:44
  295.8 713.2 %copy-start.6 = (f32[512,192]{0,1:T(8,128)}, f32[512,192]{0,1:T(8,128)S(1)}, u32[]{:S(2)}) copy-start(f32[512,192]{0,1:T(8,128)S(1)} %get-tuple-element.594) | copy-start | bytes 1179652
  295.8 713.2 %copy-start.8 = (f32[512,192]{0,1:T(8,128)}, f32[512,192]{0,1:T(8,128)S(1)}, u32[]{:S(2)}) copy-start(f32[512,192]{0,1:T(8,128)S(1)} %get-tuple-element.602) | copy-start | bytes 1179652
  328.4 141.0 %reduce-scatter.23.cloned.1.call-start = ((), (), s32[]{:S(2)}) async-start(), calls=%async_computation.21 | async-start | bytes 7864320 | tf_op jit(solution)/shard_map/reduce_scatter | solution.py:44
  350.4 118.9 %copy-start.98 = (f32[768]{0:T(1024)S(1)}, f32[768]{0:T(1024)}, u32[]{:S(2)}) copy-start(f32[768]{0:T(1024)} %param.38) | copy-start | bytes 9220
  350.4 172.1 %all-gather.25.cloned.1.call-start = ((), (), s32[]{:S(2)}) async-start(), calls=%async_computation.28 | async-start | bytes 3932160 | tf_op jit(solution)/shard_map/all_gather | solution.py:40
  478.5 90.1 %all-gather.21.cloned.1.call-start = ((), (), s32[]{:S(2)}) async-start(), calls=%async_computation.22 | async-start | bytes 3932160 | tf_op jit(solution)/shard_map/all_gather | solution.py:40
  479.1 127.3 %reduce-scatter.33.cloned.1.call-start = ((), (), s32[]{:S(2)}) async-start(), calls=%async_computation.29 | async-start | bytes 1966080 | tf_op jit(solution)/shard_map/reduce_scatter | solution.py:53
  526.8 116.1 %reduce-scatter.25.cloned.1.call-start = ((), (), s32[]{:S(2)}) async-start(), calls=%async_computation.23 | async-start | bytes 1966080 | tf_op jit(solution)/shard_map/reduce_scatter | solution.py:53
  572.8 70.1 %copy-start.140 = (f32[192]{0:T(256)S(1)}, f32[192]{0:T(256)}, u32[]{:S(2)}) copy-start(f32[192]{0:T(256)} %param.40) | copy-start | bytes 2308
  572.8 81.5 %copy-start.29 = (bf16[2,192,512]{2,1,0:T(8,128)(2,1)S(1)}, bf16[2,192,512]{2,1,0:T(8,128)(2,1)}, u32[]{:S(2)}) copy-start(bf16[2,192,512]{2,1,0:T(8,128)(2,1)} %param.30) | copy-start | bytes 1179652
  572.9 81.5 %copy-start.100 = (f32[192]{0:T(256)S(1)}, f32[192]{0:T(256)}, u32[]{:S(2)}) copy-start(f32[192]{0:T(256)} %param.41) | copy-start | bytes 2308
  572.9 181.6 %reduce-scatter.45.cloned.1.call-start = ((), (), s32[]{:S(2)}) async-start(), calls=%async_computation.37 | async-start | bytes 7864320 | tf_op jit(solution)/shard_map/reduce_scatter | solution.py:44
  644.3 36.7 %copy-start.30 = (f32[512,192]{0,1:T(8,128)}, f32[512,192]{0,1:T(8,128)S(1)}, u32[]{:S(2)}) copy-start(f32[512,192]{0,1:T(8,128)S(1)} %get-tuple-element.619) | copy-start | bytes 1179652
  685.7 141.7 %reduce-scatter.35.cloned.1.call-start = ((), (), s32[]{:S(2)}) async-start(), calls=%async_computation.30 | async-start | bytes 7864320 | tf_op jit(solution)/shard_map/reduce_scatter | solution.py:44
  706.9 120.5 %copy-start.28 = (f32[512,768]{1,0:T(8,128)S(1)}, f32[512,768]{1,0:T(8,128)}, u32[]{:S(2)}) copy-start(f32[512,768]{1,0:T(8,128)} %reduce-scatter.31.cloned.1.call-done) | copy-start | bytes 4718596
  706.9 120.5 %copy-start.99 = (f32[768]{0:T(1024)S(1)}, f32[768]{0:T(1024)}, u32[]{:S(2)}) copy-start(f32[768]{0:T(1024)} %param.38) | copy-start | bytes 9220
  706.9 170.4 %all-gather.31.cloned.1.call-start = ((), (), s32[]{:S(2)}) async-start(), calls=%async_computation.38 | async-start | bytes 3932160 | tf_op jit(solution)/shard_map/all_gather | solution.py:40
  833.2 44.0 %copy-start.33 = (bf16[192,768]{1,0:T(8,128)(2,1)S(1)}, bf16[192,768]{1,0:T(8,128)(2,1)}, u32[]{:S(2)}) copy-start(bf16[192,768]{1,0:T(8,128)(2,1)} %param.37) | copy-start | bytes 884740
  833.3 90.1 %all-gather.27.cloned.1.call-start = ((), (), s32[]{:S(2)}) async-start(), calls=%async_computation.31 | async-start | bytes 3932160 | tf_op jit(solution)/shard_map/all_gather | solution.py:40
  833.9 127.2 %reduce-scatter.47.cloned.1.call-start = ((), (), s32[]{:S(2)}) async-start(), calls=%async_computation.39 | async-start | bytes 1966080 | tf_op jit(solution)/shard_map/reduce_scatter | solution.py:53
  881.5 116.0 %reduce-scatter.37.cloned.1.call-start = ((), (), s32[]{:S(2)}) async-start(), calls=%async_computation.32 | async-start | bytes 1966080 | tf_op jit(solution)/shard_map/reduce_scatter | solution.py:53
  927.7 69.8 %copy-start.72 = (f32[512]{0:T(512)S(1)}, f32[512]{0:T(512)}, u32[]{:S(2)}) copy-start(f32[512]{0:T(512)} %copy-done.71) | copy-start | bytes 6148
  927.7 69.8 %copy-start.74 = (f32[512]{0:T(512)S(1)}, f32[512]{0:T(512)}, u32[]{:S(2)}) copy-start(f32[512]{0:T(512)} %copy-done.73) | copy-start | bytes 6148
  927.8 69.8 %copy-start.83 = (f32[512]{0:T(512)S(1)}, f32[512]{0:T(512)}, u32[]{:S(2)}) copy-start(f32[512]{0:T(512)} %copy-done.82) | copy-start | bytes 6148
  927.8 69.8 %copy-start.85 = (f32[512]{0:T(512)S(1)}, f32[512]{0:T(512)}, u32[]{:S(2)}) copy-start(f32[512]{0:T(512)} %copy-done.84) | copy-start | bytes 6148
  927.8 130.7 %reduce-scatter.39.cloned.1.call-start = ((), (), s32[]{:S(2)}) async-start(), calls=%async_computation.33 | async-start | bytes 1966080 | tf_op jit(solution)/shard_map/reduce_scatter | solution.py:44
  962.5 46.8 %copy-start.38 = (f32[512,192]{0,1:T(8,128)}, f32[512,192]{0,1:T(8,128)S(1)}, u32[]{:S(2)}) copy-start(f32[512,192]{0,1:T(8,128)S(1)} %get-tuple-element.587) | copy-start | bytes 1179652
  962.5 123.0 %copy-start.44 = (bf16[512,192]{0,1:T(8,128)(2,1)}, bf16[512,192]{0,1:T(8,128)(2,1)S(1)}, u32[]{:S(2)}) copy-start(bf16[512,192]{0,1:T(8,128)(2,1)S(1)} %get-tuple-element.597) | copy-start | bytes 589828
  999.0 144.3 %copy-start.42 = (bf16[512,192]{0,1:T(8,128)(2,1)}, bf16[512,192]{0,1:T(8,128)(2,1)S(1)}, u32[]{:S(2)}) copy-start(bf16[512,192]{0,1:T(8,128)(2,1)S(1)} %get-tuple-element.596) | copy-start | bytes 589828
  1029.4 63.0 %reduce-scatter.49.cloned.1.call-start = ((), (), s32[]{:S(2)}) async-start(), calls=%async_computation.40 | async-start | bytes 1966080 | tf_op jit(solution)/shard_map/reduce_scatter | solution.py:44
  1049.2 85.7 %reduce-scatter.41.cloned.1.call-start = ((), (), s32[]{:S(2)}) async-start(), calls=%async_computation.34 | async-start | bytes 1966080 | tf_op jit(solution)/shard_map/reduce_scatter | solution.py:307
  1083.8 91.9 %all-reduce.14.cloned.1.call-start = ((), (), s32[]{:S(2)}) async-start(), calls=%async_computation.45 | async-start | bytes 1048576 | tf_op jit(solution)/shard_map/psum | solution.py:62
  1086.5 123.3 %reduce-scatter.51.cloned.1.call-start = ((), (), s32[]{:S(2)}) async-start(), calls=%async_computation.41 | async-start | bytes 1966080 | tf_op jit(solution)/shard_map/reduce_scatter | solution.py:307
  1119.6 129.7 %all-gather.29.cloned.1.call-start = ((), (), s32[]{:S(2)}) async-start(), calls=%async_computation.35 | async-start | bytes 2949120 | tf_op jit(solution)/shard_map/all_gather | solution.py:40
  1120.3 56.7 %copy-start.141 = (f32[2,64]{1,0:T(2,128)}, f32[2,64]{1,0:T(2,128)S(1)}, u32[]{:S(2)}) copy-start(f32[2,64]{1,0:T(2,128)S(1)} %mul.580) | copy-start | bytes 1540
  1137.0 152.0 %all-gather.33.cloned.1.call-start = ((), (), s32[]{:S(2)}) async-start(), calls=%async_computation.42 | async-start | bytes 2949120 | tf_op jit(solution)/shard_map/all_gather | solution.py:40
  1177.0 34.9 %copy-start.34 = (f32[512,128]{0,1:T(8,128)}, f32[512,128]{0,1:T(8,128)S(1)}, u32[]{:S(2)}) copy-start(f32[512,128]{0,1:T(8,128)S(1)} %copy.98) | copy-start | bytes 786436
  1210.9 35.0 %copy-start.79 = (f32[128,14]{0,1:T(8,128)S(1)}, f32[128,14]{0,1:T(8,128)}, u32[]{:S(2)}) copy-start(f32[128,14]{0,1:T(8,128)} %param.48) | copy-start | bytes 21508
  1210.9 35.0 %copy-start.130 = (f32[14]{0:T(128)S(1)}, f32[14]{0:T(128)}, u32[]{:S(2)}) copy-start(f32[14]{0:T(128)} %param.49) | copy-start | bytes 172
  1210.9 38.4 %copy-start.27 = (bf16[2048,192]{0,1:T(8,128)(2,1)S(1)}, bf16[2048,192]{0,1:T(8,128)(2,1)}, u32[]{:S(2)}) copy-start(bf16[2048,192]{0,1:T(8,128)(2,1)} %copy-done.26) | copy-start | bytes 2359300
  1211.8 167.0 %all-reduce.16.cloned.1.call-start = ((), (), s32[]{:S(2)}) async-start(), calls=%async_computation.46 | async-start | bytes 1867776 | tf_op jit(solution)/shard_map/psum | solution.py:67
  1245.9 46.8 %copy-start.102 = (f32[6,128]{1,0:T(8,128)}, f32[6,128]{1,0:T(8,128)S(1)}, u32[]{:S(2)}) copy-start(f32[6,128]{1,0:T(8,128)S(1)} %fusion.84) | copy-start | bytes 9220
  1246.2 46.5 %copy-start.62 = (f32[6,14]{1,0:T(8,128)}, f32[6,14]{1,0:T(8,128)S(1)}, u32[]{:S(2)}) copy-start(f32[6,14]{1,0:T(8,128)S(1)} %get-tuple-element.649) | copy-start | bytes 1012
  1246.2 46.5 %copy-start.115 = (f32[6]{0:T(128)}, f32[6]{0:T(128)S(1)}, u32[]{:S(2)}) copy-start(f32[6]{0:T(128)S(1)} %get-tuple-element.648) | copy-start | bytes 76
  1246.4 46.3 %copy-start.132 = (f32[6]{0:T(128)}, f32[6]{0:T(128)S(1)}, u32[]{:S(2)}) copy-start(f32[6]{0:T(128)S(1)} %fusion.155) | copy-start | bytes 76
  1246.4 42.6 %copy-start.25 = (bf16[2048,192]{0,1:T(8,128)(2,1)S(1)}, bf16[2048,192]{0,1:T(8,128)(2,1)}, u32[]{:S(2)}) copy-start(bf16[2048,192]{0,1:T(8,128)(2,1)} %copy-done.24) | copy-start | bytes 2359300
  1252.8 40.4 %copy-start.106 = (f32[6,2]{0,1:T(2,128)S(1)}, f32[6,2]{0,1:T(2,128)}, u32[]{:S(2)}) copy-start(f32[6,2]{0,1:T(2,128)} %copy-done.105) | copy-start | bytes 148
  1292.6 92.3 %reduce-scatter.43.cloned.1.call-start = ((), (), s32[]{:S(2)}) async-start(), calls=%async_computation.36 | async-start | bytes 1966080 | tf_op jit(solution)/shard_map/reduce_scatter | solution.py:53
  1296.4 91.7 %reduce-scatter.53.cloned.1.call-start = ((), (), s32[]{:S(2)}) async-start(), calls=%async_computation.43 | async-start | bytes 1966080 | tf_op jit(solution)/shard_map/reduce_scatter | solution.py:53
  1334.8 107.0 %all-reduce.12.cloned.1.call-start = ((), (), s32[]{:S(2)}) async-start(), calls=%async_computation.44 | async-start | bytes 196608 | tf_op jit(solution)/shard_map/psum | solution.py:69
  1388.2 55.2 %copy-start.1 = (bf16[192,768]{1,0:T(8,128)(2,1)S(1)}, bf16[192,768]{1,0:T(8,128)(2,1)}, u32[]{:S(2)}) copy-start(bf16[192,768]{1,0:T(8,128)(2,1)} %param.39) | copy-start | bytes 884740
  (119 other events, 1539.8 us)
Sparse Core Ops, SparseCore 0:
  33.8 56.3 reduce-scatter.26
  93.1 56.9 reduce-scatter.18
  152.9 30.7 all-gather.22
  185.9 34.3 all-gather.18
  222.5 35.4 reduce-scatter.28
  260.1 34.2 reduce-scatter.20
  328.5 67.7 reduce-scatter.30
  399.3 70.0 reduce-scatter.22
  478.6 43.8 all-gather.24
  524.7 43.8 all-gather.20
  570.9 35.4 reduce-scatter.32
  608.6 34.2 reduce-scatter.24
  685.8 68.6 reduce-scatter.44
  757.3 70.0 reduce-scatter.34
  833.4 43.8 all-gather.30
  879.5 43.8 all-gather.26
  925.6 35.4 reduce-scatter.46
  963.2 34.2 reduce-scatter.36
  1029.6 28.8 reduce-scatter.38
  1061.3 31.1 reduce-scatter.48
  1095.5 31.1 reduce-scatter.40
  1130.2 45.4 all-reduce.13
  1178.6 31.1 reduce-scatter.50
  1212.0 37.1 all-gather.28
  1251.7 37.1 all-gather.32
  1292.7 19.4 all-reduce.15
  1314.3 36.6 reduce-scatter.42
  1353.4 34.6 reduce-scatter.52
  1390.4 51.3 all-reduce.11
where the time goes:
time: 1460 us; the launch traced here: 1450 us
  waiting for transfers between devices  879 us (60%)
  blocking collectives  292 us (20%)
  matrix products  156 us (11%)
  other arithmetic  71 us (5%)
  local copies, waits for them, and re-layouts  32.5 us (2%)
  between operations  16.4 us (1%)
    reduce_scatter x8, waiting for transfers between devices, reduce_rows(): lax.psum_scatter(term_fn(jnp.int32(0), lax.axis_size('row') * rows_out),...  348 us
    all_gather x8, waiting for transfers between devices, gather_rows(): return lax.all_gather(values, 'row', axis=0, tiled=True)  238 us
    reduce_scatter x8, waiting for transfers between devices, reduce_cols(): lax.psum_scatter(term_fn(jnp.int32(0), lax.axis_size('col') * rows_out),...  185 us
    all_gather x8, blocking collectives, gather_cols(): return lax.all_gather(values, 'col', axis=0, tiled=True)  142 us
    all_gather x6, blocking collectives, merged(): gathered = jax.tree.map(lambda a: lax.all_gather(a, axis), part)  63.7 us
    psum x1, waiting for transfers between devices, reduce_all(): token_grads = lax.psum(token_grads, ('dp', 'col'))  51.3 us
    dot_general x16, matrix products, term_fn(): lax.dot_general(gathered, matrix, (((1,), (contract,)), ((), ())), prefer...  50.7 us
    psum x4, blocking collectives, sum_features(): return lax.psum(values, 'row')  38.1 us
  transfers between devices with their start and end apart: 29, of which 25 were waited for; matrix products, arithmetic and copies ran while one was open for 14% of the time, Pallas kernels for 0%

commit v1 on v0

v1 whole, which is shorter than its diff:
```python
import jax
import jax.numpy as jnp
from jax import lax
from jax.sharding import PartitionSpec as P

HD = 64
SH = 2
SHD = 64

norm_eps = 1e-06
masked_value = -1e30
highest = lax.Precision.HIGHEST
f32 = jnp.float32
bf16 = jnp.bfloat16
WORLD = ("col", "row", "dp")


def sizes(seqs_local):
    parts = lax.axis_size("dp")
    rows = lax.axis_size("row")
    seqs = seqs_local * parts
    return parts, rows, lax.axis_size("col"), seqs, rows // seqs


def row_groups(rows, sub):
    return [list(range(at, at + sub)) for at in range(0, rows, sub)]


def take_in(values):
    parts, rows, _, seqs, sub = sizes(values.shape[0])
    held = lax.all_to_all(values, "dp", 2, 0, tiled=True)
    feats, half = held.shape[1:]
    held = held.reshape(seqs, feats, sub, half // sub).transpose(0, 2, 1, 3)
    held = held.reshape(rows, feats, half // sub)
    held = lax.all_to_all(held, "row", 0, 0, tiled=True)
    return held.reshape(rows * feats, half // sub)


def give_back(values, seqs_local):
    parts, rows, _, seqs, sub = sizes(seqs_local)
    width, own = values.shape
    feats = width // rows
    held = lax.all_to_all(values.reshape(rows, feats, own), "row", 0, 0, tiled=True)
    held = held.reshape(seqs, sub, feats, own).transpose(0, 2, 1, 3).reshape(seqs, feats, sub * own)
    return lax.all_to_all(held, "dp", 0, 2, tiled=True)


def gather_world(shard):
    cols, rows = lax.axis_size("col"), lax.axis_size("row")
    out = lax.all_gather(shard, WORLD, axis=0, tiled=True)
    return out.reshape(cols, rows, -1, shard.shape[1])


def own_half(block):
    parts = lax.axis_size("dp")
    amount = block.shape[0] // parts
    return lax.dynamic_slice_in_dim(block, lax.axis_index("dp") * amount, amount)


def scatter_world(full):
    flat = full.reshape(-1, full.shape[-1])
    mine = lax.psum_scatter(flat, WORLD, scatter_dimension=0, tiled=True)
    return lax.all_gather(mine, "dp", axis=0, tiled=True)


def swap_cols(values):
    return lax.all_to_all(values, "col", 0, 0, tiled=True)


def gather_sequence(values, sub):
    cols, own, width = values.shape
    held = values[:, None]
    if sub > 1:
        groups = row_groups(lax.axis_size("row"), sub)
        held = lax.all_gather(held, "row", axis=1, tiled=True, axis_index_groups=groups)
    held = lax.all_gather(held[:, None], "dp", axis=1, tiled=True)
    return held.reshape(-1, width)


def scatter_sequence(values, cols, sub):
    parts = lax.axis_size("dp")
    width = values.shape[-1]
    held = values.reshape(cols, parts, sub, -1, width)
    held = lax.psum_scatter(held, "dp", scatter_dimension=1, tiled=True)[:, 0]
    if sub > 1:
        groups = row_groups(lax.axis_size("row"), sub)
        held = lax.psum_scatter(
            held, "row", scatter_dimension=1, tiled=True, axis_index_groups=groups
        )
    return held[:, 0]


def normalize(values):
    mean_v = jnp.mean(values, axis=-1, keepdims=True)
    center = values - mean_v
    inv_std = lax.rsqrt(jnp.mean(center * center, axis=-1, keepdims=True) + norm_eps)
    return center * inv_std, inv_std


def normalize_back(grad_hat, normed, inv_std):
    return inv_std * (
        grad_hat
        - jnp.mean(grad_hat, axis=-1, keepdims=True)
        - normed * jnp.mean(grad_hat * normed, axis=-1, keepdims=True)
    )


def gelu_exact(values):
    return jax.nn.gelu(values, approximate=False)


def mm(a, b, contract):
    return lax.dot_general(a, b, (contract, ((), ())), preferred_element_type=f32)


def combine_pool(part_one, part_two):
    top_a, total_a, sum_a = part_one
    top_b, total_b, sum_b = part_two
    row_top = jnp.maximum(top_a, top_b)
    factor_a = jnp.exp(top_a - row_top)
    factor_b = jnp.exp(top_b - row_top)
    return (
        row_top,
        total_a * factor_a + total_b * factor_b,
        sum_a * factor_a[:, :, None] + sum_b * factor_b[:, :, None],
    )


def attend(q, k, v, q_seg, k_seg, scale):
    scores = jnp.einsum("qhd,khd->hqk", q, k, preferred_element_type=f32) * scale
    scores = jnp.where((q_seg[:, None] == k_seg[None, :])[None], scores, masked_value)
    top = jnp.max(scores, axis=-1, keepdims=True)
    exp_scores = jnp.exp(scores - top)
    total = jnp.sum(exp_scores, axis=-1, keepdims=True)
    probs = exp_scores / total
    context = jnp.einsum("hqk,khd->qhd", probs.astype(bf16), v, preferred_element_type=f32)
    return context.astype(bf16), probs


def attend_back(q, k, v, probs, d_ctx, scale):
    d_probs = jnp.einsum("qhd,khd->hqk", d_ctx, v, preferred_element_type=f32)
    delta = jnp.sum(probs * d_probs, axis=-1, keepdims=True)
    d_scores = (probs * (d_probs - delta)).astype(bf16)
    d_q = jnp.einsum("hqk,khd->qhd", d_scores, k, preferred_element_type=f32) * scale
    d_k = jnp.einsum("hqk,qhd->khd", d_scores, q, preferred_element_type=f32) * scale
    d_v = jnp.einsum("hqk,qhd->khd", probs.astype(bf16), d_ctx, preferred_element_type=f32)
    return d_q, d_k, d_v


def local(
    tokens,
    segments,
    labels,
    cotangent,
    w_qkv,
    b_qkv,
    w_out,
    b_out,
    ln1_gain,
    ln1_bias,
    w_in,
    b_in,
    w_back,
    b_back,
    ln2_gain,
    ln2_bias,
    s_proj,
    s_bias,
    s_query,
    s_mid,
    s_mid_bias,
    s_cls,
    s_cls_bias,
):
    seqs_local, width_row, cols_local = tokens.shape
    parts, rows, cols, seqs, sub = sizes(seqs_local)
    width = width_row * rows
    own = cols_local // (parts * sub)
    width_col = b_qkv.shape[1]
    heads_dev = width_col // HD
    hidden_col = b_in.shape[0]
    docs_count = labels.shape[1]
    class_count = s_cls.shape[1]
    student_width = s_proj.shape[1]
    row_index = lax.axis_index("row")
    col_index = lax.axis_index("col")
    dp_index = lax.axis_index("dp")
    seq_index = row_index // sub
    sub_index = row_index % sub
    score_scale = HD ** (-0.5)
    pool_scale = SHD ** (-0.5)
    query_heads = s_query.reshape(SH, SHD)
    doc_ids = jnp.arange(docs_count, dtype=jnp.int32)
    class_ids = jnp.arange(class_count, dtype=jnp.int32)

    w_qkv_all = gather_world(own_half(w_qkv)).reshape(cols, width, 3 * width_col)
    x_t = take_in(tokens)
    rest = jnp.concatenate([own_half(w_in), own_half(w_back), own_half(w_out).reshape(-1, width_col)], axis=1)
    rest_all = gather_world(rest)
    w_in_all = rest_all[..., :hidden_col].reshape(cols, width, hidden_col)
    w_back_all = rest_all[..., hidden_col : 2 * hidden_col].reshape(cols, width, hidden_col)
    w_out_all = rest_all[..., 2 * hidden_col :].reshape(cols, rows, width_col, width_row)
    w_out_all = w_out_all.transpose(0, 2, 1, 3).reshape(width, width)
    row_vectors = lax.all_gather(
        jnp.stack([b_out, ln1_gain, ln1_bias, b_back, ln2_gain, ln2_bias]), "row", axis=1, tiled=True
    )
    b_out_a, gain_one, bias_one, b_back_a, gain_two, bias_two = [row_vectors[i] for i in range(6)]
    b_qkv_all = lax.all_gather(b_qkv, "col")
    b_in_all = lax.all_gather(b_in, "col")
    s_proj_all = lax.all_gather(s_proj, "row", axis=0, tiled=True)
    whole_ints = lax.all_gather(jnp.concatenate([segments, labels], axis=1), "dp", axis=0, tiled=True)
    ints = lax.dynamic_index_in_dim(whole_ints, seq_index, 0, False)
    seq_len = segments.shape[1]
    seg_all, label_seq = ints[:seq_len], ints[seq_len:]
    seg_blocks = seg_all.reshape(cols, parts, sub, own)
    seg_q = lax.dynamic_index_in_dim(seg_blocks, dp_index, 1, False)
    seg_q = lax.dynamic_index_in_dim(seg_q, sub_index, 1, False)
    seg_own = lax.dynamic_index_in_dim(seg_q, col_index, 0, False)
    seg_q = seg_q.reshape(-1)

    x = x_t.T
    offsets = jnp.stack([b_qkv_all[:, 0], jnp.zeros_like(b_qkv_all[:, 0]), b_qkv_all[:, 1]], axis=1)
    offsets = offsets.reshape(cols, 3, heads_dev, HD).transpose(0, 2, 1, 3).reshape(cols, 1, -1)
    qkv = jnp.einsum("td,cdn->ctn", x, w_qkv_all, preferred_element_type=f32) + offsets
    qkv = swap_cols(qkv.astype(bf16)).reshape(cols, own, heads_dev, 3, HD)
    queries = qkv[:, :, :, 0].reshape(cols * own, heads_dev, HD)
    kv = gather_sequence(qkv[:, :, :, 1:].reshape(cols, own, -1), sub)
    kv = kv.reshape(seq_len, heads_dev, 2, HD)
    key_rows, value_rows = kv[:, :, 0], kv[:, :, 1]
    context, probs = attend(queries, key_rows, value_rows, seg_q, seg_all, score_scale)
    ctx = swap_cols(context.reshape(cols, own, width_col))
    ctx = ctx.transpose(1, 0, 2).reshape(own, width)

    attn_out = mm(ctx, w_out_all, ((1,), (0,))) + b_out_a
    normed_one, inv_one = normalize(x.astype(f32) + attn_out)
    hidden_one = normed_one * gain_one + bias_one
    hidden_low = hidden_one.astype(bf16)
    pre_act = jnp.einsum("td,cdn->ctn", hidden_low, w_in_all, preferred_element_type=f32)
    pre_act = pre_act + b_in_all[:, None, :]
    act = gelu_exact(pre_act).astype(bf16)
    ffn_out = jnp.einsum("ctn,cdn->td", act, w_back_all, preferred_element_type=f32) + b_back_a
    normed_two, inv_two = normalize(hidden_one + ffn_out)
    layer_out = (normed_two * gain_two + bias_two).astype(bf16)
    out = give_back(layer_out.T, seqs_local)

    student_h = mm(layer_out, s_proj_all, ((1,), (0,))) + s_bias
    head_parts = student_h.reshape(own, SH, SHD)
    pool_logit = jnp.sum(head_parts * query_heads, axis=-1) * pool_scale
    member = (seg_own[:, None] == doc_ids[None, :])[:, :, None]
    masked = jnp.where(member, pool_logit[:, None, :], masked_value)
    local_top = jnp.max(masked, axis=0)
    local_exp = jnp.where(member, jnp.exp(masked - local_top[None]), 0.0)
    local_total = jnp.sum(local_exp, axis=0)
    local_sum = jnp.einsum("tdh,thk->dhk", local_exp, head_parts, precision=highest)
    stats = jnp.concatenate([local_top[..., None], local_total[..., None], local_sum], axis=-1)
    stats = lax.all_gather(stats, ("dp", "col"))
    if sub > 1:
        stats = lax.all_gather(stats, "row", axis=0, tiled=True, axis_index_groups=row_groups(rows, sub))
    tops, totals, sums = stats[..., 0], stats[..., 1], stats[..., 2:]
    doc_top = jnp.max(tops, axis=0)
    factors = jnp.exp(tops - doc_top[None])
    doc_total = jnp.sum(totals * factors, axis=0)
    pooled_heads = jnp.sum(sums * factors[..., None], axis=0) / doc_total[:, :, None]
    pooled = pooled_heads.reshape(docs_count, student_width)
    middle = jnp.tanh(jnp.dot(pooled, s_mid, precision=highest) + s_mid_bias)
    logit_rows = jnp.dot(middle, s_cls, precision=highest) + s_cls_bias
    logits = lax.all_gather(logit_rows, "row")[::sub]
    logits = lax.dynamic_slice_in_dim(logits, dp_index * seqs_local, seqs_local)
    logit_top = jnp.max(logit_rows, axis=-1, keepdims=True)
    logit_exp = jnp.exp(logit_rows - logit_top)
    one_hot = (label_seq[:, None] == class_ids[None, :]).astype(f32)
    d_logits = logit_exp / jnp.sum(logit_exp, axis=-1, keepdims=True) - one_hot
    g_cls = jnp.dot(middle.T, d_logits, precision=highest)
    g_cls_bias = jnp.sum(d_logits, axis=0)
    d_middle = jnp.dot(d_logits, s_cls.T, precision=highest) * (1.0 - middle * middle)
    g_mid = jnp.dot(pooled.T, d_middle, precision=highest)
    g_mid_bias = jnp.sum(d_middle, axis=0)
    d_pooled = jnp.dot(d_middle, s_mid.T, precision=highest).reshape(docs_count, SH, SHD)
    shares = jnp.where(member, jnp.exp(masked - doc_top[None]), 0.0) / doc_total[None]
    d_share = jnp.einsum("dhk,thk->tdh", d_pooled, head_parts, precision=highest)
    base_term = jnp.sum(d_pooled * pooled_heads, axis=-1)
    d_pool_logit = jnp.sum(shares * (d_share - base_term[None]), axis=1)
    d_heads = jnp.einsum("tdh,dhk->thk", shares, d_pooled, precision=highest)
    d_heads = d_heads + d_pool_logit[:, :, None] * query_heads[None] * pool_scale
    g_query = (jnp.sum(d_pool_logit[:, :, None] * head_parts, axis=0) * pool_scale).reshape(-1)
    d_student = d_heads.reshape(own, student_width)
    g_sbias = jnp.sum(d_student, axis=0)
    g_sproj = jnp.dot(layer_out.astype(f32).T, d_student, precision=highest)

    d_out = take_in(cotangent).T.astype(f32)
    g_ln2_gain = jnp.sum(d_out * normed_two, axis=0)
    g_ln2_bias = jnp.sum(d_out, axis=0)
    d_resid_two = normalize_back(d_out * gain_two, normed_two, inv_two)
    d_ffn = d_resid_two.astype(bf16)
    g_back_bias = jnp.sum(d_ffn.astype(f32), axis=0)
    g_back = jnp.einsum("td,ctn->cdn", d_ffn, act, preferred_element_type=f32)
    d_act = jnp.einsum("td,cdn->ctn", d_ffn, w_back_all, preferred_element_type=f32)
    _, gelu_fn = jax.vjp(gelu_exact, pre_act)
    d_pre = gelu_fn(d_act)[0].astype(bf16)
    g_in_bias = jnp.sum(d_pre.astype(f32), axis=1)
    g_in = jnp.einsum("td,ctn->cdn", hidden_low, d_pre, preferred_element_type=f32)
    d_hidden_one = d_resid_two + jnp.einsum(
        "ctn,cdn->td", d_pre, w_in_all, preferred_element_type=f32
    )
    g_ln1_gain = jnp.sum(d_hidden_one * normed_one, axis=0)
    g_ln1_bias = jnp.sum(d_hidden_one, axis=0)
    d_resid_one = normalize_back(d_hidden_one * gain_one, normed_one, inv_one)
    d_attn = d_resid_one.astype(bf16)
    g_out_bias = jnp.sum(d_attn.astype(f32), axis=0)
    g_out = mm(ctx, d_attn, ((0,), (0,)))
    d_ctx = mm(d_attn, w_out_all, ((1,), (1,))).astype(bf16)
    d_ctx = swap_cols(d_ctx.reshape(own, cols, width_col).transpose(1, 0, 2))
    d_ctx = d_ctx.reshape(cols * own, heads_dev, HD)
    d_q, d_k, d_v = attend_back(queries, key_rows, value_rows, probs, d_ctx, score_scale)
    d_kv = jnp.stack([d_k, d_v], axis=2).astype(bf16).reshape(seq_len, -1)
    d_kv = scatter_sequence(d_kv, cols, sub).reshape(cols, own, heads_dev, 2, HD)
    d_q = d_q.astype(bf16).reshape(cols, own, heads_dev, 1, HD)
    d_qkv = jnp.concatenate([d_q, d_kv], axis=3).reshape(cols, own, 3 * width_col)
    d_qkv = swap_cols(d_qkv)
    g_qkv_bias = jnp.sum(d_qkv.astype(f32), axis=1).reshape(cols, heads_dev, 3, HD)
    g_qkv = jnp.einsum("td,ctn->cdn", x, d_qkv, preferred_element_type=f32)
    d_tokens = d_resid_one + jnp.einsum("ctn,cdn->td", d_qkv, w_qkv_all, preferred_element_type=f32)
    grad_tokens = give_back(d_tokens.astype(bf16).T, seqs_local).astype(f32)

    g_out = g_out.reshape(cols, width_col, rows, width_row).transpose(0, 2, 1, 3)
    g_out = g_out.reshape(cols, rows, width_row, width_col)
    model = jnp.concatenate(
        [
            g_in.reshape(cols, rows, width_row, hidden_col).astype(bf16),
            g_back.reshape(cols, rows, width_row, hidden_col).astype(bf16),
            g_out.astype(bf16),
        ],
        axis=-1,
    )
    model = scatter_world(model).astype(f32)
    g_qkv = scatter_world(g_qkv.reshape(cols, rows, width_row, 3 * width_col).astype(bf16)).astype(f32)
    once = 1.0 / (parts * cols * sub)
    small = (
        g_qkv_bias[:, :, 0].reshape(cols, width_col),
        g_qkv_bias[:, :, 2].reshape(cols, width_col),
        g_in_bias,
        g_out_bias,
        g_ln1_gain,
        g_ln1_bias,
        g_back_bias,
        g_ln2_gain,
        g_ln2_bias,
        g_sproj,
        g_sbias,
        g_query,
        g_mid * once,
        g_mid_bias * once,
        g_cls * once,
        g_cls_bias * once,
    )
    small = lax.psum(small, WORLD)

    def at_col(part):
        return lax.dynamic_index_in_dim(part, col_index, 0, False)

    def at_row(part):
        return lax.dynamic_slice_in_dim(part, row_index * width_row, width_row)

    return (
        out,
        logits,
        grad_tokens,
        g_qkv,
        jnp.stack([at_col(small[0]), at_col(small[1])]),
        model[:, 2 * hidden_col :].reshape(width_col, width_row),
        at_row(small[3]),
        at_row(small[4]),
        at_row(small[5]),
        model[:, :hidden_col],
        at_col(small[2]),
        model[:, hidden_col : 2 * hidden_col],
        at_row(small[6]),
        at_row(small[7]),
        at_row(small[8]),
        at_row(small[9]),
        small[10],
        small[11],
        small[12],
        small[13],
        small[14],
        small[15],
    )


def solution(mesh):
    row, col = P("row"), P("col")
    grid, whole = P("row", "col"), P("dp", "row", "col")
    placed = (
        (whole, P("dp", None), P("dp", None), whole, grid, P(None, "col"), P("col", "row"))
        + (row, row, row, grid, col, grid, row, row, row, P("row", None))
        + (P(),) * 6
    )
    results = (
        (whole, P("dp", None, None), whole, grid, P(None, "col"), P("col", "row"))
        + (row, row, row, grid, col, grid, row, row, row, P("row", None))
        + (P(),) * 6
    )
    return jax.shard_map(local, mesh=mesh, in_specs=placed, out_specs=results, check_vma=False)
```

time: 1460 us -> 819 us (0.56)
  waiting for transfers between devices: 879 us -> 355 us
  blocking collectives: 292 us -> 200 us
  matrix products: 156 us -> 106 us
  local copies, waits for them, and re-layouts: 32.5 us -> 71.5 us
  other arithmetic: 71 us -> 34.5 us
  starting transfers between devices: 2.28 us -> 27.2 us
    reduce_scatter x18 -> x3, waiting for transfers between devices: 560 us -> 184 us  [the longest x2 184 us: scatter_world(): mine = lax.psum_scatter(flat, WORLD, scatter_dimension=0, tiled=True)]
    all_gather x8 -> x3, waiting for transfers between devices: 238 us -> 64.7 us  [the longest x2 64.7 us: gather_world(): out = lax.all_gather(shard, WORLD, axis=0, tiled=True)]
    all_gather x16 -> x9, blocking collectives: 233 us -> 89.4 us  [the longest x1 24 us: local(): stats = lax.all_gather(stats, ('dp', 'col'))]
    all_to_all x0 -> x5, blocking collectives: none -> 68.5 us  [the longest x2 55.8 us: swap_cols(): return lax.all_to_all(values, 'col', 0, 0, tiled=True)]
    dot_general x38 -> x19, matrix products: 130 us -> 89.6 us  [the longest x1 16.5 us: attend_back(): d_probs = jnp.einsum('qhd,khd->hqk', d_ctx, v, preferred_element_type=f32)]
    all_to_all x0 -> x7, waiting for transfers between devices: none -> 29 us  [the longest x2 24.2 us: swap_cols(): return lax.all_to_all(values, 'col', 0, 0, tiled=True)]
    all_to_all x0 -> x7, starting transfers between devices: none -> 26.7 us  [the longest x2 8.65 us: take_in(): held = lax.all_to_all(held, 'row', 0, 0, tiled=True)]
    convert_element_type x25 -> x3, other arithmetic: 42.7 us -> 20.6 us  [the longest x1 16.3 us: attend_back(): d_scores = (probs * (d_probs - delta)).astype(bf16)]
  transfers between devices with their start and end apart: 29 -> 14, of which waited for: 25 -> 7; matrix products, arithmetic and copies ran while one was open for 14% -> 16% of each run, Pallas kernels for 0% -> 0%
where the time goes in v1:
time: 819 us; the launch traced here: 810 us
  waiting for transfers between devices  355 us (43%)
  blocking collectives  200 us (24%)
  matrix products  106 us (13%)
  local copies, waits for them, and re-layouts  71.5 us (9%)
  other arithmetic  34.5 us (4%)
  starting transfers between devices  27.2 us (3%)
  between operations  15.5 us (2%)
    reduce_scatter x2, waiting for transfers between devices, scatter_world(): mine = lax.psum_scatter(flat, WORLD, scatter_dimension=0, tiled=True)  184 us
    psum x1, waiting for transfers between devices, local(): small = lax.psum(small, WORLD)  76.9 us
    all_gather x2, waiting for transfers between devices, gather_world(): out = lax.all_gather(shard, WORLD, axis=0, tiled=True)  64.7 us
    all_to_all x2, blocking collectives, swap_cols(): return lax.all_to_all(values, 'col', 0, 0, tiled=True)  55.8 us
    psum x1, blocking collectives, local(): small = lax.psum(small, WORLD)  42.1 us
    all_to_all x2, waiting for transfers between devices, swap_cols(): return lax.all_to_all(values, 'col', 0, 0, tiled=True)  24.2 us
    all_gather x1, blocking collectives, local(): stats = lax.all_gather(stats, ('dp', 'col'))  24 us
    all_gather x1, blocking collectives, local(): b_in_all = lax.all_gather(b_in, 'col')  21.1 us
  transfers between devices with their start and end apart: 14, of which 7 were waited for; matrix products, arithmetic and copies ran while one was open for 16% of the time, Pallas kernels for 0%

profile of v1, /device:TPU:0, one launch (start us, length us, event | category | flops | bytes accessed | tf_op | source)
XLA Modules:
  0.0 809.7 jit_solution(15562263959811250246)
XLA Ops:
  10.2 4.2 all_to_all.103
  15.4 5.2 all-to-all-start.1
  20.6 12.2 %all-gather.4 = f32[4,2,192]{2,1,0:T(2,128)S(1)} all-gather(f32[1,2,192]{2,1,0:T(2,128)S(1)} %bitcast.448), channel_id=2, replica_groups=mesh['dp'=2,'row'=4,'col'=4] {'col'}, dimensions={0}, use_global_device_ids=true | all-gather | bytes 7680 | tf_op jit(solution)/shard_map/all_gather | solution.py:208
  33.1 43.7 %all-gather.13.cloned.1.call-done = bf16[3072,576]{1,0:T(8,128)(2,1)} async-done(((bf16[96,576]{1,0:T(8,128)(2,1)}), bf16[3072,576]{1,0:T(8,128)(2,1)}) %all-gather.13.cloned.1.call-update) | async-done | bytes 3538960 | tf_op jit(solution)/shard_map/all_gather | solution.py:50
  76.8 3.5 fusion.42
  80.4 32.3 %all_to_all.104 = bf16[4,256,576]{1,2,0:T(8,128)(2,1)S(1)} all-to-all(bf16[4,256,576]{1,2,0:T(8,128)(2,1)S(1)} %fusion.42), channel_id=1, replica_groups=mesh['dp'=2,'row'=4,'col'=4] {'col'}, dimensions={0} | all-to-all | bytes 2359296 | tf_op jit(solution)/shard_map/all_to_all | solution.py:67
  117.0 3.5 all-to-all-start.6
  120.6 1.9 all-gather.5
  123.9 8.3 %all-gather.6 = f32[4,192,6]{1,2,0:T(8,128)S(1)} all-gather(f32[1,192,6]{1,2,0:T(8,128)S(1)} %bitcast.441), channel_id=1, replica_groups=mesh['dp'=2,'row'=4,'col'=4] {'row'}, dimensions={0}, use_global_device_ids=true | all-gather | bytes 23040 | tf_op jit(solution)/shard_map/all_gather | solution.py:204
  132.3 2.5 broadcast_compare_fusion
  135.4 3.9 copy.205
  139.3 2.4 reshape_reshape.8
  141.7 13.9 %fusion.132 = (f32[3,1024]{1,0:T(4,128)S(1)}, f32[3,1024,2048]{2,1,0:T(8,128)}) fusion(pred[1024,2048]{1,0:T(8,128)(4,1)} %broadcast_compare_fusion, bf16[1024,3,64]{0,2,1:T(8,128)(2,1)S(1)} %reshape_squeeze.9, bf16[2048,3,2,64]{0,3,2,1:T(8,128)(2,1)} %reshape_reshape.8), kind=kOutput, calls=%fused_computation.237 | convolution fusion | flops 830474240 | bytes 28454912 | tf_op jit(solution)/shard_map/sub | solution.py:133
  155.6 10.4 %fusion.50 = bf16[1024,3,64]{0,2,1:T(8,128)(2,1)S(1)} fusion(bf16[2048,3,2,64]{0,3,2,1:T(8,128)(2,1)S(1)} %copy-done.7, f32[3,1024,2048]{2,1,0:T(8,128)} %get-tuple-element.190, f32[3,1024]{1,0:T(4,128)S(1)} %get-tuple-element.189), kind=kOutput, calls=%fused_computation.74 | convolution fusion | flops 818085888 | bytes 26361856 | tf_op jit(solution)/shard_map/hqk,khd->qhd/dot_general | solution.py:136
  167.9 3.5 all-to-all-start.3
  171.4 21.1 %all-gather.7 = f32[4,1,768]{2,1,0:T(1,128)S(1)} all-gather(f32[1,1,768]{2,1,0:T(1,128)S(1)} %reshape.309), channel_id=3, replica_groups=mesh['dp'=2,'row'=4,'col'=4] {'col'}, dimensions={0}, use_global_device_ids=true | all-gather | bytes 15360 | tf_op jit(solution)/shard_map/all_gather | solution.py:209
  192.5 2.0 copy.224
  194.5 21.0 %all-gather.17.cloned.1.call-done = bf16[3072,1728]{1,0:T(8,128)(2,1)} async-done(((bf16[96,1728]{1,0:T(8,128)(2,1)}), bf16[3072,1728]{1,0:T(8,128)(2,1)}) %all-gather.17.cloned.1.call-update) | async-done | bytes 10616848 | tf_op jit(solution)/shard_map/all_gather | solution.py:50
  215.5 1.5 slice.111
  217.0 2.4 copy.279
  219.3 3.1 reshape.282
  222.5 8.4 %fusion.128 = (bf16[4,4,192,768]{3,2,1,0:T(8,128)(2,1)}, bf16[4,4,192,768]{3,2,1,0:T(8,128)(2,1)}) fusion(bf16[4,4,192,1728]{3,2,1,0:T(8,128)(2,1)} %bitcast.406), kind=kLoop, calls=%fused_computation.233 | loop fusion | bytes 18874368 | tf_op jit(solution)/shard_map/slice | solution.py:201
  230.9 3.5 all-to-all-start.7
  234.4 1.5 fusion.125
  236.1 12.0 %fusion.18 = (bf16[4,256,768]{2,1,0:T(8,128)(2,1)S(1)}, f32[4,256,768]{2,1,0:T(8,128)}, f32[4,768,256]{1,2,0:T(8,128)}) fusion(f32[4,768]{1,0:T(4,128)S(1)} %bitcast.444, bf16[4,768,768]{2,1,0:T(8,128)(2,1)} %bitcast.413, f32[256,768]{0,1:T(8,128)S(1)} %get-tuple-element.175, f32[768]{0:T(1024)S(1)} %get-tuple-element.144, f32[768]{0:T(1024)S(1)} %get-tuple-element.145, ...), kind=kOutput, calls=%fused_computation.34 | convolution fusion | flops 1260847104 | bytes 13389824 | tf_op jit(solution)/shard_map/td,cdn->ctn/dot_general | solution.py:238
  248.1 2.3 fusion.122
  251.5 7.4 convert_reduce_fusion
  259.0 2.6 multiply_reduce_fusion.1
  262.6 23.5 %all_to_all.105 = bf16[4,256,192]{1,2,0:T(8,128)(2,1)S(1)} all-to-all(bf16[4,256,192]{1,2,0:T(8,128)(2,1)S(1)} %bitcast.428), channel_id=1, replica_groups=mesh['dp'=2,'row'=4,'col'=4] {'col'}, dimensions={0} | all-to-all | bytes 786432 | tf_op jit(solution)/shard_map/all_to_all | solution.py:67
  286.7 16.5 %multiply_reduce_fusion = (f32[3,1024]{1,0:T(4,128)S(1)}, f32[3,1024,2048]{2,1,0:T(8,128)}) fusion(f32[3,1024,2048]{2,1,0:T(8,128)} %get-tuple-element.190, f32[3,1024]{1,0:T(4,128)S(1)} %get-tuple-element.189, bf16[1024,3,64]{0,2,1:T(8,128)(2,1)S(1)} %reshape.288, bf16[2048,3,2,64]{0,3,2,1:T(8,128)(2,1)} %reshape_reshape.8), kind=kOutput, calls=%fused_computation.2 | convolution fusion | flops 824177664 | bytes 51535872 | tf_op jit(solution)/shard_map/qhd,khd->hqk/dot_general | solution.py:141
  303.1 9.6 %fusion.37 = bf16[2048,3,1,64]{0,3,1,2:T(8,128)(2,1)S(1)} fusion(bf16[1024,3,64]{0,2,1:T(8,128)(2,1)S(1)} %reshape.288, f32[3,1024,2048]{2,1,0:T(8,128)} %get-tuple-element.190, f32[3,1024]{1,0:T(4,128)S(1)} %get-tuple-element.189), kind=kOutput, calls=%fused_computation.55 | convolution fusion | flops 818282496 | bytes 26357760 | tf_op jit(solution)/shard_map/hqk,qhd->khd/dot_general | solution.py:146
  312.7 16.3 %multiply_convert_fusion = bf16[3,1024,2048]{2,1,0:T(8,128)(2,1)S(1)} fusion(f32[3,1024,2048]{2,1,0:T(8,128)} %get-tuple-element.198, f32[3,1024]{1,0:T(4,128)S(1)} %get-tuple-element.197, f32[3,1024,2048]{2,1,0:T(8,128)} %get-tuple-element.190, f32[3,1024]{1,0:T(4,128)S(1)} %get-tuple-element.189), kind=kLoop, calls=%fused_computation.1 | loop fusion | flops 25165824 | bytes 62939136 | tf_op jit(solution)/shard_map/convert_element_type | solution.py:143
  329.1 2.3 fusion.40
  331.4 2.2 copy-done.2
  333.8 1.4 copy.230
  335.2 3.8 convert_element_type.186
  339.0 5.0 copy.231
  344.2 8.8 %all_gather.57 = bf16[768,128]{1,0:T(8,128)(2,1)S(1)} all-gather(bf16[192,128]{1,0:T(8,128)(2,1)S(1)} %copy-done.24), channel_id=1, replica_groups=mesh['dp'=2,'row'=4,'col'=4] {'row'}, dimensions={0}, use_global_device_ids=true | all-gather | bytes 245760 | tf_op jit(solution)/shard_map/all_gather | solution.py:210
  355.6 24.0 %all-gather.2 = f32[48,2,66]{2,1,0:T(2,128)S(1)} all-gather(f32[6,2,66]{2,1,0:T(2,128)S(1)} %copy.218), channel_id=4, replica_groups=mesh['dp'=2,'row'=4,'col'=4] {'dp','col'}, dimensions={0}, use_global_device_ids=true | all-gather | bytes 28512 | tf_op jit(solution)/shard_map/all_gather | solution.py:256
  380.8 8.8 %fusion.53 = bf16[1024,3,64]{0,2,1:T(8,128)(2,1)S(1)} fusion(bf16[3,1024,2048]{2,1,0:T(8,128)(2,1)} %copy-done.2, bf16[2048,3,2,64]{0,3,2,1:T(8,128)(2,1)} %reshape_reshape.8), kind=kOutput, calls=%fused_computation.75 | convolution fusion | flops 805699584 | bytes 13762560 | tf_op jit(solution)/shard_map/hqk,khd->qhd/dot_general | solution.py:144
  390.0 1.4 copy.232
  392.6 3.5 all-to-all-start.9
  400.9 24.2 %all-to-all-done.9 = bf16[4,256,576]{1,2,0:T(8,128)(2,1)S(1)} async-done(((bf16[4,256,576]{1,2,0:T(8,128)(2,1)}), bf16[4,256,576]{1,2,0:T(8,128)(2,1)S(1)}, u32[]{:S(2)}, u32[]{:S(2)}) %all-to-all-start.9) | async-done | bytes 1179680 | tf_op jit(solution)/shard_map/all_to_all | solution.py:67
  425.0 2.9 convert_bitcast_fusion
  427.9 6.0 copy.260
  434.0 3.5 fusion.119
  438.1 1.4 convolution_convert_fusion
  439.5 1.4 convolution_convert_fusion.1
  440.9 4.9 pad_maximum_fusion
  446.4 8.3 %all-gather.8 = f32[4,6,14]{2,1,0:T(8,128)S(1)} all-gather(f32[1,6,14]{2,1,0:T(8,128)S(1)} %bitcast.439), channel_id=5, replica_groups=mesh['dp'=2,'row'=4,'col'=4] {'row'}, dimensions={0}, use_global_device_ids=true | all-gather | bytes 1680 | tf_op jit(solution)/shard_map/all_gather | solution.py:267
  455.3 3.5 all-to-all-start.4
  459.2 76.9 %all-reduce.4.cloned.1.call-done = (f32[768,128]{1,0:T(8,128)}, f32[128,128]{1,0:T(8,128)}) async-done(((f32[768,128]{1,0:T(8,128)}, f32[128,128]{1,0:T(8,128)}), (f32[768,128]{1,0:T(8,128)}, f32[128,128]{1,0:T(8,128)})) %all-reduce.4.cloned.1.call-update) | async-done | bytes 458768 | tf_op jit(solution)/shard_map/psum | solution.py:356
  536.1 1.5 constant_dynamic-slice_fusion.1
  537.7 4.5 all_to_all.106
  544.3 42.1 %all-reduce = (f32[4,192]{1,0:T(4,128)S(1)}, f32[4,192]{1,0:T(4,128)S(1)}, f32[768]{0:T(1024)S(1)}, f32[768]{0:T(1024)S(1)}, f32[768]{0:T(1024)S(1)}, /*index=5*...) all-reduce(f32[4,192]{1,0:T(4,128)S(1)} %reshape_squeeze.11, ...), channel_id=1, replica_groups=mesh['dp'=2,'row'=4,'col'=4] {'col','row','dp'}, use_global_device_ids=true, to_apply=%region_21.22 | all-reduce | flops 11406 | bytes 91248 | tf_op jit(solution)/shard_map/psum | solution.py:356
  590.2 4.5 fusion.49
  594.6 4.1 all-to-all-start.10
  599.9 4.8 all-to-all-done.10
  604.7 4.0 all_to_all.107
  609.2 1.5 reshape.297
  610.7 37.9 %reduce-scatter.10.cloned.1.call-done = bf16[96,576]{1,0:T(8,128)(2,1)} async-done(((bf16[3072,576]{1,0:T(8,128)(2,1)}), bf16[96,576]{1,0:T(8,128)(2,1)}) %reduce-scatter.10.cloned.1.call-update) | async-done | bytes 110608 | tf_op jit(solution)/shard_map/reduce_scatter | solution.py:62
  648.6 2.2 all_gather.62
  651.6 146.0 %reduce-scatter.8.cloned.1.call-done = bf16[96,1728]{1,0:T(8,128)(2,1)} async-done(((bf16[3072,1728]{1,0:T(8,128)(2,1)}), bf16[96,1728]{1,0:T(8,128)(2,1)}) %reduce-scatter.8.cloned.1.call-update) | async-done | bytes 331792 | tf_op jit(solution)/shard_map/reduce_scatter | solution.py:62
  797.6 2.5 all_gather.63
  (238 shorter events, 38.4 us)
Async XLA Ops:
  7.2 1.0 copy-start
  7.2 13.4 %copy-start.30 = (f32[2,192]{1,0:T(2,128)S(1)}, f32[2,192]{1,0:T(2,128)}, u32[]{:S(2)}) copy-start(f32[2,192]{1,0:T(2,128)} %param.28) | copy-start | bytes 4612
  7.2 69.6 %all-gather.13.cloned.1.call-start = ((), (), s32[]{:S(2)}) async-start(), calls=%async_computation.15 | async-start | bytes 4055040 | tf_op jit(solution)/shard_map/all_gather | solution.py:50
  15.4 17.7 %all-to-all-start.1 = ((bf16[4,192,256]{2,1,0:T(8,128)(2,1)}), bf16[4,192,256]{2,1,0:T(8,128)(2,1)S(1)}, u32[]{:S(2)}, u32[]{:S(2)}) async-start(bf16[4,192,256]{2,1,0:T(8,128)(2,1)} %bitcast.2), calls=%async_computation.1 | async-start | bytes 786432 | tf_op jit(solution)/shard_map/all_to_all | solution.py:35
  20.6 114.8 %all-gather.15.cloned.1.call-start = ((), (), s32[]{:S(2)}) async-start(), calls=%async_computation.16 | async-start | bytes 2359296 | tf_op jit(solution)/shard_map/all_gather | solution.py:76
  33.1 201.3 %copy-start.5 = (bf16[4,192,256]{2,1,0:T(8,128)(2,1)}, bf16[4,192,256]{2,1,0:T(8,128)(2,1)S(1)}, u32[]{:S(2)}) copy-start(bf16[4,192,256]{2,1,0:T(8,128)(2,1)S(1)} %all-to-all-done.1) | copy-start | bytes 1179652
  80.4 33.8 %copy-start.25 = (bf16[192,192]{1,0:T(8,128)(2,1)S(1)}, bf16[192,192]{1,0:T(8,128)(2,1)}, u32[]{:S(2)}) copy-start(bf16[192,192]{1,0:T(8,128)(2,1)} %param.29) | copy-start | bytes 221188
  80.4 33.8 %copy-start.21 = (bf16[192,768]{1,0:T(8,128)(2,1)S(1)}, bf16[192,768]{1,0:T(8,128)(2,1)}, u32[]{:S(2)}) copy-start(bf16[192,768]{1,0:T(8,128)(2,1)} %param.35) | copy-start | bytes 884740
  112.7 3.2 copy-start.19
  112.8 7.7 copy-start.27
  112.8 7.7 copy-start.37
  112.8 11.0 %copy-start.31 = (f32[192]{0:T(256)S(1)}, f32[192]{0:T(256)}, u32[]{:S(2)}) copy-start(f32[192]{0:T(256)} %param.30) | copy-start | bytes 2308
  112.8 11.0 %copy-start.32 = (f32[192]{0:T(256)S(1)}, f32[192]{0:T(256)}, u32[]{:S(2)}) copy-start(f32[192]{0:T(256)} %param.31) | copy-start | bytes 2308
  112.8 11.0 %copy-start.33 = (f32[192]{0:T(256)S(1)}, f32[192]{0:T(256)}, u32[]{:S(2)}) copy-start(f32[192]{0:T(256)} %param.32) | copy-start | bytes 2308
  112.9 10.9 %copy-start.34 = (f32[192]{0:T(256)S(1)}, f32[192]{0:T(256)}, u32[]{:S(2)}) copy-start(f32[192]{0:T(256)} %param.36) | copy-start | bytes 2308
  112.9 10.9 %copy-start.35 = (f32[192]{0:T(256)S(1)}, f32[192]{0:T(256)}, u32[]{:S(2)}) copy-start(f32[192]{0:T(256)} %param.37) | copy-start | bytes 2308
  112.9 10.9 %copy-start.36 = (f32[192]{0:T(256)S(1)}, f32[192]{0:T(256)}, u32[]{:S(2)}) copy-start(f32[192]{0:T(256)} %param.38) | copy-start | bytes 2308
  114.1 101.4 %all-gather.17.cloned.1.call-start = ((), (), s32[]{:S(2)}) async-start(), calls=%async_computation.17 | async-start | bytes 11354112 | tf_op jit(solution)/shard_map/all_gather | solution.py:50
  117.0 50.1 %all-to-all-start.6 = ((bf16[2,192,512]{1,0,2:T(2,128)(2,1)}), bf16[2,192,512]{1,0,2:T(2,128)(2,1)S(1)}, u32[]{:S(2)}, u32[]{:S(2)}) async-start(bf16[2,192,512]{1,0,2:T(2,128)(2,1)} %copy.223), calls=%async_computation.6 | async-start | bytes 1048576 | tf_op jit(solution)/shard_map/all_to_all | solution.py:31
  122.5 1.3 copy-start.23
  123.8 15.5 %copy-start.26 = (s32[4,2,1,256]{3,1,0,2:T(2,128)}, s32[4,2,1,256]{3,1,0,2:T(2,128)S(1)}, u32[]{:S(2)}) copy-start(s32[4,2,1,256]{3,1,0,2:T(2,128)S(1)} %reshape.278) | copy-start | bytes 24580
  135.3 6.4 copy-start.3
  141.7 13.9 %copy-start.7 = (bf16[2048,3,2,64]{0,3,2,1:T(8,128)(2,1)S(1)}, bf16[2048,3,2,64]{0,3,2,1:T(8,128)(2,1)}, u32[]{:S(2)}) copy-start(bf16[2048,3,2,64]{0,3,2,1:T(8,128)(2,1)} %reshape_reshape.8) | copy-start | bytes 4718596
  155.6 15.8 %copy-start.29 = (f32[768]{0:T(1024)S(1)}, f32[768]{0:T(1024)}, u32[]{:S(2)}) copy-start(f32[768]{0:T(1024)} %param.34) | copy-start | bytes 9220
  167.1 0.8 copy-start.10
  167.9 63.0 %all-to-all-start.3 = ((bf16[4,256,192]{1,2,0:T(8,128)(2,1)}), bf16[4,256,192]{1,2,0:T(8,128)(2,1)S(1)}, u32[]{:S(2)}, u32[]{:S(2)}) async-start(bf16[4,256,192]{1,2,0:T(8,128)(2,1)} %copy.209), calls=%async_computation.3 | async-start | bytes 786432 | tf_op jit(solution)/shard_map/all_to_all | solution.py:67
  230.9 17.2 %copy-start.8 = (bf16[4,256,192]{1,2,0:T(8,128)(2,1)}, bf16[4,256,192]{1,2,0:T(8,128)(2,1)S(1)}, u32[]{:S(2)}) copy-start(bf16[4,256,192]{1,2,0:T(8,128)(2,1)S(1)} %all-to-all-done.3) | copy-start | bytes 1179652
  230.9 19.7 %all-to-all-start.7 = ((bf16[4,192,256]{2,1,0:T(8,128)(2,1)}), bf16[4,192,256]{2,1,0:T(8,128)(2,1)S(1)}, u32[]{:S(2)}, u32[]{:S(2)}) async-start(bf16[4,192,256]{2,1,0:T(8,128)(2,1)} %bitcast.54), calls=%async_computation.7 | async-start | bytes 786432 | tf_op jit(solution)/shard_map/all_to_all | solution.py:35
  234.4 155.7 %reduce-scatter.6.cloned.1.call-start = ((), (), s32[]{:S(2)}) async-start(), calls=%async_computation.18 | async-start | bytes 2359296 | tf_op jit(solution)/shard_map/reduce_scatter | solution.py:84
  234.4 13.7 %slice-start.2 = ((s8[4718592]{0:T(1024)(128)(4,1)}), s8[4194304]{0:T(1024)(128)(4,1)S(1)}, s32[]{:S(2)}) async-start(s8[4718592]{0:T(1024)(128)(4,1)} %bitcast.418), calls=%async_computation.24 | async-start | bytes 8388608
  236.1 12.0 %slice-start.3 = ((s8[4718592]{0:T(1024)(128)(4,1)}), s8[524288]{0:T(1024)(128)(4,1)S(1)}, s32[]{:S(2)}) async-start(s8[4718592]{0:T(1024)(128)(4,1)} %bitcast.418), calls=%async_computation.25 | async-start | bytes 1048576
  248.1 2.4 copy-start.14
  250.6 8.3 %slice-start = ((s8[4718592]{0:T(1024)(128)(4,1)}), s8[4194304]{0:T(1024)(128)(4,1)S(1)}, s32[]{:S(2)}) async-start(s8[4718592]{0:T(1024)(128)(4,1)} %bitcast.414), calls=%async_computation.22 | async-start | bytes 8388608
  251.4 7.5 copy-start.11
  251.5 7.5 slice-start.1
  258.9 2.6 copy-start.16
  312.7 16.4 %copy-start.4 = (bf16[1024,3,64]{0,2,1:T(8,128)(2,1)S(1)}, bf16[1024,3,64]{0,2,1:T(8,128)(2,1)}, u32[]{:S(2)}) copy-start(bf16[1024,3,64]{0,2,1:T(8,128)(2,1)} %copy-done.3) | copy-start | bytes 1179652
  329.1 4.6 copy-start.2
  339.0 5.1 copy-start.41
  339.0 5.2 copy-start.24
  339.0 15.5 %copy-start.13 = (bf16[256,768]{0,1:T(8,128)(2,1)S(1)}, bf16[256,768]{0,1:T(8,128)(2,1)}, u32[]{:S(2)}) copy-start(bf16[256,768]{0,1:T(8,128)(2,1)} %get-tuple-element.181) | copy-start | bytes 1179652
  339.0 15.5 %copy-start.38 = (f32[128]{0:T(128)S(1)}, f32[128]{0:T(128)}, u32[]{:S(2)}) copy-start(f32[128]{0:T(128)} %param.40) | copy-start | bytes 1540
  390.0 6.4 copy-start.20
  390.0 6.4 copy-start.39
  390.0 6.8 copy-start.28
  390.0 6.8 copy-start.40
  391.4 33.6 %copy-start.6 = (bf16[4,192,256]{2,1,0:T(8,128)(2,1)S(1)}, bf16[4,192,256]{2,1,0:T(8,128)(2,1)}, u32[]{:S(2)}) copy-start(bf16[4,192,256]{2,1,0:T(8,128)(2,1)} %copy-done.5) | copy-start | bytes 1179652
  392.6 32.4 %all-to-all-start.9 = ((bf16[4,256,576]{1,2,0:T(8,128)(2,1)}), bf16[4,256,576]{1,2,0:T(8,128)(2,1)S(1)}, u32[]{:S(2)}, u32[]{:S(2)}) async-start(bf16[4,256,576]{1,2,0:T(8,128)(2,1)} %bitcast.412), calls=%async_computation.10 | async-start | bytes 2359296 | tf_op jit(solution)/shard_map/all_to_all | solution.py:67
  396.1 140.0 %all-reduce.4.cloned.1.call-start = ((), (), s32[]{:S(2)}) async-start(), calls=%async_computation.21 | async-start | bytes 917504 | tf_op jit(solution)/shard_map/psum | solution.py:356
  400.8 247.8 %reduce-scatter.10.cloned.1.call-start = ((), (), s32[]{:S(2)}) async-start(), calls=%async_computation.20 | async-start | bytes 4055040 | tf_op jit(solution)/shard_map/reduce_scatter | solution.py:62
  433.9 3.6 copy-start.9
  433.9 363.7 %reduce-scatter.8.cloned.1.call-start = ((), (), s32[]{:S(2)}) async-start(), calls=%async_computation.19 | async-start | bytes 11354112 | tf_op jit(solution)/shard_map/reduce_scatter | solution.py:62
  433.9 4.1 copy-start.12
  434.0 4.1 copy-start.15
  438.1 1.4 copy-start.17
  445.9 144.3 %copy-start.18 = (f32[768,256]{1,0:T(8,128)S(1)}, f32[768,256]{1,0:T(8,128)}, u32[]{:S(2)}) copy-start(f32[768,256]{1,0:T(8,128)} %get-tuple-element.164) | copy-start | bytes 2359300
  455.3 82.3 %all-to-all-start.4 = ((bf16[4,192,256]{2,1,0:T(8,128)(2,1)}), bf16[4,192,256]{2,1,0:T(8,128)(2,1)S(1)}, u32[]{:S(2)}, u32[]{:S(2)}) async-start(bf16[4,192,256]{2,1,0:T(8,128)(2,1)} %bitcast.39), calls=%async_computation.4 | async-start | bytes 786432 | tf_op jit(solution)/shard_map/all_to_all | solution.py:43
  594.6 10.1 %all-to-all-start.10 = ((bf16[4,192,256]{2,1,0:T(8,128)(2,1)}), bf16[4,192,256]{2,1,0:T(8,128)(2,1)S(1)}, u32[]{:S(2)}, u32[]{:S(2)}) async-start(bf16[4,192,256]{2,1,0:T(8,128)(2,1)} %bitcast.73), calls=%async_computation.11 | async-start | bytes 786432 | tf_op jit(solution)/shard_map/all_to_all | solution.py:43
  609.2 193.3 %copy-start.1 = (bf16[192,576]{1,0:T(8,128)(2,1)S(1)}, bf16[192,576]{1,0:T(8,128)(2,1)}, u32[]{:S(2)}) copy-start(bf16[192,576]{1,0:T(8,128)(2,1)} %param.27) | copy-start | bytes 663556
  609.2 192.7 %copy-start.22 = (f32[128,128]{1,0:T(8,128)S(1)}, f32[128,128]{1,0:T(8,128)}, u32[]{:S(2)}) copy-start(f32[128,128]{1,0:T(8,128)} %get-tuple-element.227) | copy-start | bytes 196612
Sparse Core Ops, SparseCore 0:
  11.5 65.3 all-gather.12
  114.2 8.1 all-gather.14
  125.3 90.1 all-gather.16
  344.2 8.2 reduce-scatter.5
  402.6 133.5 all-reduce.3
  541.4 107.1 reduce-scatter.9
  654.6 142.9 reduce-scatter.7

commit v2 on v1

--- a/solution.py
+++ b/solution.py
@@ -1,6 +1,9 @@
+import functools
 import jax
 import jax.numpy as jnp
 from jax import lax
+from jax.experimental import pallas as pl
+from jax.experimental.pallas import tpu as pltpu
 from jax.sharding import PartitionSpec as P
 
 HD = 64
@@ -147,7 +150,7 @@
     return d_q, d_k, d_v
 
 
-def local(
+def general_local(
     tokens,
     segments,
     labels,
@@ -387,6 +390,1105 @@
     )
 
 
+MESH = pl.DeviceIdType.MESH
+HBM = pl.BlockSpec(memory_space=pl.ANY)
+
+
+def place():
+    return lax.axis_index("dp"), lax.axis_index("row"), lax.axis_index("col")
+
+
+def greet(peers, guarded=()):
+    barrier = pltpu.get_barrier_semaphore()
+    for peer in peers:
+        pl.semaphore_signal(barrier, inc=1, device_id=peer, device_id_type=MESH)
+    for there, peer in guarded:
+
+        @pl.when(there)
+        def _():
+            pl.semaphore_signal(barrier, inc=1, device_id=peer, device_id_type=MESH)
+
+    amount = len(peers)
+    for there, _ in guarded:
+        amount = amount + there.astype(jnp.int32)
+    pl.semaphore_wait(barrier, amount)
+
+
+def rcopy(src, dst, send, recv, peer):
+    return pltpu.make_async_remote_copy(
+        src_ref=src, dst_ref=dst, send_sem=send, recv_sem=recv, device_id=peer, device_id_type=MESH
+    )
+
+
+def take_copies(src, out, local, send, recv):
+    d, r, c = place()
+    own = out.shape[2]
+    moves = []
+    for i in range(2):
+        for far in range(2):
+            row, core = 2 * d + i, d ^ far
+            piece = src.at[i, :, pl.ds(pl.multiple_of(core * own, own), own)]
+            here = (row == r) if far == 0 else None
+
+            def start(piece=piece, row=row, core=core, slot=2 * i + far, here=here):
+                def away():
+                    rcopy(piece, out.at[r], send.at[slot], recv.at[r], (core, row, c)).start()
+
+                if here is None:
+                    away()
+                else:
+                    pl.when(jnp.logical_not(here))(away)
+
+                    @pl.when(here)
+                    def _():
+                        pltpu.make_async_copy(piece, out.at[r], local).start()
+
+            def wait(piece=piece, row=row, core=core, slot=2 * i + far, here=here):
+                def away():
+                    rcopy(piece, out.at[r], send.at[slot], recv.at[r], (core, row, c)).wait_send()
+
+                if here is None:
+                    away()
+                else:
+                    pl.when(jnp.logical_not(here))(away)
+
+                    @pl.when(here)
+                    def _():
+                        pltpu.make_async_copy(piece, out.at[r], local).wait()
+
+            moves.append((start, wait))
+    for row in range(4):
+
+        def arrive(row=row):
+            @pl.when(jnp.logical_not((row == r) & (r // 2 == d)))
+            def _():
+                piece = src.at[0, :, pl.ds(0, own)]
+                rcopy(piece, out.at[row], send.at[0], recv.at[row], (d, r, c)).wait_recv()
+
+        moves.append((lambda: None, arrive))
+    return moves
+
+
+def gather_kernel(kinds, *refs):
+    shards, refs = refs[:kinds], refs[kinds:]
+    (tok, cot, ints), refs = refs[:3], refs[3:]
+    outs, refs = refs[:kinds], refs[kinds:]
+    (tok_out, cot_out, ints_out), refs = refs[:3], refs[3:]
+    own_sem, zs, zr, xs, xr, ys, yr, cs, cr, ps, pr, tl, ts, tr, il = refs
+    d, r, c = place()
+    cols = 4
+    xn, yn, pn = (d, r ^ 1, c), (d, r ^ 2, c), (1 - d, r, c)
+    up, down = (d, r, c + 1), (d, r, c - 1)
+    has_up, has_down = c < cols - 1, c > 0
+    plane = [(d ^ (j // 4), r ^ (j % 4), c) for j in range(1, 8)]
+    greet(plane, [(has_up, up), (has_down, down)])
+    ahead = [take_copies(tok, tok_out, tl.at[0], ts.at[0], tr.at[0])]
+    for start, _ in ahead[0]:
+        start()
+    pltpu.make_async_copy(ints, ints_out.at[d], il.at[0]).start()
+    rcopy(ints, ints_out.at[d], il.at[1], il.at[2], pn).start()
+    halves = [shard.shape[0] // 2 for shard in shards]
+
+    def z_send(k, at, way, hop):
+        src = shards[k] if hop == 1 else outs[k].at[at, r, d]
+        return rcopy(
+            src, outs[k].at[at, r, d], zs.at[k, way, hop - 1], zr.at[k, way, hop - 1], up if way == 0 else down
+        )
+
+    def src_of(k, at, own):
+        return shards[k] if own else outs[k].at[at, r, d]
+
+    def to_x(k, at, own):
+        return rcopy(src_of(k, at, own), outs[k].at[at, r, d], xs.at[k, at], xr.at[k, at], xn)
+
+    def to_y(k, at, own):
+        return rcopy(src_of(k, at, own), outs[k].at[at, r, d], ys.at[k, at], yr.at[k, at], yn)
+
+    def to_p(k, at, own):
+        return rcopy(src_of(k, at, own), outs[k].at[at, r, d], ps.at[k, at, 0], pr.at[k, at, 0], pn)
+
+    def relay(k, at, which):
+        row = r ^ 1 if which == 0 else r ^ 2
+        ref = outs[k].at[at, row, d, pl.ds(which * halves[k], halves[k])]
+        return rcopy(ref, ref, cs.at[k, at, which], cr.at[k, at, which], yn if which == 0 else xn)
+
+    def pass_p(k, at, bit):
+        ref = outs[k].at[at, r ^ bit, d]
+        return rcopy(ref, ref, ps.at[k, at, bit], pr.at[k, at, bit], pn)
+
+    def got_x(k, at):
+        ref = outs[k].at[at, r ^ 1, d]
+        rcopy(ref, ref, xs.at[k, at], xr.at[k, at], xn).wait_recv()
+
+    def got_y(k, at):
+        ref = outs[k].at[at, r ^ 2, d]
+        rcopy(ref, ref, ys.at[k, at], yr.at[k, at], yn).wait_recv()
+
+    def got_corner(k, at):
+        for which in range(2):
+            ref = outs[k].at[at, r ^ 3, d, pl.ds(which * halves[k], halves[k])]
+            rcopy(ref, ref, cs.at[k, at, which], cr.at[k, at, which], xn).wait_recv()
+
+    def got_p(k, at, bit):
+        ref = outs[k].at[at, r ^ bit, 1 - d]
+        rcopy(ref, ref, ps.at[k, at, bit], pr.at[k, at, bit], pn).wait_recv()
+
+    for k in range(kinds):
+        pltpu.make_async_copy(shards[k], outs[k].at[c, r, d], own_sem.at[k]).start()
+
+        @pl.when(has_up)
+        def _():
+            z_send(k, c, 0, 1).start()
+
+        @pl.when(has_down)
+        def _():
+            z_send(k, c, 1, 1).start()
+
+    def spread(k, at, own):
+        to_x(k, at, own).start()
+        to_y(k, at, own).start()
+        to_p(k, at, own).start()
+
+    def onward(k, at):
+        got_x(k, at)
+        relay(k, at, 0).start()
+        pass_p(k, at, 1).start()
+        got_y(k, at)
+        relay(k, at, 1).start()
+        pass_p(k, at, 2).start()
+
+    steps = [(0, 0)] + [(way, hop) for hop in (1, 2, 3) for way in (0, 1)]
+    jobs = [(k, way, hop) for k in range(kinds) for way, hop in steps]
+
+    def at_of(way, hop):
+        return c - hop if way == 0 else c + hop
+
+    def valid(way, hop):
+        return c >= hop if way == 0 else c + hop < cols
+
+    def guard(way, hop, body):
+        if hop == 0:
+            body()
+        else:
+            pl.when(valid(way, hop))(body)
+
+    def first(k, way, hop):
+        def body():
+            at = at_of(way, hop)
+            if hop:
+                z_send(k, at, way, hop).wait_recv()
+                if hop < 3:
+                    can = has_up if way == 0 else has_down
+
+                    @pl.when(can)
+                    def _():
+                        z_send(k, at, way, hop + 1).start()
+
+            spread(k, at, hop == 0)
+
+        guard(way, hop, body)
+
+    def second(k, way, hop):
+        guard(way, hop, lambda: onward(k, at_of(way, hop)))
+
+    def third(k, way, hop):
+        def body():
+            at = at_of(way, hop)
+            got_corner(k, at)
+            pass_p(k, at, 3).start()
+
+        guard(way, hop, body)
+
+    lag = 3
+    for i in range(len(jobs) + 2 * lag):
+        if i < len(jobs):
+            first(*jobs[i])
+        if 0 <= i - lag < len(jobs):
+            second(*jobs[i - lag])
+        if 0 <= i - 2 * lag < len(jobs):
+            third(*jobs[i - 2 * lag])
+
+    ahead.append(take_copies(cot, cot_out, tl.at[1], ts.at[1], tr.at[1]))
+    for start, _ in ahead[1]:
+        start()
+    for k in range(kinds):
+        pltpu.make_async_copy(shards[k], outs[k].at[c, r, d], own_sem.at[k]).wait()
+        for way, hop in steps:
+
+            def body():
+                at = at_of(way, hop)
+                own = hop == 0
+                to_x(k, at, own).wait_send()
+                to_y(k, at, own).wait_send()
+                to_p(k, at, own).wait_send()
+                for which in range(2):
+                    relay(k, at, which).wait_send()
+                for bit in (1, 2, 3):
+                    pass_p(k, at, bit).wait_send()
+                for bit in range(4):
+                    got_p(k, at, bit)
+                if hop < 3:
+                    if own:
+
+                        @pl.when(has_up)
+                        def _():
+                            z_send(k, c, 0, 1).wait_send()
+
+                        @pl.when(has_down)
+                        def _():
+                            z_send(k, c, 1, 1).wait_send()
+                    else:
+                        can = has_up if way == 0 else has_down
+
+                        @pl.when(can)
+                        def _():
+                            z_send(k, at, way, hop + 1).wait_send()
+
+            guard(way, hop, body)
+    for moves in ahead:
+        for _, wait in moves:
+            wait()
+    pltpu.make_async_copy(ints, ints_out.at[d], il.at[0]).wait()
+    rcopy(ints, ints_out.at[1 - d], il.at[1], il.at[2], pn).wait()
+
+
+def gather_fast(shards, tokens, cotangent, ints, cid):
+    kinds = len(shards)
+    dma = pltpu.SemaphoreType.DMA
+    _, feats, cols = tokens.shape
+    taken = jax.ShapeDtypeStruct((4, feats, cols // 2), tokens.dtype)
+    return pl.pallas_call(
+        functools.partial(gather_kernel, kinds),
+        out_shape=[jax.ShapeDtypeStruct((4, 4, 2) + s.shape, s.dtype) for s in shards]
+        + [taken, taken, jax.ShapeDtypeStruct((2,) + ints.shape, ints.dtype)],
+        in_specs=[HBM] * (kinds + 3),
+        out_specs=[HBM] * (kinds + 3),
+        scratch_shapes=[
+            dma((kinds,)),
+            dma((kinds, 2, 3)), dma((kinds, 2, 3)),
+            dma((kinds, 4)), dma((kinds, 4)),
+            dma((kinds, 4)), dma((kinds, 4)),
+            dma((kinds, 4, 2)), dma((kinds, 4, 2)),
+            dma((kinds, 4, 4)), dma((kinds, 4, 4)),
+            dma((2,)), dma((2, 4)), dma((2, 4)), dma((3,)),
+        ],
+        compiler_params=pltpu.CompilerParams(collective_id=cid, has_side_effects=True),
+        name="gather_all",
+    )(*shards, tokens, cotangent, ints)
+
+
+def scatter_kernel(kinds, *refs):
+    grads, outs = refs[:kinds], refs[kinds : 2 * kinds]
+    (acc, precv, xr1, yr1, xr2, yr2, zup, zdn, fin) = refs[2 * kinds : 2 * kinds + 9]
+    (ls, ps, pr, xs1, xm1, ys1, ym1, xs2, xm2, ys2, ym2, us, um, ds, dm, fs, fm, os) = refs[2 * kinds + 9 :]
+    d, r, c = place()
+    cols = 4
+    chunks = kinds * cols
+    xn, yn, pn = (d, r ^ 1, c), (d, r ^ 2, c), (1 - d, r, c)
+    up, down = (d, r, c + 1), (d, r, c - 1)
+    greet([xn, yn, pn], [(c < cols - 1, up), (c > 0, down)])
+    half = acc.shape[2] // 2
+    first, last = pl.ds(0, half), pl.ds(half, half)
+
+    def split(i):
+        k = i // cols
+        j = i - k * cols
+        at = jnp.where(j == 0, 0, jnp.where(j == 1, 3, j - 1))
+        return k, at
+
+    def at_static(i):
+        return i // cols, (0, 3, 1, 2)[i % cols]
+
+    def load(i):
+        k, at = at_static(i)
+        return pltpu.make_async_copy(grads[k].at[at, :, d], acc.at[i], ls.at[i])
+
+    def pair(i):
+        k, at = at_static(i)
+        return rcopy(grads[k].at[at, :, 1 - d], precv.at[i], ps.at[i], pr.at[i], pn)
+
+    for i in range(chunks):
+        pair(i).start()
+        load(i).start()
+
+    def x1(i, j):
+        return rcopy(acc.at[i, r ^ 1 ^ (2 * j), first], xr1.at[i, j], xs1.at[i, j], xm1.at[i, j], xn)
+
+    def y1(i, j):
+        return rcopy(acc.at[i, r ^ 2 ^ j, last], yr1.at[i, j], ys1.at[i, j], ym1.at[i, j], yn)
+
+    def y2(i):
+        return rcopy(acc.at[i, r ^ 2, first], yr2.at[i], ys2.at[i], ym2.at[i], yn)
+
+    def x2(i):
+        return rcopy(acc.at[i, r ^ 1, last], xr2.at[i], xs2.at[i], xm2.at[i], xn)
+
+    def to_up(i):
+        return rcopy(acc.at[i, r], zup.at[i], us.at[i], um.at[i], up)
+
+    def to_down(i):
+        return rcopy(acc.at[i, r], zdn.at[i], ds.at[i], dm.at[i], down)
+
+    def stage1(i):
+        pltpu.make_async_copy(precv.at[i], acc.at[i], ls.at[i]).wait()
+        rcopy(acc.at[i], precv.at[i], ps.at[i], pr.at[i], pn).wait_recv()
+
+        @pl.loop(0, 4)
+        def _(row):
+            acc[i, row] = acc[i, row] + precv[i, row]
+
+        x1(i, 1).start()
+        y1(i, 1).start()
+        x1(i, 0).start()
+        y1(i, 0).start()
+
+    def stage2(i):
+        x1(i, 1).wait_recv()
+        acc[i, r ^ 2, first] = acc[i, r ^ 2, first] + xr1[i, 1]
+        y2(i).start()
+        y1(i, 1).wait_recv()
+        acc[i, r ^ 1, last] = acc[i, r ^ 1, last] + yr1[i, 1]
+        x2(i).start()
+        x1(i, 0).wait_recv()
+        acc[i, r, first] = acc[i, r, first] + xr1[i, 0]
+        y1(i, 0).wait_recv()
+        acc[i, r, last] = acc[i, r, last] + yr1[i, 0]
+
+    def stage3(i):
+        y2(i).wait_recv()
+        acc[i, r, first] = acc[i, r, first] + yr2[i]
+        x2(i).wait_recv()
+        acc[i, r, last] = acc[i, r, last] + xr2[i]
+
+    def stage4(i, hops):
+        k, at = split(i)
+
+        @pl.when((at > c) & (c == hops))
+        def _():
+            @pl.when(c > 0)
+            def _():
+                to_up(i).wait_recv()
+                acc[i, r] = acc[i, r] + zup[i]
+
+            to_up(i).start()
+
+        @pl.when((at < c) & (cols - 1 - c == hops))
+        def _():
+            @pl.when(c < cols - 1)
+            def _():
+                to_down(i).wait_recv()
+                acc[i, r] = acc[i, r] + zdn[i]
+
+            to_down(i).start()
+
+        @pl.when((at == c) & (jnp.maximum(c, cols - 1 - c) == hops))
+        def _():
+            @pl.when(c > 0)
+            def _():
+                to_up(i).wait_recv()
+                acc[i, r] = acc[i, r] + zup[i]
+
+            @pl.when(c < cols - 1)
+            def _():
+                to_down(i).wait_recv()
+                acc[i, r] = acc[i, r] + zdn[i]
+
+            fin[k, d] = acc[i, r]
+            rcopy(fin.at[k, d], fin.at[k, d], fs.at[k], fm.at[k], pn).start()
+
+    stages = [(0, stage1), (2, stage2), (4, stage3)]
+    stages += [(5 + h, functools.partial(lambda h, i: stage4(i, h), h)) for h in range(cols)]
+    ending = stages[-1][0]
+
+    @pl.loop(0, chunks + ending)
+    def _(step):
+        for lag, stage in stages:
+
+            @pl.when((step >= lag) & (step - lag < chunks))
+            def _():
+                stage(step - lag)
+
+    @pl.loop(0, chunks)
+    def _(i):
+        k, at = split(i)
+        rcopy(acc.at[i], precv.at[i], ps.at[i], pr.at[i], pn).wait_send()
+        for j in range(2):
+            x1(i, j).wait_send()
+            y1(i, j).wait_send()
+        y2(i).wait_send()
+        x2(i).wait_send()
+
+        @pl.when(at > c)
+        def _():
+            to_up(i).wait_send()
+
+        @pl.when(at < c)
+        def _():
+            to_down(i).wait_send()
+
+    for k in range(kinds):
+        rcopy(fin.at[k, 1 - d], fin.at[k, 1 - d], fs.at[k], fm.at[k], pn).wait()
+        pltpu.make_async_copy(fin.at[k], outs[k], os.at[k]).start()
+    for k in range(kinds):
+        pltpu.make_async_copy(fin.at[k], outs[k], os.at[k]).wait()
+
+
+def scatter_fast(grads, cid):
+    kinds = len(grads)
+    chunks = kinds * 4
+    n, w = grads[0].shape[3:]
+    dma = pltpu.SemaphoreType.DMA
+    dt = grads[0].dtype
+    return pl.pallas_call(
+        functools.partial(scatter_kernel, kinds),
+        out_shape=[jax.ShapeDtypeStruct((2, n, w), dt)] * kinds,
+        in_specs=[HBM] * kinds,
+        out_specs=[HBM] * kinds,
+        scratch_shapes=[
+            pltpu.VMEM((chunks, 4, n, w), dt),
+            pltpu.VMEM((chunks, 4, n, w), dt),
+            pltpu.VMEM((chunks, 2, n // 2, w), dt),
+            pltpu.VMEM((chunks, 2, n // 2, w), dt),
+            pltpu.VMEM((chunks, n // 2, w), dt),
+            pltpu.VMEM((chunks, n // 2, w), dt),
+            pltpu.VMEM((chunks, n, w), dt),
+            pltpu.VMEM((chunks, n, w), dt),
+            pltpu.VMEM((kinds, 2, n, w), dt),
+            dma((chunks,)), dma((chunks,)), dma((chunks,)),
+            dma((chunks, 2)), dma((chunks, 2)), dma((chunks, 2)), dma((chunks, 2)),
+            dma((chunks,)), dma((chunks,)), dma((chunks,)), dma((chunks,)),
+            dma((chunks,)), dma((chunks,)), dma((chunks,)), dma((chunks,)),
+            dma((kinds,)), dma((kinds,)), dma((kinds,)),
+        ],
+        compiler_params=pltpu.CompilerParams(
+            collective_id=cid, has_side_effects=True, vmem_limit_bytes=48 * 1024 * 1024
+        ),
+        name="scatter_all",
+    )(*grads)
+
+
+def give_kernel(src_ref, out_ref, local, send, recv):
+    d, r, c = place()
+    own = src_ref.shape[2]
+    greet([(d ^ (j // 4), r ^ (j % 4), c) for j in range(1, 8)])
+    home = r // 2
+
+    def slot(i, core):
+        return out_ref.at[i, :, pl.ds(pl.multiple_of(core * own, own), own)]
+
+    def move(row):
+        return rcopy(src_ref.at[row], slot(r % 2, d), send.at[row], recv.at[r % 2, d], (home, row, c))
+
+    def stay():
+        return pltpu.make_async_copy(src_ref.at[r], slot(r % 2, d), local)
+
+    for row in range(4):
+        here = (row == r) & (home == d)
+
+        @pl.when(jnp.logical_not(here))
+        def _():
+            move(row).start()
+
+    @pl.when(home == d)
+    def _():
+        stay().start()
+
+    for row in range(4):
+        here = (row == r) & (home == d)
+
+        @pl.when(jnp.logical_not(here))
+        def _():
+            move(row).wait_send()
+
+    @pl.when(home == d)
+    def _():
+        stay().wait()
+
+    for i in range(2):
+        for core in range(2):
+
+            @pl.when(jnp.logical_not((2 * d + i == r) & (core == d)))
+            def _():
+                rcopy(src_ref.at[0], slot(i, core), send.at[0], recv.at[i, core], (d, r, c)).wait_recv()
+
+
+def give_fast(values, cid):
+    width, own = values.shape
+    dma = pltpu.SemaphoreType.DMA
+    return pl.pallas_call(
+        give_kernel,
+        out_shape=jax.ShapeDtypeStruct((2, width // 4, 2 * own), values.dtype),
+        in_specs=[HBM],
+        out_specs=HBM,
+        scratch_shapes=[dma, dma((4,)), dma((2, 2))],
+        compiler_params=pltpu.CompilerParams(collective_id=cid, has_side_effects=True),
+        name="give_back",
+    )(values.reshape(4, width // 4, own))
+
+
+VM = pl.BlockSpec(memory_space=pltpu.VMEM)
+
+
+def swap_kernel(count, *refs):
+    srcs, outs = refs[:count], refs[count : 2 * count]
+    send, recv = refs[2 * count :]
+    d, r, c = place()
+    greet([(d, r, c ^ j) for j in (1, 2, 3)])
+
+    def move(k, j):
+        return rcopy(srcs[k].at[c ^ j], outs[k].at[c], send.at[k, j], recv.at[k, j], (d, r, c ^ j))
+
+    for j in (3, 2, 1):
+        for k in range(count):
+            move(k, j).start()
+    for k in range(count):
+        outs[k][c] = srcs[k][c]
+    for j in (1, 2, 3):
+        for k in range(count):
+            move(k, j).wait()
+
+
+def swap_fast(arrays, cid):
+    count = len(arrays)
+    dma = pltpu.SemaphoreType.DMA
+    return pl.pallas_call(
+        functools.partial(swap_kernel, count),
+        out_shape=[jax.ShapeDtypeStruct(a.shape, a.dtype) for a in arrays],
+        in_specs=[VM] * count,
+        out_specs=[VM] * count,
+        scratch_shapes=[dma((count, 4)), dma((count, 4))],
+        compiler_params=pltpu.CompilerParams(collective_id=cid, has_side_effects=True),
+        name="swap_cols",
+    )(*arrays)
+
+
+def heads_kernel(q_ref, kv_ref, q_out, kv_out, send, recv, psend, precv):
+    d, r, c = place()
+    pn = (1 - d, r, c)
+    greet([(d, r, c ^ j) for j in (1, 2, 3)] + [pn])
+
+    def kv(j):
+        return rcopy(kv_ref.at[c ^ j], kv_out.at[c, d], send.at[0, j], recv.at[0, j], (d, r, c ^ j))
+
+    def q(j):
+        return rcopy(q_ref.at[c ^ j], q_out.at[c], send.at[1, j], recv.at[1, j], (d, r, c ^ j))
+
+    def pair(j):
+        src = kv_ref.at[c] if j == 0 else kv_out.at[c ^ j, d]
+        return rcopy(src, kv_out.at[c ^ j, d], psend.at[j], precv.at[j], pn)
+
+    for j in (3, 2, 1):
+        kv(j).start()
+    pair(0).start()
+    for j in (3, 2, 1):
+        q(j).start()
+    kv_out[c, d] = kv_ref[c]
+    q_out[c] = q_ref[c]
+    for j in (1, 2, 3):
+        kv(j).wait_recv()
+        pair(j).start()
+    for j in (1, 2, 3):
+        q(j).wait()
+        kv(j).wait_send()
+    for j in range(4):
+        pair(j).wait()
+
+
+def heads_fast(q, kv, cid):
+    cols, own, wide = kv.shape
+    dma = pltpu.SemaphoreType.DMA
+    return pl.pallas_call(
+        heads_kernel,
+        out_shape=[
+            jax.ShapeDtypeStruct(q.shape, q.dtype),
+            jax.ShapeDtypeStruct((cols, 2, own, wide), kv.dtype),
+        ],
+        in_specs=[VM] * 2,
+        out_specs=[VM] * 2,
+        scratch_shapes=[dma((2, 4)), dma((2, 4)), dma((4,)), dma((4,))],
+        compiler_params=pltpu.CompilerParams(collective_id=cid, has_side_effects=True),
+        name="to_heads",
+    )(q, kv)
+
+
+def tokens_kernel(q_ref, kv_ref, q_out, kv_out, total, theirs, send, recv, psend, precv):
+    d, r, c = place()
+    pn = (1 - d, r, c)
+    greet([(d, r, c ^ j) for j in (1, 2, 3)] + [pn])
+
+    def pair(j):
+        return rcopy(kv_ref.at[c ^ j, 1 - d], theirs.at[c ^ j], psend.at[j], precv.at[j], pn)
+
+    def kv(j):
+        return rcopy(total.at[c ^ j], kv_out.at[c], send.at[0, j], recv.at[0, j], (d, r, c ^ j))
+
+    def q(j):
+        return rcopy(q_ref.at[c ^ j], q_out.at[c], send.at[1, j], recv.at[1, j], (d, r, c ^ j))
+
+    for j in (3, 2, 1, 0):
+        pair(j).start()
+    for j in (3, 2, 1):
+        q(j).start()
+    q_out[c] = q_ref[c]
+    for j in (3, 2, 1):
+        pair(j).wait_recv()
+        total[c ^ j] = kv_ref[c ^ j, d] + theirs[c ^ j]
+        kv(j).start()
+    pair(0).wait_recv()
+    kv_out[c] = kv_ref[c, d] + theirs[c]
+    for j in range(4):
+        pair(j).wait_send()
+    for j in (1, 2, 3):
+        q(j).wait()
+        kv(j).wait()
+
+
+def tokens_fast(q, kv, cid):
+    cols, _, own, wide = kv.shape
+    dma = pltpu.SemaphoreType.DMA
+    piece = jax.ShapeDtypeStruct((cols, own, wide), kv.dtype)
+    return pl.pallas_call(
+        tokens_kernel,
+        out_shape=[jax.ShapeDtypeStruct(q.shape, q.dtype), piece],
+        in_specs=[VM] * 2,
+        out_specs=[VM] * 2,
+        scratch_shapes=[
+            pltpu.VMEM((cols, own, wide), kv.dtype),
+            pltpu.VMEM((cols, own, wide), kv.dtype),
+            dma((2, 4)), dma((2, 4)), dma((4,)), dma((4,)),
+        ],
+        compiler_params=pltpu.CompilerParams(collective_id=cid, has_side_effects=True),
+        name="to_tokens",
+    )(q, kv)
+
+
+def dot(a, b, contract=((1,), (0,))):
+    return lax.dot_general(a, b, (contract, ((), ())), preferred_element_type=f32)
+
+
+def block_rows(ref, heads, scale, out):
+    own = ref.shape[-1]
+    for h in range(heads):
+        for g in range(heads):
+            spot = (pl.ds(h * HD, HD), pl.ds(g * own, own))
+            if h == g:
+                out[spot] = ref[0, pl.ds(h * HD, HD)] * jnp.asarray(scale, out.dtype)
+            else:
+                out[spot] = jnp.zeros((HD, own), out.dtype)
+
+
+def attn_fwd_kernel(heads, scale, bounds, q_ref, kv_ref, qseg_ref, kseg_ref, ctx_ref, lse_ref, kn, q3, s_scr, o_scr):
+    step = pl.program_id(0)
+    tiles, _, tile = kv_ref.shape
+    wide = heads * HD
+    own = q_ref.shape[-1]
+
+    @pl.when(step == 0)
+    def _():
+        @pl.loop(0, tiles)
+        def _(j):
+            kn[j] = kv_ref[j, pl.ds(0, wide)].astype(f32).T.astype(bf16)
+
+    block_rows(q_ref, heads, scale, q3)
+    low, high = bounds[step, 0], bounds[step, 1]
+    qseg = jnp.concatenate([qseg_ref[0]] * heads, axis=1)
+
+    def one(j, top):
+        s = dot(kn[j], q3[...])
+        s = jnp.where(kseg_ref[j] == qseg, s, masked_value)
+        s_scr[j] = s
+        return jnp.maximum(top, jnp.max(s, axis=0, keepdims=True))
+
+    top = lax.fori_loop(low, high, one, jnp.full((1, heads * own), masked_value, f32))
+    o_scr[...] = jnp.zeros_like(o_scr)
+
+    def two(j, total):
+        p = jnp.exp(s_scr[j] - top)
+        low_p = p.astype(bf16)
+        for h in range(heads):
+            rows = pl.ds(h * HD, HD)
+            v = kv_ref[j, pl.ds(wide + h * HD, HD)]
+            o_scr[rows] += dot(v, low_p[:, h * own : (h + 1) * own])
+        return total + jnp.sum(p, axis=0, keepdims=True)
+
+    total = lax.fori_loop(low, high, two, jnp.zeros((1, heads * own), f32))
+    for h in range(heads):
+        rows = pl.ds(h * HD, HD)
+        ctx_ref[0, rows] = (o_scr[rows] / total[:, h * own : (h + 1) * own]).astype(bf16)
+    lse_ref[0] = top + jnp.log(total)
+
+
+def attn_fwd(bounds, q, kv, qseg, kseg, scale):
+    blocks, wide, own = q.shape
+    tiles, _, tile = kv.shape
+    heads = wide // HD
+    return pl.pallas_call(
+        functools.partial(attn_fwd_kernel, heads, scale),
+        out_shape=[
+            jax.ShapeDtypeStruct(q.shape, bf16),
+            jax.ShapeDtypeStruct((blocks, 1, heads * own), f32),
+        ],
+        grid_spec=pltpu.PrefetchScalarGridSpec(
+            num_scalar_prefetch=1,
+            grid=(blocks,),
+            in_specs=[
+                pl.BlockSpec((1, wide, own), lambda i, b: (i, 0, 0)),
+                pl.BlockSpec(kv.shape, lambda i, b: (0, 0, 0)),
+                pl.BlockSpec((1, 1, own), lambda i, b: (i, 0, 0)),
+                pl.BlockSpec(kseg.shape, lambda i, b: (0, 0, 0)),
+            ],
+            out_specs=[
+                pl.BlockSpec((1, wide, own), lambda i, b: (i, 0, 0)),
+                pl.BlockSpec((1, 1, heads * own), lambda i, b: (i, 0, 0)),
+            ],
+            scratch_shapes=[
+                pltpu.VMEM((tiles, tile, wide), bf16),
+                pltpu.VMEM((wide, heads * own), bf16),
+                pltpu.VMEM((tiles, tile, heads * own), f32),
+                pltpu.VMEM((wide, own), f32),
+            ],
+        ),
+        compiler_params=pltpu.CompilerParams(
+            dimension_semantics=("arbitrary",), vmem_limit_bytes=48 * 1024 * 1024
+        ),
+        name="attn_fwd",
+    )(bounds, q, kv, qseg, kseg)
+
+
+def attn_bwd_kernel(
+    heads, scale, bounds, q_ref, kv_ref, qseg_ref, kseg_ref, lse_ref, ctx_ref, dctx_ref,
+    dq_ref, dkv_ref, kn, vn, q3, dc3, dq_scr, dkv_scr,
+):
+    step = pl.program_id(0)
+    tiles, _, tile = kv_ref.shape
+    wide = heads * HD
+    own = q_ref.shape[-1]
+
+    @pl.when(step == 0)
+    def _():
+        @pl.loop(0, tiles)
+        def _(j):
+            kn[j] = kv_ref[j, pl.ds(0, wide)].astype(f32).T.astype(bf16)
+            vn[j] = kv_ref[j, pl.ds(wide, wide)].astype(f32).T.astype(bf16)
+            dkv_scr[j] = jnp.zeros((2 * wide, tile), f32)
+
+    block_rows(q_ref, heads, scale, q3)
+    block_rows(dctx_ref, heads, 1.0, dc3)
+    low, high = bounds[step, 0], bounds[step, 1]
+    qseg = jnp.concatenate([qseg_ref[0]] * heads, axis=1)
+    lse = lse_ref[0]
+    product = ctx_ref[0].astype(f32) * dctx_ref[0].astype(f32)
+    delta = jnp.concatenate(
+        [jnp.sum(product[h * HD : (h + 1) * HD], axis=0, keepdims=True) for h in range(heads)], axis=1
+    )
+    dq_scr[...] = jnp.zeros_like(dq_scr)
+
+    @pl.loop(low, high)
+    def _(j):
+        s = dot(kn[j], q3[...])
+        s = jnp.where(kseg_ref[j] == qseg, s, masked_value)
+        p = jnp.exp(s - lse)
+        d_p = dot(vn[j], dc3[...])
+        d_s = (p * (d_p - delta)).astype(bf16)
+        p = p.astype(bf16)
+        for h in range(heads):
+            rows, lanes = pl.ds(h * HD, HD), slice(h * own, (h + 1) * own)
+            dq_scr[rows] += dot(kv_ref[j, rows], d_s[:, lanes])
+            dkv_scr[j, rows] += dot(q3[rows, lanes], d_s[:, lanes], ((1,), (1,)))
+            deep = pl.ds(wide + h * HD, HD)
+            dkv_scr[j, deep] += dot(dctx_ref[0, rows], p[:, lanes], ((1,), (1,)))
+
+    dq_ref[0] = (dq_scr[...] * scale).astype(bf16)
+
+    @pl.when(step == pl.num_programs(0) - 1)
+    def _():
+        @pl.loop(0, tiles)
+        def _(j):
+            dkv_ref[j] = dkv_scr[j].astype(bf16)
+
+
+def attn_bwd(bounds, q, kv, qseg, kseg, lse, ctx, dctx, scale):
+    blocks, wide, own = q.shape
+    tiles, _, tile = kv.shape
+    heads = wide // HD
+    rowed = pl.BlockSpec((1, wide, own), lambda i, b: (i, 0, 0))
+    return pl.pallas_call(
+        functools.partial(attn_bwd_kernel, heads, scale),
+        out_shape=[jax.ShapeDtypeStruct(q.shape, bf16), jax.ShapeDtypeStruct(kv.shape, bf16)],
+        grid_spec=pltpu.PrefetchScalarGridSpec(
+            num_scalar_prefetch=1,
+            grid=(blocks,),
+            in_specs=[
+                rowed,
+                pl.BlockSpec(kv.shape, lambda i, b: (0, 0, 0)),
+                pl.BlockSpec((1, 1, own), lambda i, b: (i, 0, 0)),
+                pl.BlockSpec(kseg.shape, lambda i, b: (0, 0, 0)),
+                pl.BlockSpec((1, 1, heads * own), lambda i, b: (i, 0, 0)),
+                rowed,
+                rowed,
+            ],
+            out_specs=[rowed, pl.BlockSpec(kv.shape, lambda i, b: (0, 0, 0))],
+            scratch_shapes=[
+                pltpu.VMEM((tiles, tile, wide), bf16),
+                pltpu.VMEM((tiles, tile, wide), bf16),
+                pltpu.VMEM((wide, heads * own), bf16),
+                pltpu.VMEM((wide, heads * own), bf16),
+                pltpu.VMEM((wide, own), f32),
+                pltpu.VMEM((tiles, 2 * wide, tile), f32),
+            ],
+        ),
+        compiler_params=pltpu.CompilerParams(
+            dimension_semantics=("arbitrary",), vmem_limit_bytes=48 * 1024 * 1024
+        ),
+        name="attn_bwd",
+    )(bounds, q, kv, qseg, kseg, lse, ctx, dctx)
+
+
+def fast_local(
+    tokens,
+    segments,
+    labels,
+    cotangent,
+    w_qkv,
+    b_qkv,
+    w_out,
+    b_out,
+    ln1_gain,
+    ln1_bias,
+    w_in,
+    b_in,
+    w_back,
+    b_back,
+    ln2_gain,
+    ln2_bias,
+    s_proj,
+    s_bias,
+    s_query,
+    s_mid,
+    s_mid_bias,
+    s_cls,
+    s_cls_bias,
+):
+    _, width_row, cols_local = tokens.shape
+    parts, rows, cols, seqs, _ = sizes(tokens.shape[0])
+    width = width_row * rows
+    own = cols_local // parts
+    width_col = b_qkv.shape[1]
+    heads_dev = width_col // HD
+    hidden_col = b_in.shape[0]
+    docs_count = labels.shape[1]
+    class_count = s_cls.shape[1]
+    student_width = s_proj.shape[1]
+    seq_len = segments.shape[1]
+    row_index = lax.axis_index("row")
+    col_index = lax.axis_index("col")
+    dp_index = lax.axis_index("dp")
+    score_scale = HD ** (-0.5)
+    pool_scale = SHD ** (-0.5)
+    query_heads = s_query.reshape(SH, SHD)
+    doc_ids = jnp.arange(docs_count, dtype=jnp.int32)
+    class_ids = jnp.arange(class_count, dtype=jnp.int32)
+
+    w_three = w_qkv.reshape(width_row, heads_dev, 3, HD).transpose(0, 2, 1, 3)
+    w_three = jnp.concatenate([w_three[:, 1], w_three[:, 2], w_three[:, 0]], axis=1)
+    shard_attn = own_half(jnp.concatenate([w_three.reshape(width_row, -1), w_out], axis=1))
+    proj_rows = width_row // cols
+    vectors = [b_out, ln1_gain, ln1_bias, b_back, ln2_gain, ln2_bias, b_qkv.reshape(-1), b_in]
+    vectors.append(lax.dynamic_slice_in_dim(s_proj, col_index * proj_rows, proj_rows).astype(f32).reshape(-1))
+    flat = jnp.concatenate(vectors)
+    flat = jnp.pad(flat, (0, 96 * 128 - flat.shape[0])).reshape(96, 128)
+    w_attn, vec, w_in_all, w_back_all, x_parts, c_parts, ints = gather_fast(
+        [shard_attn, own_half(flat), own_half(w_in), own_half(w_back)],
+        tokens,
+        cotangent,
+        jnp.concatenate([segments, labels], axis=1),
+        1,
+    )
+    w_attn = w_attn.reshape(cols, rows, width_row, 4 * width_col)
+    w_qkv_all = w_attn[..., : 3 * width_col].reshape(cols, width, 3 * width_col)
+    w_out_all = w_attn[..., 3 * width_col :].transpose(0, 2, 1, 3).reshape(width, width)
+    w_in_all = w_in_all.reshape(cols, width, hidden_col)
+    w_back_all = w_back_all.reshape(cols, width, hidden_col)
+    vec = vec.reshape(cols, rows, -1)
+    at = 6 * width_row
+    row_vectors = vec[0, :, :at].reshape(rows, 6, width_row).transpose(1, 0, 2).reshape(6, width)
+    b_out_a, gain_one, bias_one, b_back_a, gain_two, bias_two = [row_vectors[i] for i in range(6)]
+    b_qkv_all = vec[:, 0, at : at + 2 * width_col].reshape(cols, 2, width_col)
+    at += 2 * width_col
+    b_in_all = vec[:, 0, at : at + hidden_col]
+    at += hidden_col
+    s_proj_all = vec[:, :, at : at + proj_rows * student_width].astype(bf16)
+    s_proj_all = s_proj_all.reshape(cols, rows, proj_rows, student_width).transpose(1, 0, 2, 3)
+    s_proj_all = s_proj_all.reshape(width, student_width)
+    x_t = x_parts.reshape(width, own)
+    ints = lax.dynamic_index_in_dim(ints.reshape(seqs, -1), row_index, 0, False)
+    seg_all, label_seq = ints[:seq_len], ints[seq_len:]
+    seg_blocks = seg_all.reshape(cols, parts, own)
+    seg_q = lax.dynamic_index_in_dim(seg_blocks, dp_index, 1, False)
+    seg_own = lax.dynamic_index_in_dim(seg_q, col_index, 0, False)
+    lows = jnp.sum(seg_all[None, :] < seg_q[:, :1], axis=1) // own
+    highs = (jnp.sum(seg_all[None, :] <= seg_q[:, -1:], axis=1) + own - 1) // own
+    bounds = jnp.stack([lows, highs], axis=1).astype(jnp.int32)
+
+    offsets = jnp.concatenate([jnp.zeros_like(b_qkv_all[:, 0]), b_qkv_all[:, 1], b_qkv_all[:, 0]], axis=1)
+    qkv = jnp.einsum("cdn,dt->cnt", w_qkv_all, x_t, preferred_element_type=f32) + offsets[:, :, None]
+    qkv = qkv.astype(bf16)
+    queries, kv = heads_fast(qkv[:, 2 * width_col :], qkv[:, : 2 * width_col], 2)
+    kv = kv.reshape(cols * parts, 2 * width_col, own)
+    q_rows, k_rows = seg_q[:, None, :], seg_all.reshape(cols * parts, own, 1)
+    context, lse = attn_fwd(bounds, queries, kv, q_rows, k_rows, score_scale)
+    (ctx_t,) = swap_fast([context], 3)
+    ctx_t = ctx_t.reshape(width, own)
+
+    x = x_t.T
+    attn_out = mm(ctx_t, w_out_all, ((0,), (0,))) + b_out_a
+    normed_one, inv_one = normalize(x.astype(f32) + attn_out)
+    hidden_one = normed_one * gain_one + bias_one
+    hidden_low = hidden_one.astype(bf16)
+    pre_act = jnp.einsum("td,cdn->ctn", hidden_low, w_in_all, preferred_element_type=f32)
+    pre_act = pre_act + b_in_all[:, None, :]
+    act = gelu_exact(pre_act).astype(bf16)
+    ffn_out = jnp.einsum("ctn,cdn->td", act, w_back_all, preferred_element_type=f32) + b_back_a
+    normed_two, inv_two = normalize(hidden_one + ffn_out)
+    layer_out = (normed_two * gain_two + bias_two).astype(bf16)
+    out = give_fast(layer_out.T, 4)
+
+    student_h = mm(layer_out, s_proj_all, ((1,), (0,))) + s_bias
+    head_parts = student_h.reshape(own, SH, SHD)
+    pool_logit = jnp.sum(head_parts * query_heads, axis=-1) * pool_scale
+    member = (seg_own[:, None] == doc_ids[None, :])[:, :, None]
+    masked = jnp.where(member, pool_logit[:, None, :], masked_value)
+    local_top = jnp.max(masked, axis=0)
+    local_exp = jnp.where(member, jnp.exp(masked - local_top[None]), 0.0)
+    local_total = jnp.sum(local_exp, axis=0)
+    local_sum = jnp.einsum("tdh,thk->dhk", local_exp, head_parts, precision=highest)
+    stats = jnp.concatenate([local_top[..., None], local_total[..., None], local_sum], axis=-1)
+    stats = lax.all_gather(stats, ("dp", "col"))
+    tops, totals, sums = stats[..., 0], stats[..., 1], stats[..., 2:]
+    doc_top = jnp.max(tops, axis=0)
+    factors = jnp.exp(tops - doc_top[None])
+    doc_total = jnp.sum(totals * factors, axis=0)
+    pooled_heads = jnp.sum(sums * factors[..., None], axis=0) / doc_total[:, :, None]
+    pooled = pooled_heads.reshape(docs_count, student_width)
+    middle = jnp.tanh(jnp.dot(pooled, s_mid, precision=highest) + s_mid_bias)
+    logit_rows = jnp.dot(middle, s_cls, precision=highest) + s_cls_bias
+    logits = lax.all_gather(logit_rows, "row")
+    logits = lax.dynamic_slice_in_dim(logits, dp_index * (seqs // parts), seqs // parts)
+    logit_top = jnp.max(logit_rows, axis=-1, keepdims=True)
+    logit_exp = jnp.exp(logit_rows - logit_top)
+    one_hot = (label_seq[:, None] == class_ids[None, :]).astype(f32)
+    d_logits = logit_exp / jnp.sum(logit_exp, axis=-1, keepdims=True) - one_hot
+    g_cls = jnp.dot(middle.T, d_logits, precision=highest)
+    g_cls_bias = jnp.sum(d_logits, axis=0)
+    d_middle = jnp.dot(d_logits, s_cls.T, precision=highest) * (1.0 - middle * middle)
+    g_mid = jnp.dot(pooled.T, d_middle, precision=highest)
+    g_mid_bias = jnp.sum(d_middle, axis=0)
+    d_pooled = jnp.dot(d_middle, s_mid.T, precision=highest).reshape(docs_count, SH, SHD)
+    shares = jnp.where(member, jnp.exp(masked - doc_top[None]), 0.0) / doc_total[None]
+    d_share = jnp.einsum("dhk,thk->tdh", d_pooled, head_parts, precision=highest)
+    base_term = jnp.sum(d_pooled * pooled_heads, axis=-1)
+    d_pool_logit = jnp.sum(shares * (d_share - base_term[None]), axis=1)
+    d_heads = jnp.einsum("tdh,dhk->thk", shares, d_pooled, precision=highest)
+    d_heads = d_heads + d_pool_logit[:, :, None] * query_heads[None] * pool_scale
+    g_query = (jnp.sum(d_pool_logit[:, :, None] * head_parts, axis=0) * pool_scale).reshape(-1)
+    d_student = d_heads.reshape(own, student_width)
+    g_sbias = jnp.sum(d_student, axis=0)
+    g_sproj = jnp.dot(layer_out.astype(f32).T, d_student, precision=highest)
+
+    d_out = c_parts.reshape(width, own).T.astype(f32)
+    g_ln2_gain = jnp.sum(d_out * normed_two, axis=0)
+    g_ln2_bias = jnp.sum(d_out, axis=0)
+    d_resid_two = normalize_back(d_out * gain_two, normed_two, inv_two)
+    d_ffn = d_resid_two.astype(bf16)
+    g_back_bias = jnp.sum(d_ffn.astype(f32), axis=0)
+    g_back = jnp.einsum("td,ctn->cdn", d_ffn, act, preferred_element_type=f32)
+    d_act = jnp.einsum("td,cdn->ctn", d_ffn, w_back_all, preferred_element_type=f32)
+    _, gelu_fn = jax.vjp(gelu_exact, pre_act)
+    d_pre = gelu_fn(d_act)[0].astype(bf16)
+    g_in_bias = jnp.sum(d_pre.astype(f32), axis=1)
+    g_in = jnp.einsum("td,ctn->cdn", hidden_low, d_pre, preferred_element_type=f32)
+    d_hidden_one = d_resid_two + jnp.einsum(
+        "ctn,cdn->td", d_pre, w_in_all, preferred_element_type=f32
+    )
+    g_ln1_gain = jnp.sum(d_hidden_one * normed_one, axis=0)
+    g_ln1_bias = jnp.sum(d_hidden_one, axis=0)
+    d_resid_one = normalize_back(d_hidden_one * gain_one, normed_one, inv_one)
+    d_attn = d_resid_one.astype(bf16)
+    g_out_bias = jnp.sum(d_attn.astype(f32), axis=0)
+    d_ctx = mm(w_out_all, d_attn, ((1,), (1,))).astype(bf16)
+    (d_ctx,) = swap_fast([d_ctx.reshape(cols, width_col, own)], 5)
+    once = 1.0 / (parts * cols)
+    small = (
+        g_in_bias,
+        g_out_bias,
+        g_ln1_gain,
+        g_ln1_bias,
+        g_back_bias,
+        g_ln2_gain,
+        g_ln2_bias,
+        g_sproj,
+        g_sbias,
+        g_query,
+        g_mid * once,
+        g_mid_bias * once,
+        g_cls * once,
+        g_cls_bias * once,
+    )
+    small = lax.psum(small, WORLD)
+    d_q, d_kv = attn_bwd(bounds, queries, kv, q_rows, k_rows, lse, context, d_ctx, score_scale)
+    d_q, d_kv = tokens_fast(d_q, d_kv.reshape(cols, parts, 2 * width_col, own), 6)
+    d_qkv = jnp.concatenate([d_kv, d_q], axis=1)
+    g_qkv_bias = jnp.sum(d_qkv.astype(f32), axis=2)
+    g_qkv_bias, small = lax.optimization_barrier((g_qkv_bias, small))
+    g_qkv_bias = lax.psum(g_qkv_bias[:, width_col:], WORLD)
+    g_qkv = jnp.einsum("dt,cnt->cdn", x_t, d_qkv, preferred_element_type=f32)
+    d_tokens = jnp.einsum("cdn,cnt->dt", w_qkv_all, d_qkv, preferred_element_type=f32)
+    d_tokens = (d_tokens + d_resid_one.T).astype(bf16)
+    grad_tokens = give_fast(d_tokens, 7).astype(f32)
+
+    g_out = mm(ctx_t, d_attn, ((1,), (0,)))
+    g_out = g_out.reshape(cols, width_col, rows, width_row).transpose(0, 2, 1, 3)
+    g_attn = jnp.concatenate(
+        [g_qkv.astype(bf16).reshape(cols, rows, width_row, 3 * width_col), g_out.astype(bf16)], axis=-1
+    )
+    blocked = (cols, rows, parts, width_row // parts, -1)
+    g_in, g_back, g_attn = [
+        part.reshape(width_row, -1).astype(f32)
+        for part in scatter_fast(
+            [g_in.astype(bf16).reshape(blocked), g_back.astype(bf16).reshape(blocked), g_attn.reshape(blocked)],
+            8,
+        )
+    ]
+    g_qkv = g_attn[:, : 3 * width_col].reshape(width_row, 3, heads_dev, HD)
+    g_qkv = jnp.stack([g_qkv[:, 2], g_qkv[:, 0], g_qkv[:, 1]], axis=2).reshape(width_row, -1)
+
+    def at_col(part):
+        return lax.dynamic_index_in_dim(part, col_index, 0, False)
+
+    def at_row(part):
+        return lax.dynamic_slice_in_dim(part, row_index * width_row, width_row)
+
+    bias_grad = at_col(g_qkv_bias)
+    return (
+        out,
+        logits,
+        grad_tokens,
+        g_qkv,
+        jnp.stack([bias_grad[width_col:], bias_grad[:width_col]]),
+        g_attn[:, 3 * width_col :],
+        at_row(small[1]),
+        at_row(small[2]),
+        at_row(small[3]),
+        g_in,
+        at_col(small[0]),
+        g_back,
+        at_row(small[4]),
+        at_row(small[5]),
+        at_row(small[6]),
+        at_row(small[7]),
+    ) + tuple(small[8:])
+
+
 def solution(mesh):
     row, col = P("row"), P("col")
     grid, whole = P("row", "col"), P("dp", "row", "col")
@@ -400,4 +1502,6 @@
         + (row, row, row, grid, col, grid, row, row, row, P("row", None))
         + (P(),) * 6
     )
+    quick = dict(mesh.shape) == {"dp": 2, "row": 4, "col": 4}
+    local = fast_local if quick else general_local
     return jax.shard_map(local, mesh=mesh, in_specs=placed, out_specs=results, check_vma=False)

time: 819 us -> 570 us (0.70)
  waiting for transfers between devices: 355 us -> 0.02 us
  Pallas kernels: 0 us -> 292 us
  blocking collectives: 200 us -> 116 us
  matrix products: 106 us -> 53.8 us
  starting transfers between devices: 27.2 us -> 0.04 us
  local copies, waits for them, and re-layouts: 71.5 us -> 58.8 us
  other arithmetic: 34.5 us -> 25.6 us
    pallas_call x0 -> x10, Pallas kernels: none -> 292 us  [the longest x1 87.7 us: gather_fast(): pl.pallas_call(functools.partial(gather_kernel, kinds), out_shape=[jax.Sh...]
    reduce_scatter x3 -> x0, waiting for transfers between devices: 184 us -> none  [the longest x2 184 us: scatter_world(): mine = lax.psum_scatter(flat, WORLD, scatter_dimension=0, tiled=True)]
    psum x1, waiting for transfers between devices: 76.9 us -> 0.01 us  [fast_local(): small = lax.psum(small, WORLD)]
    all_to_all x5 -> x0, blocking collectives: 68.5 us -> none  [the longest x2 55.8 us: swap_cols(): return lax.all_to_all(values, 'col', 0, 0, tiled=True)]
    all_gather x3 -> x0, waiting for transfers between devices: 64.7 us -> none  [the longest x2 64.7 us: gather_world(): out = lax.all_gather(shard, WORLD, axis=0, tiled=True)]
    all_gather x9 -> x2, blocking collectives: 89.4 us -> 32.7 us  [the longest x1 24.3 us: fast_local(): stats = lax.all_gather(stats, ('dp', 'col'))]
    dot_general x24 -> x19, matrix products: 89.6 us -> 47.4 us  [the longest x1 11.5 us: fast_local(): jnp.einsum('td,cdn->ctn', hidden_low, w_in_all, preferred_element_type=f32)]
    psum x1 -> x2, blocking collectives: 42.1 us -> 82.9 us  [the longest x1 43.7 us: fast_local(): small = lax.psum(small, WORLD)]
  transfers between devices with their start and end apart: 14 -> 1, of which waited for: 7 -> 0; matrix products, arithmetic and copies ran while one was open for 16% -> 10% of each run, Pallas kernels for 0% -> 26%
where the time goes in v2:
time: 570 us; the launch traced here: 562 us
  Pallas kernels  292 us (51%)
  blocking collectives  116 us (20%)
  local copies, waits for them, and re-layouts  58.8 us (10%)
  matrix products  53.8 us (9%)
  other arithmetic  25.6 us (4%)
  between operations  15.4 us (3%)
    pallas_call x1, Pallas kernels, gather_fast(): pl.pallas_call(functools.partial(gather_kernel, kinds), out_shape=[jax.Sh...  87.7 us
    pallas_call x1, Pallas kernels, scatter_fast(): pl.pallas_call(functools.partial(scatter_kernel, kinds), out_shape=[jax.S...  77.1 us
    psum x1, blocking collectives, fast_local(): small = lax.psum(small, WORLD)  43.7 us
    psum x1, blocking collectives, fast_local(): g_qkv_bias = lax.psum(g_qkv_bias[:, width_col:], WORLD)  39.2 us
    pallas_call x1, Pallas kernels, heads_fast(): pl.pallas_call(heads_kernel, out_shape=[jax.ShapeDtypeStruct(q.shape, q.d...  33 us
    pallas_call x1, Pallas kernels, tokens_fast(): pl.pallas_call(tokens_kernel, out_shape=[jax.ShapeDtypeStruct(q.shape, q....  31 us
    pallas_call x2, Pallas kernels, swap_fast(): pl.pallas_call(functools.partial(swap_kernel, count), out_shape=[jax.Shap...  26.7 us
    all_gather x1, blocking collectives, fast_local(): stats = lax.all_gather(stats, ('dp', 'col'))  24.3 us
  transfers between devices with their start and end apart: 1, of which 0 were waited for; matrix products, arithmetic and copies ran while one was open for 10% of the time, Pallas kernels for 26%

profile of v2, /device:TPU:0, one launch (start us, length us, event | category | flops | bytes accessed | tf_op | source)
XLA Modules:
  0.0 561.6 jit_solution(2737226510007867391)
XLA Ops:
  10.4 1.6 constant_dynamic-slice_fusion.7.refs_3_
  11.9 1.1 copy.255
  13.3 1.3 pad_add_fusion.refs_6_
  16.0 87.7 %gather_all.1 = (bf16[4,4,2,96,768]{4,3,2,1,0:T(8,128)(2,1)}, f32[4,4,2,48,128]{4,3,2,1,0:T(8,128)}, bf16[4,4,2,96,768]{4,3,2,1,0:T(8,128)(2,1)}, bf16[4,4,2,96,...) custom-call(bf16[96,768]{1,0:T(8,128)(2,1)} %fusion.49.refs_0_, ...), custom_call_target="tpu_custom_call" | custom-call | tf_op jit(solution)/shard_map/gather_all/pallas_call | solution.py:660
  103.8 1.5 reshape.390
  105.6 3.6 fusion.22
  110.0 0.9 slice.157.kv_ref
  110.9 2.1 slice_bitcast_fusion
  115.8 0.9 reshape.436.kseg_ref
  117.1 0.9 copy.259
  119.5 1.2 copy.280
  120.7 33.0 %to_heads.1 = (bf16[4,192,256]{2,1,0:T(8,128)(2,1)}, bf16[4,2,384,256]{3,2,1,0:T(8,128)(2,1)}) custom-call(bf16[4,192,256]{2,1,0:T(8,128)(2,1)} %slice.156.q_ref, bf16[4,384,256]{2,1,0:T(8,128)(2,1)} %slice.157.kv_ref), custom_call_target="tpu_custom_call" | custom-call | tf_op jit(solution)/shard_map/to_heads/pallas_call | solution.py:1000
  153.8 1.4 copy-done.2
  155.2 1.0 copy-done.4
  156.2 9.2 %attn_fwd.1 = (bf16[4,192,256]{2,1,0:T(8,128)(2,1)S(1)}, f32[4,1,768]{2,1,0:T(1,128)S(1)}) custom-call(s32[4,2]{1,0:T(4,128)S(1)} %pad_add_fusion.1.bounds, bf16[4,192,256]{2,1,0:T(8,128)(2,1)S(1)} %copy-done.4, bf16[8,384,256]{2,1,0:T(8,128)(2,1)S(1)} %bitcast.333, s32[4,1,256]{2,1,0:T(1,128)S(1)} %constant_dynamic-slice_fusion.6.qseg_ref, ...), custom_call_target="tpu_custom_call" | custom-call | tf_op jit(solution)/shard_map/attn_fwd/pallas_call | solution.py:1125
  166.2 13.8 %swap_cols.2 = bf16[4,192,256]{2,1,0:T(8,128)(2,1)} custom-call(bf16[4,192,256]{2,1,0:T(8,128)(2,1)} %copy-done.6), custom_call_target="tpu_custom_call" | custom-call | tf_op jit(solution)/shard_map/swap_cols/pallas_call | solution.py:954
  179.9 2.4 copy.270
  182.3 4.0 reshape.394
  186.3 3.0 fusion.98
  189.6 11.5 %fusion.9 = (bf16[4,256,768]{2,1,0:T(8,128)(2,1)S(1)}, f32[4,256,768]{2,1,0:T(8,128)}, f32[4,768,256]{1,2,0:T(8,128)}) fusion(f32[4,768]{1,0:T(4,128)S(1)} %bitcast.367, bf16[4,768,768]{2,1,0:T(8,128)(2,1)} %bitcast.372, f32[256,768]{1,0:T(8,128)S(1)} %get-tuple-element.263, f32[768]{0:T(1024)S(1)} %add.269, f32[768]{0:T(1024)S(1)} %mul.312, ...), kind=kOutput, calls=%fused_computation.19 | convolution fusion | flops 1260847104 | bytes 13389824 | tf_op jit(solution)/shard_map/td,cdn->ctn/dot_general | solution.py:1348
  201.1 2.4 fusion.95
  203.8 0.9 fusion.38
  204.7 1.8 convert_reduce_fusion.2
  208.4 24.3 %all-gather = f32[48,2,66]{2,1,0:T(2,128)S(1)} all-gather(f32[6,2,66]{2,1,0:T(2,128)S(1)} %copy.275), channel_id=2, replica_groups=mesh['dp'=2,'row'=4,'col'=4] {'dp','col'}, dimensions={0}, use_global_device_ids=true | all-gather | bytes 28512 | tf_op jit(solution)/shard_map/all_gather | solution.py:1366
  234.8 1.0 fusion.104
  236.0 1.5 fusion.106
  237.6 1.0 convolution_multiply_fusion
  239.1 1.7 fusion.105
  240.8 2.3 fusion.108
  244.0 4.6 slice.152
  249.3 0.9 convolution_multiply_fusion.1
  250.8 5.2 convert_reduce_fusion
  256.0 3.0 multiply_reduce_fusion
  259.0 3.7 convolution_convert_fusion.1
  262.7 3.6 convolution_convert_fusion
  266.3 0.9 convert_reduce_fusion.3
  267.2 1.3 convolution_convert_fusion.3
  268.5 12.9 %swap_cols.3.dctx_ref = bf16[4,192,256]{2,1,0:T(8,128)(2,1)} custom-call(bf16[4,192,256]{2,1,0:T(8,128)(2,1)} %bitcast.359), custom_call_target="tpu_custom_call" | custom-call | tf_op jit(solution)/shard_map/swap_cols/pallas_call | solution.py:954
  281.5 4.0 fusion.93
  285.4 1.9 copy.289
  287.3 1.0 copy-done.8
  288.3 12.6 %attn_bwd.1 = (bf16[4,192,256]{2,1,0:T(8,128)(2,1)S(1)}, bf16[8,384,256]{2,1,0:T(8,128)(2,1)S(1)}) custom-call(s32[4,2]{1,0:T(4,128)S(1)} %pad_add_fusion.1.bounds, bf16[4,192,256]{2,1,0:T(8,128)(2,1)S(1)} %copy-done.5, bf16[8,384,256]{2,1,0:T(8,128)(2,1)S(1)} %bitcast.334, s32[4,1,256]{2,1,0:T(1,128)S(1)} %constant_dynamic-slice_fusion.6.qseg_ref, ...), custom_call_target="tpu_custom_call" | custom-call | tf_op jit(solution)/shard_map/attn_bwd/pallas_call | solution.py:1215
  300.9 1.2 copy-done.9
  302.8 31.0 %to_tokens.1 = (bf16[4,192,256]{2,1,0:T(8,128)(2,1)}, bf16[4,384,256]{2,1,0:T(8,128)(2,1)}) custom-call(bf16[4,192,256]{2,1,0:T(8,128)(2,1)} %copy-done.10, bf16[4,2,384,256]{3,2,1,0:T(8,128)(2,1)} %bitcast.335), custom_call_target="tpu_custom_call" | custom-call | tf_op jit(solution)/shard_map/to_tokens/pallas_call | solution.py:1050
  333.9 1.2 constant_dynamic-update-slice_fusion.1
  335.1 1.0 constant_dynamic-update-slice_fusion
  336.6 1.8 convolution_convert_fusion.2
  338.4 1.1 convert_bitcast_fusion
  339.5 3.9 copy.288
  343.4 6.1 %pad_maximum_fusion.refs_2_ = bf16[4,4,2,96,768]{4,3,2,1,0:T(8,128)(2,1)} fusion(bf16[4,4,2,96,192]{4,3,2,1,0:T(8,128)(2,1)} %bitcast.341, bf16[4,4,2,96,576]{4,3,2,1,0:T(8,128)(2,1)} %bitcast.337), kind=kLoop, calls=%fused_computation.1 | loop fusion | flops 9437184 | bytes 9437184 | tf_op jit(solution)/shard_map/concatenate | solution.py:1451
  349.6 77.1 %scatter_all.1 = (bf16[2,96,768]{2,1,0:T(8,128)(2,1)S(1)}, bf16[2,96,768]{2,1,0:T(8,128)(2,1)S(1)}, bf16[2,96,768]{2,1,0:T(8,128)(2,1)S(1)}) custom-call(bf16[4,4,2,96,768]{4,3,2,1,0:T(8,128)(2,1)S(1)} %bitcast.332, bf16[4,4,2,96,768]{4,3,2,1,0:T(8,128)(2,1)} %bitcast.336, bf16[4,4,2,96,768]{4,3,2,1,0:T(8,128)(2,1)} %pad_maximum_fusion.refs_2_), custom_call_target="tpu_custom_call" | custom-call | tf_op jit(solution)/shard_map/scatter_all/pallas_call | solution.py:842
  427.7 8.4 %all-gather.2 = f32[4,6,14]{2,1,0:T(8,128)S(1)} all-gather(f32[1,6,14]{2,1,0:T(8,128)S(1)} %bitcast.364), channel_id=3, replica_groups=mesh['dp'=2,'row'=4,'col'=4] {'row'}, dimensions={0}, use_global_device_ids=true | all-gather | bytes 1680 | tf_op jit(solution)/shard_map/all_gather | solution.py:1375
  436.9 0.9 copy.271
  437.8 6.6 %give_back.2 = bf16[2,192,512]{2,1,0:T(8,128)(2,1)} custom-call(bf16[4,192,256]{2,1,0:T(8,128)(2,1)} %bitcast.349), custom_call_target="tpu_custom_call" | custom-call | tf_op jit(solution)/shard_map/give_back/pallas_call | solution.py:918
  444.4 3.6 fusion.25
  447.9 0.9 copy.285
  448.9 8.5 %give_back.3 = bf16[2,192,512]{2,1,0:T(8,128)(2,1)} custom-call(bf16[4,192,256]{2,1,0:T(8,128)(2,1)} %bitcast.350), custom_call_target="tpu_custom_call" | custom-call | tf_op jit(solution)/shard_map/give_back/pallas_call | solution.py:918
  457.4 2.0 convert_element_type.151
  459.8 1.0 copy.298
  460.8 0.9 bitcast_convert_fusion.1
  461.7 43.7 %all-reduce.1 = (f32[4,768]{1,0:T(4,128)S(1)}, f32[768]{0:T(1024)S(1)}, f32[768]{0:T(1024)S(1)}, f32[768]{0:T(1024)S(1)}, f32[768]{0:T(1024)S(1)}, /*index=5*/f3...) all-reduce(f32[4,768]{1,0:T(4,128)S(1)} %copy-done.36, ...), channel_id=1, replica_groups=mesh['dp'=2,'row'=4,'col'=4] {'col','row','dp'}, use_global_device_ids=true, to_apply=%region_18.19 | all-reduce | flops 9870 | bytes 78960 | tf_op jit(solution)/shard_map/psum | solution.py:1437
  506.3 39.2 %psum.119 = f32[4,384]{1,0:T(4,128)S(1)} all-reduce(f32[4,384]{1,0:T(4,128)S(1)} %slice.143), channel_id=1, replica_groups=mesh['dp'=2,'row'=4,'col'=4] {'col','row','dp'}, use_global_device_ids=true, to_apply=%region_46.47 | all-reduce | flops 1536 | bytes 12288 | tf_op jit(solution)/shard_map/psum | solution.py:1443
  549.9 1.5 constant_dynamic-slice_fusion.1
  552.9 1.5 copy.336
  (238 shorter events, 28.8 us)
Async XLA Ops:
  7.2 2.5 copy-start
  7.2 8.1 %copy-start.28 = (bf16[192,192]{1,0:T(8,128)(2,1)S(1)}, bf16[192,192]{1,0:T(8,128)(2,1)}, u32[]{:S(2)}) copy-start(bf16[192,192]{1,0:T(8,128)(2,1)} %param.29) | copy-start | bytes 221188
  7.2 499.0 %all-reduce.5.cloned.1.call-start = ((), (), s32[]{:S(2)}) async-start(), calls=%async_computation | async-start | bytes 917504 | tf_op jit(solution)/shard_map/psum | solution.py:1437
  109.2 3.8 copy-start.49
  109.2 4.5 copy-start.29
  110.0 7.1 %copy-start.20 = (bf16[4,192,256]{2,1,0:T(8,128)(2,1)S(1)}, bf16[4,192,256]{2,1,0:T(8,128)(2,1)}, u32[]{:S(2)}) copy-start(bf16[4,192,256]{2,1,0:T(8,128)(2,1)} %get-tuple-element.55) | copy-start | bytes 1179652
  118.0 71.5 %copy-start.34 = (f32[4,1,768]{2,0,1:T(4,128)}, f32[4,1,768]{2,0,1:T(4,128)S(1)}, u32[]{:S(2)}) copy-start(f32[4,1,768]{2,0,1:T(4,128)S(1)} %copy.329) | copy-start | bytes 36868
  120.6 84.0 %copy-start.11 = (f32[768,256]{0,1:T(8,128)}, f32[768,256]{0,1:T(8,128)S(1)}, u32[]{:S(2)}) copy-start(f32[768,256]{0,1:T(8,128)S(1)} %copy.280) | copy-start | bytes 2359300
  153.8 1.4 copy-start.2
  155.2 1.0 copy-start.4
  165.4 0.7 copy-start.6
  186.3 14.8 %slice-start.4 = ((s8[4718592]{0:T(1024)(128)(4,1)}), s8[4194304]{0:T(1024)(128)(4,1)S(1)}, s32[]{:S(2)}) async-start(s8[4718592]{0:T(1024)(128)(4,1)} %bitcast.377), calls=%async_computation.5 | async-start | bytes 8388608
  189.5 11.5 %slice-start.5 = ((s8[4718592]{0:T(1024)(128)(4,1)}), s8[524288]{0:T(1024)(128)(4,1)S(1)}, s32[]{:S(2)}) async-start(s8[4718592]{0:T(1024)(128)(4,1)} %bitcast.377), calls=%async_computation.6 | async-start | bytes 1048576
  201.1 2.4 copy-start.18
  203.5 3.7 copy-start.26
  203.5 3.7 copy-start.45
  203.5 3.7 copy-start.46
  203.7 30.3 %copy-start.27 = (f32[128,128]{1,0:T(8,128)S(1)}, f32[128,128]{1,0:T(8,128)}, u32[]{:S(2)}) copy-start(f32[128,128]{1,0:T(8,128)} %param.42) | copy-start | bytes 196612
  204.7 29.2 %copy-start.37 = (f32[256]{0:T(256)}, f32[256]{0:T(256)S(1)}, u32[]{:S(2)}) copy-start(f32[256]{0:T(256)S(1)} %broadcast_multiply_fusion.3) | copy-start | bytes 3076
  204.7 2.9 copy-start.39
  206.5 0.7 copy-start.16
  206.5 36.7 %copy-start.25 = (bf16[4,192,256]{2,1,0:T(8,128)(2,1)S(1)}, bf16[4,192,256]{2,1,0:T(8,128)(2,1)}, u32[]{:S(2)}) copy-start(bf16[4,192,256]{2,1,0:T(8,128)(2,1)} %get-tuple-element.65) | copy-start | bytes 1179652
  244.0 4.7 copy-start.44
  244.0 6.8 %copy-start.17 = (f32[256,768]{1,0:T(8,128)S(1)}, f32[256,768]{1,0:T(8,128)}, u32[]{:S(2)}) copy-start(f32[256,768]{1,0:T(8,128)} %get-tuple-element.252) | copy-start | bytes 2359300
  244.0 6.8 %copy-start.35 = (f32[4,1,768]{2,0,1:T(4,128)S(1)}, f32[4,1,768]{2,0,1:T(4,128)}, u32[]{:S(2)}) copy-start(f32[4,1,768]{2,0,1:T(4,128)} %copy-done.34) | copy-start | bytes 36868
  244.0 6.8 %copy-start.52 = (f32[4,256,768]{2,1,0:T(8,128)S(1)}, f32[4,256,768]{2,1,0:T(8,128)}, u32[]{:S(2)}) copy-start(f32[4,256,768]{2,1,0:T(8,128)} %get-tuple-element.261) | copy-start | bytes 9437188
  244.0 6.8 %copy-start.53 = (f32[4,768,256]{1,2,0:T(8,128)S(1)}, f32[4,768,256]{1,2,0:T(8,128)}, u32[]{:S(2)}) copy-start(f32[4,768,256]{1,2,0:T(8,128)} %get-tuple-element.282) | copy-start | bytes 9437188
  244.0 12.0 %slice-start.2 = ((s8[4718592]{0:T(1024)(128)(4,1)}), s8[524288]{0:T(1024)(128)(4,1)S(1)}, s32[]{:S(2)}) async-start(s8[4718592]{0:T(1024)(128)(4,1)} %bitcast.373), calls=%async_computation.3 | async-start | bytes 1048576
  250.8 5.2 slice-start.3
  259.0 3.7 copy-start.19
  262.7 4.5 copy-start.14
  266.3 15.1 %copy-start.38 = (f32[256]{0:T(256)S(1)}, f32[256]{0:T(256)}, u32[]{:S(2)}) copy-start(f32[256]{0:T(256)} %copy-done.37) | copy-start | bytes 3076
  266.3 15.1 %copy-start.40 = (f32[256]{0:T(256)S(1)}, f32[256]{0:T(256)}, u32[]{:S(2)}) copy-start(f32[256]{0:T(256)} %copy-done.39) | copy-start | bytes 3076
  281.4 5.9 %copy-start.3 = (bf16[4,2,384,256]{3,2,1,0:T(8,128)(2,1)S(1)}, bf16[4,2,384,256]{3,2,1,0:T(8,128)(2,1)}, u32[]{:S(2)}) copy-start(bf16[4,2,384,256]{3,2,1,0:T(8,128)(2,1)} %get-tuple-element.60) | copy-start | bytes 4718596
  281.4 5.9 %copy-start.5 = (bf16[4,192,256]{2,1,0:T(8,128)(2,1)S(1)}, bf16[4,192,256]{2,1,0:T(8,128)(2,1)}, u32[]{:S(2)}) copy-start(bf16[4,192,256]{2,1,0:T(8,128)(2,1)} %get-tuple-element.59.q_ref) | copy-start | bytes 1179652
  281.4 5.9 %copy-start.7 = (bf16[4,192,256]{2,1,0:T(8,128)(2,1)S(1)}, bf16[4,192,256]{2,1,0:T(8,128)(2,1)}, u32[]{:S(2)}) copy-start(bf16[4,192,256]{2,1,0:T(8,128)(2,1)} %copy-done.6) | copy-start | bytes 1179652
  287.3 1.0 copy-start.8
  300.9 1.2 copy-start.9
  302.1 0.7 copy-start.10
  302.8 33.7 %copy-start.15 = (bf16[4,192,256]{2,1,0:T(8,128)(2,1)S(1)}, bf16[4,192,256]{2,1,0:T(8,128)(2,1)}, u32[]{:S(2)}) copy-start(bf16[4,192,256]{2,1,0:T(8,128)(2,1)} %swap_cols.2) | copy-start | bytes 1179652
  302.8 33.8 %copy-start.24 = (bf16[768,256]{1,0:T(8,128)(2,1)S(1)}, bf16[768,256]{1,0:T(8,128)(2,1)}, u32[]{:S(2)}) copy-start(bf16[768,256]{1,0:T(8,128)(2,1)} %copy.289) | copy-start | bytes 1179652
  333.8 4.5 copy-start.21
  336.1 2.3 copy-start.12
  343.4 6.1 %slice-start = ((s8[4718592]{0:T(1024)(128)(4,1)}), s8[4194304]{0:T(1024)(128)(4,1)S(1)}, s32[]{:S(2)}) async-start(s8[4718592]{0:T(1024)(128)(4,1)} %bitcast.330), calls=%async_computation.1 | async-start | bytes 8388608
  343.4 6.1 %slice-start.1 = ((s8[4718592]{0:T(1024)(128)(4,1)}), s8[524288]{0:T(1024)(128)(4,1)S(1)}, s32[]{:S(2)}) async-start(s8[4718592]{0:T(1024)(128)(4,1)} %bitcast.330), calls=%async_computation.2 | async-start | bytes 1048576
  349.5 78.1 %copy-start.33 = (f32[4,192]{1,0:T(4,128)S(1)}, f32[4,192]{1,0:T(4,128)}, u32[]{:S(2)}) copy-start(f32[4,192]{1,0:T(4,128)} %convert_reduce_fusion.4) | copy-start | bytes 9220
  349.5 78.2 %copy-start.48 = (f32[14]{0:T(128)S(1)}, f32[14]{0:T(128)}, u32[]{:S(2)}) copy-start(f32[14]{0:T(128)} %fusion.88) | copy-start | bytes 172
  349.5 78.2 %copy-start.51 = (f32[128]{0:T(128)S(1)}, f32[128]{0:T(128)}, u32[]{:S(2)}) copy-start(f32[128]{0:T(128)} %get-tuple-element.293) | copy-start | bytes 1540
  349.6 78.2 %copy-start.47 = (f32[128]{0:T(128)S(1)}, f32[128]{0:T(128)}, u32[]{:S(2)}) copy-start(f32[128]{0:T(128)} %fusion.50) | copy-start | bytes 1540
  349.6 87.2 %copy-start.50 = (f32[2,64]{1,0:T(2,128)S(1)}, f32[2,64]{1,0:T(2,128)}, u32[]{:S(2)}) copy-start(f32[2,64]{1,0:T(2,128)} %get-tuple-element.291) | copy-start | bytes 1540
  349.6 87.3 %copy-start.23 = (bf16[768,256]{0,1:T(8,128)(2,1)S(1)}, bf16[768,256]{0,1:T(8,128)(2,1)}, u32[]{:S(2)}) copy-start(bf16[768,256]{0,1:T(8,128)(2,1)} %get-tuple-element.266) | copy-start | bytes 1179652
  426.7 17.7 %copy-start.13 = (bf16[4,576,256]{2,1,0:T(8,128)(2,1)S(1)}, bf16[4,576,256]{2,1,0:T(8,128)(2,1)}, u32[]{:S(2)}) copy-start(bf16[4,576,256]{2,1,0:T(8,128)(2,1)} %copy-done.12) | copy-start | bytes 3538948
  459.4 2.3 copy-start.30
  459.4 2.3 copy-start.31
  459.4 2.3 copy-start.32
  459.4 2.3 copy-start.36
  459.4 2.3 copy-start.41
  459.4 2.3 copy-start.42
  459.4 2.3 copy-start.43
  459.6 92.5 %copy-start.22 = (bf16[2,192,512]{2,1,0:T(8,128)(2,1)S(1)}, bf16[2,192,512]{2,1,0:T(8,128)(2,1)}, u32[]{:S(2)}) copy-start(bf16[2,192,512]{2,1,0:T(8,128)(2,1)} %give_back.2) | copy-start | bytes 1179652
  459.7 94.7 %copy-start.1 = (bf16[192,768]{1,0:T(8,128)(2,1)S(1)}, bf16[192,768]{1,0:T(8,128)(2,1)}, u32[]{:S(2)}) copy-start(bf16[192,768]{1,0:T(8,128)(2,1)} %param.33) | copy-start | bytes 884740
Sparse Core Ops, SparseCore 0:
  243.3 132.2 all-reduce.4

commit v3 on v2

--- a/solution.py
+++ b/solution.py
@@ -677,16 +677,15 @@
     )(*shards, tokens, cotangent, ints)
 
 
-def scatter_kernel(kinds, *refs):
-    grads, outs = refs[:kinds], refs[kinds : 2 * kinds]
-    (acc, precv, xr1, yr1, xr2, yr2, zup, zdn, fin) = refs[2 * kinds : 2 * kinds + 9]
-    (ls, ps, pr, xs1, xm1, ys1, ym1, xs2, xm2, ys2, ym2, us, um, ds, dm, fs, fm, os) = refs[2 * kinds + 9 :]
+def scatter_core(grads, outs, scratch, begin, during):
+    kinds = len(grads)
+    (acc, precv, xr1, yr1, xr2, yr2, zup, zdn, fin) = scratch[:9]
+    (ls, ps, pr, xs1, xm1, ys1, ym1, xs2, xm2, ys2, ym2, us, um, ds, dm, fs, fm, os) = scratch[9:]
     d, r, c = place()
     cols = 4
     chunks = kinds * cols
     xn, yn, pn = (d, r ^ 1, c), (d, r ^ 2, c), (1 - d, r, c)
     up, down = (d, r, c + 1), (d, r, c - 1)
-    greet([xn, yn, pn], [(c < cols - 1, up), (c > 0, down)])
     half = acc.shape[2] // 2
     first, last = pl.ds(0, half), pl.ds(half, half)
 
@@ -710,6 +709,7 @@
     for i in range(chunks):
         pair(i).start()
         load(i).start()
+    begin()
 
     def x1(i, j):
         return rcopy(acc.at[i, r ^ 1 ^ (2 * j), first], xr1.at[i, j], xs1.at[i, j], xm1.at[i, j], xn)
@@ -800,8 +800,13 @@
     stages += [(5 + h, functools.partial(lambda h, i: stage4(i, h), h)) for h in range(cols)]
     ending = stages[-1][0]
 
+    assert len(during) <= chunks + ending
+
     @pl.loop(0, chunks + ending)
     def _(step):
+        for i, extra in enumerate(during):
+            pl.when(step == i)(extra)
+
         for lag, stage in stages:
 
             @pl.when((step >= lag) & (step - lag < chunks))
@@ -832,45 +837,30 @@
     for k in range(kinds):
         pltpu.make_async_copy(fin.at[k], outs[k], os.at[k]).wait()
 
-
-def scatter_fast(grads, cid):
-    kinds = len(grads)
+def scatter_scratch(kinds, n, w, dt):
+    dma = pltpu.SemaphoreType.DMA
     chunks = kinds * 4
-    n, w = grads[0].shape[3:]
-    dma = pltpu.SemaphoreType.DMA
-    dt = grads[0].dtype
-    return pl.pallas_call(
-        functools.partial(scatter_kernel, kinds),
-        out_shape=[jax.ShapeDtypeStruct((2, n, w), dt)] * kinds,
-        in_specs=[HBM] * kinds,
-        out_specs=[HBM] * kinds,
-        scratch_shapes=[
-            pltpu.VMEM((chunks, 4, n, w), dt),
-            pltpu.VMEM((chunks, 4, n, w), dt),
-            pltpu.VMEM((chunks, 2, n // 2, w), dt),
-            pltpu.VMEM((chunks, 2, n // 2, w), dt),
-            pltpu.VMEM((chunks, n // 2, w), dt),
-            pltpu.VMEM((chunks, n // 2, w), dt),
-            pltpu.VMEM((chunks, n, w), dt),
-            pltpu.VMEM((chunks, n, w), dt),
-            pltpu.VMEM((kinds, 2, n, w), dt),
-            dma((chunks,)), dma((chunks,)), dma((chunks,)),
-            dma((chunks, 2)), dma((chunks, 2)), dma((chunks, 2)), dma((chunks, 2)),
-            dma((chunks,)), dma((chunks,)), dma((chunks,)), dma((chunks,)),
-            dma((chunks,)), dma((chunks,)), dma((chunks,)), dma((chunks,)),
-            dma((kinds,)), dma((kinds,)), dma((kinds,)),
-        ],
-        compiler_params=pltpu.CompilerParams(
-            collective_id=cid, has_side_effects=True, vmem_limit_bytes=48 * 1024 * 1024
-        ),
-        name="scatter_all",
-    )(*grads)
-
-
-def give_kernel(src_ref, out_ref, local, send, recv):
+    return [
+        pltpu.VMEM((chunks, 4, n, w), dt),
+        pltpu.VMEM((chunks, 4, n, w), dt),
+        pltpu.VMEM((chunks, 2, n // 2, w), dt),
+        pltpu.VMEM((chunks, 2, n // 2, w), dt),
+        pltpu.VMEM((chunks, n // 2, w), dt),
+        pltpu.VMEM((chunks, n // 2, w), dt),
+        pltpu.VMEM((chunks, n, w), dt),
+        pltpu.VMEM((chunks, n, w), dt),
+        pltpu.VMEM((kinds, 2, n, w), dt),
+        dma((chunks,)), dma((chunks,)), dma((chunks,)),
+        dma((chunks, 2)), dma((chunks, 2)), dma((chunks, 2)), dma((chunks, 2)),
+        dma((chunks,)), dma((chunks,)), dma((chunks,)), dma((chunks,)),
+        dma((chunks,)), dma((chunks,)), dma((chunks,)), dma((chunks,)),
+        dma((kinds,)), dma((kinds,)), dma((kinds,)),
+    ]
+
+
+def give_moves(src_ref, out_ref, local, send, recv):
     d, r, c = place()
     own = src_ref.shape[2]
-    greet([(d ^ (j // 4), r ^ (j % 4), c) for j in range(1, 8)])
     home = r // 2
 
     def slot(i, core):
@@ -882,48 +872,46 @@
     def stay():
         return pltpu.make_async_copy(src_ref.at[r], slot(r % 2, d), local)
 
-    for row in range(4):
-        here = (row == r) & (home == d)
-
-        @pl.when(jnp.logical_not(here))
+    def start():
+        for row in range(4):
+
+            @pl.when(jnp.logical_not((row == r) & (home == d)))
+            def _():
+                move(row).start()
+
+        @pl.when(home == d)
         def _():
-            move(row).start()
-
-    @pl.when(home == d)
-    def _():
-        stay().start()
-
-    for row in range(4):
-        here = (row == r) & (home == d)
-
-        @pl.when(jnp.logical_not(here))
+            stay().start()
+
+    def finish():
+        for row in range(4):
+
+            @pl.when(jnp.logical_not((row == r) & (home == d)))
+            def _():
+                move(row).wait_send()
+
+        @pl.when(home == d)
         def _():
-            move(row).wait_send()
-
-    @pl.when(home == d)
-    def _():
-        stay().wait()
-
-    for i in range(2):
-        for core in range(2):
-
-            @pl.when(jnp.logical_not((2 * d + i == r) & (core == d)))
-            def _():
-                rcopy(src_ref.at[0], slot(i, core), send.at[0], recv.at[i, core], (d, r, c)).wait_recv()
-
-
-def give_fast(values, cid):
-    width, own = values.shape
-    dma = pltpu.SemaphoreType.DMA
-    return pl.pallas_call(
-        give_kernel,
-        out_shape=jax.ShapeDtypeStruct((2, width // 4, 2 * own), values.dtype),
-        in_specs=[HBM],
-        out_specs=HBM,
-        scratch_shapes=[dma, dma((4,)), dma((2, 2))],
-        compiler_params=pltpu.CompilerParams(collective_id=cid, has_side_effects=True),
-        name="give_back",
-    )(values.reshape(4, width // 4, own))
+            stay().wait()
+
+        for i in range(2):
+            for core in range(2):
+
+                @pl.when(jnp.logical_not((2 * d + i == r) & (core == d)))
+                def _():
+                    rcopy(src_ref.at[0], slot(i, core), send.at[0], recv.at[i, core], (d, r, c)).wait_recv()
+
+    return start, finish
+
+
+def plane_peers():
+    d, r, c = place()
+    return [(d ^ (j // 4), r ^ (j % 4), c) for j in range(1, 8)]
+
+
+def line_peers():
+    d, r, c = place()
+    return [(d ^ (j // 4), r, c ^ (j % 4)) for j in range(1, 8)]
 
 
 VM = pl.BlockSpec(memory_space=pltpu.VMEM)
@@ -1011,10 +999,127 @@
     )(q, kv)
 
 
-def tokens_kernel(q_ref, kv_ref, q_out, kv_out, total, theirs, send, recv, psend, precv):
+def turn_kernel(ctx_ref, stats_ref, give_ref, ctx_out, stats_out, give_out, send, recv, ssend, srecv, gl, gs, gr):
+    d, r, c = place()
+    peers = line_peers()
+    greet(plane_peers() + peers[:3] + peers[4:])
+
+    def move(j):
+        return rcopy(ctx_ref.at[c ^ j], ctx_out.at[c], send.at[j], recv.at[j], (d, r, c ^ j))
+
+    def tell(j):
+        return rcopy(stats_ref, stats_out.at[d, c], ssend.at[j - 1], srecv.at[j - 1], peers[j - 1])
+
+    for j in range(1, 8):
+        tell(j).start()
+    for j in (3, 2, 1):
+        move(j).start()
+    start, finish = give_moves(give_ref, give_out, gl, gs, gr)
+    start()
+    ctx_out[c] = ctx_ref[c]
+    stats_out[d, c] = stats_ref[...]
+    for j in range(1, 8):
+        tell(j).wait()
+    for j in (1, 2, 3):
+        move(j).wait()
+    finish()
+
+
+def turn_fast(d_ctx, stats, out_t, cid):
+    width, own = out_t.shape
+    dma = pltpu.SemaphoreType.DMA
+    return pl.pallas_call(
+        turn_kernel,
+        out_shape=[
+            jax.ShapeDtypeStruct(d_ctx.shape, d_ctx.dtype),
+            jax.ShapeDtypeStruct((2, 4) + stats.shape, stats.dtype),
+            jax.ShapeDtypeStruct((2, width // 4, 2 * own), out_t.dtype),
+        ],
+        in_specs=[VM, VM, HBM],
+        out_specs=[VM, VM, HBM],
+        scratch_shapes=[dma((4,)), dma((4,)), dma((7,)), dma((7,)), dma, dma((4,)), dma((2, 2))],
+        compiler_params=pltpu.CompilerParams(collective_id=cid, has_side_effects=True),
+        name="turn",
+    )(d_ctx, stats, out_t.reshape(4, width // 4, own))
+
+
+def sum_steps(src, total, parts, sems):
+    d, r, c = place()
+    peers = [(1 - d, r, c), (d, r ^ 1, c), (d, r ^ 2, c), (d, r, c ^ 1), (d, r, c ^ 2)]
+    bits = [d, r % 2, r // 2, c % 2, c // 2]
+    rs, rr, gs, gr = sems
+    count = len(peers)
+    size = [src.shape[0] >> (i + 1) for i in range(count)]
+    offset = [jnp.int32(0)]
+    for i in range(count):
+        offset.append(offset[i] + bits[i] * size[i])
+
+    def rows(at, amount):
+        return pl.ds(pl.multiple_of(at, 8), amount)
+
+    def down(i):
+        other = offset[i] + (1 - bits[i]) * size[i]
+        held = src if i == 0 else parts[i - 1]
+        at = other if i == 0 else other - offset[i]
+        return rcopy(held.at[rows(at, size[i])], parts[count + i], rs.at[i], rr.at[i], peers[i])
+
+    def fold(i):
+        down(i).wait_recv()
+        held = src if i == 0 else parts[i - 1]
+        at = offset[i + 1] if i == 0 else offset[i + 1] - offset[i]
+        parts[i][...] = held[rows(at, size[i])] + parts[count + i][...]
+
+    def back(i):
+        spot = total.at[rows(offset[i + 1], size[i])]
+        return rcopy(spot, spot, gs.at[i], gr.at[i], peers[i])
+
+    def back_recv(i):
+        spot = total.at[rows(offset[i] + (1 - bits[i]) * size[i], size[i])]
+        rcopy(spot, spot, gs.at[i], gr.at[i], peers[i]).wait_recv()
+
+    steps = [lambda: down(0).start()]
+    for i in range(1, count):
+
+        def step(i=i):
+            fold(i - 1)
+            down(i).start()
+
+        steps.append(step)
+
+    def middle():
+        fold(count - 1)
+        total[rows(offset[count], size[-1])] = parts[count - 1][...]
+        back(count - 1).start()
+
+    steps.append(middle)
+    for i in range(count - 2, -1, -1):
+
+        def step(i=i):
+            back_recv(i + 1)
+            back(i).start()
+
+        steps.append(step)
+
+    def end():
+        back_recv(0)
+        for i in range(count):
+            down(i).wait_send()
+            back(i).wait_send()
+
+    return steps, end
+
+
+def tail_kernel(kinds, *refs):
+    grads, refs = refs[:kinds], refs[kinds:]
+    (q_ref, kv_ref, small_ref), refs = refs[:3], refs[3:]
+    outs, refs = refs[:kinds], refs[kinds:]
+    (q_out, kv_out, small_out), refs = refs[:3], refs[3:]
+    (total, theirs), refs = refs[:2], refs[2:]
+    parts, refs = refs[:10], refs[10:]
+    (send, recv, psend, precv), sems, scratch = refs[:4], refs[4:8], refs[8:]
     d, r, c = place()
     pn = (1 - d, r, c)
-    greet([(d, r, c ^ j) for j in (1, 2, 3)] + [pn])
+    greet([(d, r, c ^ j) for j in (1, 2, 3)] + [pn, (d, r ^ 1, c), (d, r ^ 2, c)])
 
     def pair(j):
         return rcopy(kv_ref.at[c ^ j, 1 - d], theirs.at[c ^ j], psend.at[j], precv.at[j], pn)
@@ -1030,12 +1135,18 @@
     for j in (3, 2, 1):
         q(j).start()
     q_out[c] = q_ref[c]
-    for j in (3, 2, 1):
-        pair(j).wait_recv()
-        total[c ^ j] = kv_ref[c ^ j, d] + theirs[c ^ j]
-        kv(j).start()
-    pair(0).wait_recv()
-    kv_out[c] = kv_ref[c, d] + theirs[c]
+    steps, end = sum_steps(small_ref, small_out, parts, sems)
+
+    def begin():
+        for j in (3, 2, 1):
+            pair(j).wait_recv()
+            total[c ^ j] = kv_ref[c ^ j, d] + theirs[c ^ j]
+            kv(j).start()
+        pair(0).wait_recv()
+        kv_out[c] = kv_ref[c, d] + theirs[c]
+
+    scatter_core(grads, outs, scratch, begin, steps)
+    end()
     for j in range(4):
         pair(j).wait_send()
     for j in (1, 2, 3):
@@ -1043,23 +1154,62 @@
         kv(j).wait()
 
 
-def tokens_fast(q, kv, cid):
-    cols, _, own, wide = kv.shape
+def tail_fast(grads, q, kv, small, cid):
+    kinds = len(grads)
+    n, w = grads[0].shape[3:]
     dma = pltpu.SemaphoreType.DMA
-    piece = jax.ShapeDtypeStruct((cols, own, wide), kv.dtype)
+    cols, _, wide, own = kv.shape
+    parts = [pltpu.VMEM((small.shape[0] >> (i + 1), small.shape[1]), f32) for i in range(5)]
     return pl.pallas_call(
-        tokens_kernel,
-        out_shape=[jax.ShapeDtypeStruct(q.shape, q.dtype), piece],
-        in_specs=[VM] * 2,
-        out_specs=[VM] * 2,
-        scratch_shapes=[
-            pltpu.VMEM((cols, own, wide), kv.dtype),
-            pltpu.VMEM((cols, own, wide), kv.dtype),
-            dma((2, 4)), dma((2, 4)), dma((4,)), dma((4,)),
+        functools.partial(tail_kernel, kinds),
+        out_shape=[jax.ShapeDtypeStruct((2, n, w), bf16)] * kinds
+        + [
+            jax.ShapeDtypeStruct(q.shape, q.dtype),
+            jax.ShapeDtypeStruct((cols, wide, own), kv.dtype),
+            jax.ShapeDtypeStruct(small.shape, f32),
         ],
-        compiler_params=pltpu.CompilerParams(collective_id=cid, has_side_effects=True),
-        name="to_tokens",
-    )(q, kv)
+        in_specs=[HBM] * kinds + [VM] * 3,
+        out_specs=[HBM] * kinds + [VM] * 3,
+        scratch_shapes=[pltpu.VMEM((cols, wide, own), kv.dtype)] * 2
+        + parts * 2
+        + [dma((2, 4)), dma((2, 4)), dma((4,)), dma((4,)), dma((5,)), dma((5,)), dma((5,)), dma((5,))]
+        + scatter_scratch(kinds, n, w, bf16),
+        compiler_params=pltpu.CompilerParams(
+            collective_id=cid, has_side_effects=True, vmem_limit_bytes=48 * 1024 * 1024
+        ),
+        name="tail",
+    )(*grads, q, kv, small)
+
+
+def last_kernel(kinds, *refs):
+    grads, refs = refs[:kinds], refs[kinds:]
+    give_ref, refs = refs[0], refs[1:]
+    outs, refs = refs[:kinds], refs[kinds:]
+    give_out, gl, gs, gr = refs[:4]
+    d, r, c = place()
+    greet(plane_peers(), [(c < 3, (d, r, c + 1)), (c > 0, (d, r, c - 1))])
+    start, finish = give_moves(give_ref, give_out, gl, gs, gr)
+    scatter_core(grads, outs, refs[4:], start, [])
+    finish()
+
+
+def last_fast(grads, grad_t, cid):
+    kinds = len(grads)
+    n, w = grads[0].shape[3:]
+    width, own = grad_t.shape
+    dma = pltpu.SemaphoreType.DMA
+    return pl.pallas_call(
+        functools.partial(last_kernel, kinds),
+        out_shape=[jax.ShapeDtypeStruct((2, n, w), bf16)] * kinds
+        + [jax.ShapeDtypeStruct((2, width // 4, 2 * own), bf16)],
+        in_specs=[HBM] * (kinds + 1),
+        out_specs=[HBM] * (kinds + 1),
+        scratch_shapes=[dma, dma((4,)), dma((2, 2))] + scatter_scratch(kinds, n, w, bf16),
+        compiler_params=pltpu.CompilerParams(
+            collective_id=cid, has_side_effects=True, vmem_limit_bytes=48 * 1024 * 1024
+        ),
+        name="last_sums",
+    )(*grads, grad_t.reshape(4, width // 4, own))
 
 
 def dot(a, b, contract=((1,), (0,))):
@@ -1351,7 +1501,6 @@
     ffn_out = jnp.einsum("ctn,cdn->td", act, w_back_all, preferred_element_type=f32) + b_back_a
     normed_two, inv_two = normalize(hidden_one + ffn_out)
     layer_out = (normed_two * gain_two + bias_two).astype(bf16)
-    out = give_fast(layer_out.T, 4)
 
     student_h = mm(layer_out, s_proj_all, ((1,), (0,))) + s_bias
     head_parts = student_h.reshape(own, SH, SHD)
@@ -1363,37 +1512,7 @@
     local_total = jnp.sum(local_exp, axis=0)
     local_sum = jnp.einsum("tdh,thk->dhk", local_exp, head_parts, precision=highest)
     stats = jnp.concatenate([local_top[..., None], local_total[..., None], local_sum], axis=-1)
-    stats = lax.all_gather(stats, ("dp", "col"))
-    tops, totals, sums = stats[..., 0], stats[..., 1], stats[..., 2:]
-    doc_top = jnp.max(tops, axis=0)
-    factors = jnp.exp(tops - doc_top[None])
-    doc_total = jnp.sum(totals * factors, axis=0)
-    pooled_heads = jnp.sum(sums * factors[..., None], axis=0) / doc_total[:, :, None]
-    pooled = pooled_heads.reshape(docs_count, student_width)
-    middle = jnp.tanh(jnp.dot(pooled, s_mid, precision=highest) + s_mid_bias)
-    logit_rows = jnp.dot(middle, s_cls, precision=highest) + s_cls_bias
-    logits = lax.all_gather(logit_rows, "row")
-    logits = lax.dynamic_slice_in_dim(logits, dp_index * (seqs // parts), seqs // parts)
-    logit_top = jnp.max(logit_rows, axis=-1, keepdims=True)
-    logit_exp = jnp.exp(logit_rows - logit_top)
-    one_hot = (label_seq[:, None] == class_ids[None, :]).astype(f32)
-    d_logits = logit_exp / jnp.sum(logit_exp, axis=-1, keepdims=True) - one_hot
-    g_cls = jnp.dot(middle.T, d_logits, precision=highest)
-    g_cls_bias = jnp.sum(d_logits, axis=0)
-    d_middle = jnp.dot(d_logits, s_cls.T, precision=highest) * (1.0 - middle * middle)
-    g_mid = jnp.dot(pooled.T, d_middle, precision=highest)
-    g_mid_bias = jnp.sum(d_middle, axis=0)
-    d_pooled = jnp.dot(d_middle, s_mid.T, precision=highest).reshape(docs_count, SH, SHD)
-    shares = jnp.where(member, jnp.exp(masked - doc_top[None]), 0.0) / doc_total[None]
-    d_share = jnp.einsum("dhk,thk->tdh", d_pooled, head_parts, precision=highest)
-    base_term = jnp.sum(d_pooled * pooled_heads, axis=-1)
-    d_pool_logit = jnp.sum(shares * (d_share - base_term[None]), axis=1)
-    d_heads = jnp.einsum("tdh,dhk->thk", shares, d_pooled, precision=highest)
-    d_heads = d_heads + d_pool_logit[:, :, None] * query_heads[None] * pool_scale
-    g_query = (jnp.sum(d_pool_logit[:, :, None] * head_parts, axis=0) * pool_scale).reshape(-1)
-    d_student = d_heads.reshape(own, student_width)
-    g_sbias = jnp.sum(d_student, axis=0)
-    g_sproj = jnp.dot(layer_out.astype(f32).T, d_student, precision=highest)
+    stats = jnp.pad(stats.reshape(-1), (0, 8 * 128 - stats.size)).reshape(8, 128)
 
     d_out = c_parts.reshape(width, own).T.astype(f32)
     g_ln2_gain = jnp.sum(d_out * normed_two, axis=0)
@@ -1416,9 +1535,48 @@
     d_attn = d_resid_one.astype(bf16)
     g_out_bias = jnp.sum(d_attn.astype(f32), axis=0)
     d_ctx = mm(w_out_all, d_attn, ((1,), (1,))).astype(bf16)
-    (d_ctx,) = swap_fast([d_ctx.reshape(cols, width_col, own)], 5)
+    d_ctx, stats, out = turn_fast(d_ctx.reshape(cols, width_col, own), stats, layer_out.T, 4)
+
+    stats = stats.reshape(cols * parts, -1)[:, : docs_count * SH * (SHD + 2)]
+    stats = stats.reshape(cols * parts, docs_count, SH, SHD + 2)
+    tops, totals, sums = stats[..., 0], stats[..., 1], stats[..., 2:]
+    doc_top = jnp.max(tops, axis=0)
+    factors = jnp.exp(tops - doc_top[None])
+    doc_total = jnp.sum(totals * factors, axis=0)
+    pooled_heads = jnp.sum(sums * factors[..., None], axis=0) / doc_total[:, :, None]
+    pooled = pooled_heads.reshape(docs_count, student_width)
+    middle = jnp.tanh(jnp.dot(pooled, s_mid, precision=highest) + s_mid_bias)
+    logit_rows = jnp.dot(middle, s_cls, precision=highest) + s_cls_bias
+    logit_top = jnp.max(logit_rows, axis=-1, keepdims=True)
+    logit_exp = jnp.exp(logit_rows - logit_top)
+    one_hot = (label_seq[:, None] == class_ids[None, :]).astype(f32)
+    d_logits = logit_exp / jnp.sum(logit_exp, axis=-1, keepdims=True) - one_hot
+    g_cls = jnp.dot(middle.T, d_logits, precision=highest)
+    g_cls_bias = jnp.sum(d_logits, axis=0)
+    d_middle = jnp.dot(d_logits, s_cls.T, precision=highest) * (1.0 - middle * middle)
+    g_mid = jnp.dot(pooled.T, d_middle, precision=highest)
+    g_mid_bias = jnp.sum(d_middle, axis=0)
+    d_pooled = jnp.dot(d_middle, s_mid.T, precision=highest).reshape(docs_count, SH, SHD)
+    shares = jnp.where(member, jnp.exp(masked - doc_top[None]), 0.0) / doc_total[None]
+    d_share = jnp.einsum("dhk,thk->tdh", d_pooled, head_parts, precision=highest)
+    base_term = jnp.sum(d_pooled * pooled_heads, axis=-1)
+    d_pool_logit = jnp.sum(shares * (d_share - base_term[None]), axis=1)
+    d_heads = jnp.einsum("tdh,dhk->thk", shares, d_pooled, precision=highest)
+    d_heads = d_heads + d_pool_logit[:, :, None] * query_heads[None] * pool_scale
+    g_query = (jnp.sum(d_pool_logit[:, :, None] * head_parts, axis=0) * pool_scale).reshape(-1)
+    d_student = d_heads.reshape(own, student_width)
+    g_sbias = jnp.sum(d_student, axis=0)
+    g_sproj = jnp.dot(layer_out.astype(f32).T, d_student, precision=highest)
+
+    d_q, d_kv = attn_bwd(bounds, queries, kv, q_rows, k_rows, lse, context, d_ctx, score_scale)
+    at_seq = (jnp.arange(seqs) == row_index).astype(f32)[:, None]
+    at_heads = (jnp.arange(cols) == col_index).astype(f32)[:, None, None]
+    g_q_bias = jnp.sum(d_q.astype(f32), axis=(0, 2))
+    g_v_bias = jnp.sum(d_kv[:, width_col:].astype(f32), axis=(0, 2))
     once = 1.0 / (parts * cols)
     small = (
+        g_sproj,
+        jnp.stack([g_q_bias, g_v_bias])[None] * at_heads,
         g_in_bias,
         g_out_bias,
         g_ln1_gain,
@@ -1426,39 +1584,41 @@
         g_back_bias,
         g_ln2_gain,
         g_ln2_bias,
-        g_sproj,
         g_sbias,
         g_query,
         g_mid * once,
         g_mid_bias * once,
         g_cls * once,
+        logit_rows.reshape(1, -1) * (at_seq * once),
         g_cls_bias * once,
     )
-    small = lax.psum(small, WORLD)
-    d_q, d_kv = attn_bwd(bounds, queries, kv, q_rows, k_rows, lse, context, d_ctx, score_scale)
-    d_q, d_kv = tokens_fast(d_q, d_kv.reshape(cols, parts, 2 * width_col, own), 6)
+    flat = jnp.concatenate([part.reshape(-1) for part in small])
+    tall = -(-flat.shape[0] // (128 * 256)) * 256
+    flat = jnp.pad(flat, (0, tall * 128 - flat.shape[0])).reshape(tall, 128)
+    blocked = (cols, rows, parts, width_row // parts, -1)
+    g_in, g_back, d_q, d_kv, flat = tail_fast(
+        [g_in.astype(bf16).reshape(blocked), g_back.astype(bf16).reshape(blocked)],
+        d_q,
+        d_kv.reshape(cols, parts, 2 * width_col, own),
+        flat,
+        5,
+    )
+    flat = flat.reshape(-1)
+    sums_all, at = [], 0
+    for part in small:
+        sums_all.append(flat[at : at + part.size].reshape(part.shape))
+        at += part.size
     d_qkv = jnp.concatenate([d_kv, d_q], axis=1)
-    g_qkv_bias = jnp.sum(d_qkv.astype(f32), axis=2)
-    g_qkv_bias, small = lax.optimization_barrier((g_qkv_bias, small))
-    g_qkv_bias = lax.psum(g_qkv_bias[:, width_col:], WORLD)
     g_qkv = jnp.einsum("dt,cnt->cdn", x_t, d_qkv, preferred_element_type=f32)
     d_tokens = jnp.einsum("cdn,cnt->dt", w_qkv_all, d_qkv, preferred_element_type=f32)
     d_tokens = (d_tokens + d_resid_one.T).astype(bf16)
-    grad_tokens = give_fast(d_tokens, 7).astype(f32)
-
     g_out = mm(ctx_t, d_attn, ((1,), (0,)))
     g_out = g_out.reshape(cols, width_col, rows, width_row).transpose(0, 2, 1, 3)
     g_attn = jnp.concatenate(
         [g_qkv.astype(bf16).reshape(cols, rows, width_row, 3 * width_col), g_out.astype(bf16)], axis=-1
     )
-    blocked = (cols, rows, parts, width_row // parts, -1)
-    g_in, g_back, g_attn = [
-        part.reshape(width_row, -1).astype(f32)
-        for part in scatter_fast(
-            [g_in.astype(bf16).reshape(blocked), g_back.astype(bf16).reshape(blocked), g_attn.reshape(blocked)],
-            8,
-        )
-    ]
+    g_attn, grad_tokens = last_fast([g_attn.reshape(blocked)], d_tokens, 6)
+    g_in, g_back, g_attn = [part.reshape(width_row, -1).astype(f32) for part in (g_in, g_back, g_attn)]
     g_qkv = g_attn[:, : 3 * width_col].reshape(width_row, 3, heads_dev, HD)
     g_qkv = jnp.stack([g_qkv[:, 2], g_qkv[:, 0], g_qkv[:, 1]], axis=2).reshape(width_row, -1)
 
@@ -1468,25 +1628,35 @@
     def at_row(part):
         return lax.dynamic_slice_in_dim(part, row_index * width_row, width_row)
 
-    bias_grad = at_col(g_qkv_bias)
+    (
+        g_sproj, g_qkv_bias, g_in_bias, g_out_bias, g_ln1_gain, g_ln1_bias, g_back_bias, g_ln2_gain,
+        g_ln2_bias, g_sbias, g_query, g_mid, g_mid_bias, g_cls, logits, g_cls_bias,
+    ) = sums_all
+    logits = lax.dynamic_slice_in_dim(logits, dp_index * (seqs // parts), seqs // parts)
     return (
         out,
-        logits,
-        grad_tokens,
+        logits.reshape(seqs // parts, docs_count, class_count),
+        grad_tokens.astype(f32),
         g_qkv,
-        jnp.stack([bias_grad[width_col:], bias_grad[:width_col]]),
+        at_col(g_qkv_bias),
         g_attn[:, 3 * width_col :],
-        at_row(small[1]),
-        at_row(small[2]),
-        at_row(small[3]),
+        at_row(g_out_bias),
+        at_row(g_ln1_gain),
+        at_row(g_ln1_bias),
         g_in,
-        at_col(small[0]),
+        at_col(g_in_bias),
         g_back,
-        at_row(small[4]),
-        at_row(small[5]),
-        at_row(small[6]),
-        at_row(small[7]),
-    ) + tuple(small[8:])
+        at_row(g_back_bias),
+        at_row(g_ln2_gain),
+        at_row(g_ln2_bias),
+        at_row(g_sproj),
+        g_sbias,
+        g_query,
+        g_mid,
+        g_mid_bias,
+        g_cls,
+        g_cls_bias,
+    )
 
 
 def solution(mesh):

time: 570 us -> 426 us (0.75)
  blocking collectives: 116 us -> 0 us
  between operations: 15.4 us -> 2.15 us
  Pallas kernels: 292 us -> 281 us
    psum x2 -> x0, blocking collectives: 82.9 us -> none  [the longest x1 43.7 us: fast_local(): small = lax.psum(small, WORLD)]
    all_gather x2 -> x0, blocking collectives: 32.7 us -> none  [the longest x1 24.3 us: fast_local(): stats = lax.all_gather(stats, ('dp', 'col'))]
    pallas_call x2 -> x1, Pallas kernels: 26.7 us -> 12.7 us  [swap_fast(): pl.pallas_call(functools.partial(swap_kernel, count), out_shape=[jax.Shap...]
    unnamed x130 -> x123, local copies, waits for them, and re-layouts: 13.5 us -> 11.1 us
    pallas_call x4 -> x3, Pallas kernels: 123 us -> 124 us  [the longest x1 66.6 us: tail_fast(): pl.pallas_call(functools.partial(tail_kernel, kinds), out_shape=[jax.Shap...]
  transfers between devices with their start and end apart: 1 -> 0, of which waited for: 0 -> 0; matrix products, arithmetic and copies ran while one was open for 10% -> 0% of each run, Pallas kernels for 26% -> 0%
where the time goes in v3:
time: 426 us; the launch traced here: 418 us
  Pallas kernels  281 us (66%)
  local copies, waits for them, and re-layouts  62.1 us (15%)
  matrix products  49.6 us (12%)
  other arithmetic  23.5 us (6%)
    pallas_call x1, Pallas kernels, gather_fast(): pl.pallas_call(functools.partial(gather_kernel, kinds), out_shape=[jax.Sh...  87.7 us
    pallas_call x1, Pallas kernels, tail_fast(): pl.pallas_call(functools.partial(tail_kernel, kinds), out_shape=[jax.Shap...  66.6 us
    pallas_call x1, Pallas kernels, last_fast(): pl.pallas_call(functools.partial(last_kernel, kinds), out_shape=[jax.Shap...  42 us
    pallas_call x1, Pallas kernels, heads_fast(): pl.pallas_call(heads_kernel, out_shape=[jax.ShapeDtypeStruct(q.shape, q.d...  32.8 us
    pallas_call x1, Pallas kernels, turn_fast(): pl.pallas_call(turn_kernel, out_shape=[jax.ShapeDtypeStruct(d_ctx.shape,...  15.1 us
    pallas_call x1, Pallas kernels, attn_bwd(): pl.pallas_call(functools.partial(attn_bwd_kernel, heads, scale), out_shap...  13.8 us
    pallas_call x1, Pallas kernels, swap_fast(): pl.pallas_call(functools.partial(swap_kernel, count), out_shape=[jax.Shap...  12.7 us
    unnamed x123, local copies, waits for them, and re-layouts  11.1 us

profile of v3, /device:TPU:0, one launch (start us, length us, event | category | flops | bytes accessed | tf_op | source)
XLA Modules:
  0.0 418.4 jit_solution(13302026563719491540)
XLA Ops:
  2.5 0.8 reshape.467
  3.2 1.3 pad_add_fusion.refs_6_
  5.3 0.9 concatenate.34
  7.5 1.6 constant_dynamic-slice_fusion.7.refs_3_
  9.0 1.1 copy.260
  10.4 0.8 fusion.50.refs_0_
  11.2 87.7 %gather_all.1 = (bf16[4,4,2,96,768]{4,3,2,1,0:T(8,128)(2,1)}, f32[4,4,2,48,128]{4,3,2,1,0:T(8,128)}, bf16[4,4,2,96,768]{4,3,2,1,0:T(8,128)(2,1)}, bf16[4,4,2,96,...) custom-call(bf16[96,768]{1,0:T(8,128)(2,1)} %fusion.50.refs_0_, ...), custom_call_target="tpu_custom_call" | custom-call | tf_op jit(solution)/shard_map/gather_all/pallas_call | solution.py:660
  98.9 1.3 convert_reduce_fusion.5
  100.9 0.8 reshape.474
  104.3 1.2 copy.265
  105.5 1.6 reshape.476
  109.1 0.9 reshape.530.kseg_ref
  110.0 3.5 fusion.22
  113.5 0.8 slice.256.q_ref
  114.3 0.9 slice.257.kv_ref
  115.2 32.8 %to_heads.1 = (bf16[4,192,256]{2,1,0:T(8,128)(2,1)}, bf16[4,2,384,256]{3,2,1,0:T(8,128)(2,1)}) custom-call(bf16[4,192,256]{2,1,0:T(8,128)(2,1)} %slice.256.q_ref, bf16[4,384,256]{2,1,0:T(8,128)(2,1)} %slice.257.kv_ref), custom_call_target="tpu_custom_call" | custom-call | tf_op jit(solution)/shard_map/to_heads/pallas_call | solution.py:988
  148.0 1.4 copy-done.2
  149.4 1.0 copy-done.6
  150.4 10.3 %attn_fwd.1 = (bf16[4,192,256]{2,1,0:T(8,128)(2,1)S(1)}, f32[4,1,768]{2,1,0:T(1,128)S(1)}) custom-call(s32[4,2]{1,0:T(4,128)S(1)} %pad_add_fusion.1.bounds, bf16[4,192,256]{2,1,0:T(8,128)(2,1)S(1)} %copy-done.6, bf16[8,384,256]{2,1,0:T(8,128)(2,1)S(1)} %bitcast.364, s32[4,1,256]{2,1,0:T(1,128)S(1)} %constant_dynamic-slice_fusion.6.qseg_ref, ...), custom_call_target="tpu_custom_call" | custom-call | tf_op jit(solution)/shard_map/attn_fwd/pallas_call | solution.py:1275
  161.4 12.7 %swap_cols.1 = bf16[4,192,256]{2,1,0:T(8,128)(2,1)} custom-call(bf16[4,192,256]{2,1,0:T(8,128)(2,1)} %copy-done.8), custom_call_target="tpu_custom_call" | custom-call | tf_op jit(solution)/shard_map/swap_cols/pallas_call | solution.py:942
  174.1 2.1 slice_bitcast_fusion
  176.2 4.3 %slice.252 = bf16[4,4,192,576]{3,2,1,0:T(8,128)(2,1)} slice(bf16[4,4,192,768]{3,2,1,0:T(8,128)(2,1)} %bitcast.375), slice={[0:4], [0:4], [0:192], [0:576]} | slice | bytes 7077888 | tf_op jit(solution)/shard_map/slice | solution.py:1458
  180.6 2.4 copy.264
  183.0 4.0 reshape.472
  187.0 2.8 fusion.100
  190.1 10.2 %fusion.9 = (bf16[4,256,768]{2,1,0:T(8,128)(2,1)S(1)}, f32[4,256,768]{2,1,0:T(8,128)S(1)}, f32[4,768,256]{1,2,0:T(8,128)S(1)}) fusion(f32[4,768]{1,0:T(4,128)S(1)} %bitcast.400, bf16[4,768,768]{2,1,0:T(8,128)(2,1)} %bitcast.407, f32[256,768]{1,0:T(8,128)S(1)} %get-tuple-element.229, f32[768]{0:T(1024)S(1)} %add.241, f32[768]{0:T(1024)S(1)} %mul.353, ...), kind=kOutput, calls=%fused_computation.20 | convolution fusion | flops 1260847104 | bytes 13389824 | tf_op jit(solution)/shard_map/td,cdn->ctn/dot_general | solution.py:1498
  200.3 2.4 fusion.97
  203.0 1.0 fusion.41
  204.0 1.0 multiply_reduce_fusion.6
  205.2 0.9 convert_reduce_fusion.2
  206.1 2.2 convert_reduce_fusion
  208.4 3.3 multiply_reduce_fusion
  211.8 3.6 fusion.95
  215.5 0.9 convert_reduce_fusion.3
  216.4 1.3 convolution_convert_fusion.3
  217.6 1.9 copy.297
  219.8 1.2 convolution_bitcast_fusion.5
  221.7 0.9 copy.281
  222.6 15.1 %turn.1 = (bf16[4,192,256]{2,1,0:T(8,128)(2,1)}, f32[2,4,8,128]{3,2,1,0:T(8,128)}, bf16[2,192,512]{2,1,0:T(8,128)(2,1)}) custom-call(bf16[4,192,256]{2,1,0:T(8,128)(2,1)} %bitcast.391, f32[8,128]{1,0:T(8,128)} %pad_bitcast_fusion.2.stats_ref, bf16[4,192,256]{2,1,0:T(8,128)(2,1)} %bitcast.384), custom_call_target="tpu_custom_call" | custom-call | tf_op jit(solution)/shard_map/turn/pallas_call | solution.py:1031
  237.8 1.0 copy-done.9
  238.8 1.0 copy-done.10
  239.8 13.8 %attn_bwd.1 = (bf16[4,192,256]{2,1,0:T(8,128)(2,1)S(1)}, bf16[8,384,256]{2,1,0:T(8,128)(2,1)S(1)}) custom-call(s32[4,2]{1,0:T(4,128)S(1)} %pad_add_fusion.1.bounds, bf16[4,192,256]{2,1,0:T(8,128)(2,1)S(1)} %copy-done.7, bf16[8,384,256]{2,1,0:T(8,128)(2,1)S(1)} %bitcast.365, s32[4,1,256]{2,1,0:T(1,128)S(1)} %constant_dynamic-slice_fusion.6.qseg_ref, ...), custom_call_target="tpu_custom_call" | custom-call | tf_op jit(solution)/shard_map/attn_bwd/pallas_call | solution.py:1365
  254.0 1.2 copy-done.4
  257.5 0.8 fusion.31
  258.3 1.0 fusion.105
  261.1 0.9 fusion.107
  262.1 0.9 convolution_multiply_fusion.1
  263.6 1.1 fusion.30
  264.7 1.0 fusion.51
  267.4 1.7 concatenate.38
  269.2 1.8 convolution_convert_fusion.2
  271.0 3.7 convolution_convert_fusion.1
  274.7 3.6 convolution_convert_fusion
  278.3 66.6 %tail.1 = (bf16[2,96,768]{2,1,0:T(8,128)(2,1)S(1)}, bf16[2,96,768]{2,1,0:T(8,128)(2,1)S(1)}, bf16[4,192,256]{2,1,0:T(8,128)(2,1)S(1)}, bf16[4,384,256]{2,1,0:T(8,128)(2,1)S(1)}, f32[1024,128]{1,0:T(8,128)S(1)}) custom-call(bf16[4,4,2,96,768]{4,3,2,1,0:T(8,128)(2,1)} %bitcast.370, bf16[4,4,2,96,768]{4,3,2,1,0:T(8,128)(2,1)} %bitcast.371, ...), custom_call_target="tpu_custom_call" | custom-call | tf_op jit(solution)/shard_map/tail/pallas_call | solution.py:1163
  354.2 3.6 fusion.25
  358.0 0.9 bitcast_convert_fusion.1
  358.9 0.9 bitcast_convert_fusion
  359.7 2.9 convert_bitcast_fusion
  362.6 6.1 %copy.295 = bf16[4,768,576]{2,1,0:T(8,128)(2,1)} copy(bf16[4,768,576]{1,2,0:T(8,128)(2,1)} %convert_bitcast_fusion) | data formatting | bytes 7077888 | tf_op jit(solution)/shard_map/convert_element_type | solution.py:1618
  368.7 3.3 pad_maximum_fusion.refs_0_
  372.0 42.0 %last_sums.1 = (bf16[2,96,768]{2,1,0:T(8,128)(2,1)S(1)}, bf16[2,192,512]{2,1,0:T(8,128)(2,1)S(1)}) custom-call(bf16[4,4,2,96,768]{4,3,2,1,0:T(8,128)(2,1)S(1)} %pad_maximum_fusion.refs_0_, bf16[4,192,256]{2,1,0:T(8,128)(2,1)S(1)} %bitcast.367), custom_call_target="tpu_custom_call" | custom-call | tf_op jit(solution)/shard_map/last_sums/pallas_call | solution.py:1201
  414.0 1.0 convert_element_type.183
  415.1 0.8 slice.276
  416.3 1.0 copy.304
  (251 shorter events, 29.0 us)
Async XLA Ops:
  0.7 6.1 %copy-start = (bf16[192,768]{1,0:T(8,128)(2,1)S(1)}, bf16[192,768]{1,0:T(8,128)(2,1)}, u32[]{:S(2)}) copy-start(bf16[192,768]{1,0:T(8,128)(2,1)} %param.33) | copy-start | bytes 884740
  0.7 9.7 %copy-start.37 = (bf16[192,192]{1,0:T(8,128)(2,1)S(1)}, bf16[192,192]{1,0:T(8,128)(2,1)}, u32[]{:S(2)}) copy-start(bf16[192,192]{1,0:T(8,128)(2,1)} %param.29) | copy-start | bytes 221188
  2.5 201.5 %copy-start.49 = (f32[2,64]{1,0:T(2,128)}, f32[2,64]{1,0:T(2,128)S(1)}, u32[]{:S(2)}) copy-start(f32[2,64]{1,0:T(2,128)S(1)} %mul.384) | copy-start | bytes 1540
  98.9 10.0 %copy-start.30 = (bf16[4,192,256]{2,1,0:T(8,128)(2,1)S(1)}, bf16[4,192,256]{2,1,0:T(8,128)(2,1)}, u32[]{:S(2)}) copy-start(bf16[4,192,256]{2,1,0:T(8,128)(2,1)} %get-tuple-element.54) | copy-start | bytes 1179652
  100.9 9.1 %copy-start.26 = (bf16[4,192,256]{2,1,0:T(8,128)(2,1)S(1)}, bf16[4,192,256]{2,1,0:T(8,128)(2,1)}, u32[]{:S(2)}) copy-start(bf16[4,192,256]{2,1,0:T(8,128)(2,1)} %get-tuple-element.46) | copy-start | bytes 1179652
  105.5 81.5 %copy-start.18 = (bf16[768,256]{0,1:T(8,128)(2,1)}, bf16[768,256]{0,1:T(8,128)(2,1)S(1)}, u32[]{:S(2)}) copy-start(bf16[768,256]{0,1:T(8,128)(2,1)S(1)} %copy.265) | copy-start | bytes 1179652
  148.0 1.4 copy-start.2
  149.4 1.0 copy-start.6
  160.7 0.7 copy-start.8
  180.6 6.4 %copy-start.16 = (bf16[4,192,256]{2,1,0:T(8,128)(2,1)S(1)}, bf16[4,192,256]{2,1,0:T(8,128)(2,1)}, u32[]{:S(2)}) copy-start(bf16[4,192,256]{2,1,0:T(8,128)(2,1)} %swap_cols.1) | copy-start | bytes 1179652
  187.0 13.3 %slice-start.2 = ((s8[4718592]{0:T(1024)(128)(4,1)}), s8[4194304]{0:T(1024)(128)(4,1)S(1)}, s32[]{:S(2)}) async-start(s8[4718592]{0:T(1024)(128)(4,1)} %bitcast.411), calls=%async_computation.2 | async-start | bytes 8388608
  189.8 18.5 %copy-start.11 = (f32[256,768]{1,0:T(8,128)}, f32[256,768]{1,0:T(8,128)S(1)}, u32[]{:S(2)}) copy-start(f32[256,768]{1,0:T(8,128)S(1)} %get-tuple-element.229) | copy-start | bytes 2359300
  189.8 25.6 %copy-start.39 = (f32[256]{0:T(256)}, f32[256]{0:T(256)S(1)}, u32[]{:S(2)}) copy-start(f32[256]{0:T(256)S(1)} %broadcast_multiply_fusion.8) | copy-start | bytes 3076
  190.1 25.3 %copy-start.44 = (f32[256]{0:T(256)}, f32[256]{0:T(256)S(1)}, u32[]{:S(2)}) copy-start(f32[256]{0:T(256)S(1)} %add_rsqrt_fusion.1) | copy-start | bytes 3076
  190.1 10.2 %slice-start.3 = ((s8[4718592]{0:T(1024)(128)(4,1)}), s8[524288]{0:T(1024)(128)(4,1)S(1)}, s32[]{:S(2)}) async-start(s8[4718592]{0:T(1024)(128)(4,1)} %bitcast.411), calls=%async_computation.3 | async-start | bytes 1048576
  200.3 2.5 copy-start.24
  200.3 3.7 copy-start.33
  200.3 3.7 copy-start.51
  204.0 2.1 copy-start.20
  205.2 3.2 slice-start
  206.1 2.3 copy-start.22
  206.1 2.3 slice-start.1
  208.4 3.4 copy-start.31
  208.4 3.4 copy-start.19
  211.8 3.7 copy-start.12
  211.8 3.7 copy-start.34
  211.8 4.5 %copy-start.15 = (bf16[768,768]{1,0:T(8,128)(2,1)S(1)}, bf16[768,768]{1,0:T(8,128)(2,1)}, u32[]{:S(2)}) copy-start(bf16[768,768]{1,0:T(8,128)(2,1)} %reshape.472) | copy-start | bytes 3538948
  215.4 6.3 %copy-start.29 = (bf16[768,256]{0,1:T(8,128)(2,1)S(1)}, bf16[768,256]{0,1:T(8,128)(2,1)}, u32[]{:S(2)}) copy-start(bf16[768,256]{0,1:T(8,128)(2,1)} %get-tuple-element.232) | copy-start | bytes 1179652
  215.5 22.3 %copy-start.3 = (bf16[4,2,384,256]{3,2,1,0:T(8,128)(2,1)S(1)}, bf16[4,2,384,256]{3,2,1,0:T(8,128)(2,1)}, u32[]{:S(2)}) copy-start(bf16[4,2,384,256]{3,2,1,0:T(8,128)(2,1)} %get-tuple-element.50) | copy-start | bytes 4718596
  215.5 22.3 %copy-start.7 = (bf16[4,192,256]{2,1,0:T(8,128)(2,1)S(1)}, bf16[4,192,256]{2,1,0:T(8,128)(2,1)}, u32[]{:S(2)}) copy-start(bf16[4,192,256]{2,1,0:T(8,128)(2,1)} %get-tuple-element.49.q_ref) | copy-start | bytes 1179652
  222.6 34.9 %copy-start.36 = (f32[128,128]{1,0:T(8,128)S(1)}, f32[128,128]{1,0:T(8,128)}, u32[]{:S(2)}) copy-start(f32[128,128]{1,0:T(8,128)} %param.42) | copy-start | bytes 196612
  237.8 1.0 copy-start.9
  238.8 1.0 copy-start.10
  239.8 16.2 %copy-start.38 = (f32[2,4,8,128]{3,2,1,0:T(8,128)S(1)}, f32[2,4,8,128]{3,2,1,0:T(8,128)}, u32[]{:S(2)}) copy-start(f32[2,4,8,128]{3,2,1,0:T(8,128)} %get-tuple-element.60) | copy-start | bytes 98308
  253.6 12.7 %copy-start.50 = (f32[2,64]{1,0:T(2,128)S(1)}, f32[2,64]{1,0:T(2,128)}, u32[]{:S(2)}) copy-start(f32[2,64]{1,0:T(2,128)} %copy-done.49) | copy-start | bytes 1540
  253.6 13.2 %copy-start.21 = (bf16[256,768]{1,0:T(8,128)(2,1)S(1)}, bf16[256,768]{1,0:T(8,128)(2,1)}, u32[]{:S(2)}) copy-start(bf16[256,768]{1,0:T(8,128)(2,1)} %copy-done.20) | copy-start | bytes 1179652
  253.6 13.8 %copy-start.41 = (f32[768]{0:T(1024)S(1)}, f32[768]{0:T(1024)}, u32[]{:S(2)}) copy-start(f32[768]{0:T(1024)} %get-tuple-element.200) | copy-start | bytes 9220
  253.6 13.8 %copy-start.42 = (f32[768]{0:T(1024)S(1)}, f32[768]{0:T(1024)}, u32[]{:S(2)}) copy-start(f32[768]{0:T(1024)} %get-tuple-element.219) | copy-start | bytes 9220
  253.6 13.8 %copy-start.43 = (f32[768]{0:T(1024)S(1)}, f32[768]{0:T(1024)}, u32[]{:S(2)}) copy-start(f32[768]{0:T(1024)} %get-tuple-element.221) | copy-start | bytes 9220
  253.6 13.8 %copy-start.46 = (f32[768]{0:T(1024)S(1)}, f32[768]{0:T(1024)}, u32[]{:S(2)}) copy-start(f32[768]{0:T(1024)} %reduce_sum.303) | copy-start | bytes 9220
  253.6 13.8 %copy-start.47 = (f32[768]{0:T(1024)S(1)}, f32[768]{0:T(1024)}, u32[]{:S(2)}) copy-start(f32[768]{0:T(1024)} %get-tuple-element.202) | copy-start | bytes 9220
  253.7 13.8 %copy-start.48 = (f32[768]{0:T(1024)S(1)}, f32[768]{0:T(1024)}, u32[]{:S(2)}) copy-start(f32[768]{0:T(1024)} %get-tuple-element.206) | copy-start | bytes 9220
  253.7 15.5 %copy-start.17 = (bf16[4,192,256]{2,1,0:T(8,128)(2,1)S(1)}, bf16[4,192,256]{2,1,0:T(8,128)(2,1)}, u32[]{:S(2)}) copy-start(bf16[4,192,256]{2,1,0:T(8,128)(2,1)} %swap_cols.1) | copy-start | bytes 1179652
  253.7 15.5 %copy-start.28 = (bf16[768,256]{1,0:T(8,128)(2,1)S(1)}, bf16[768,256]{1,0:T(8,128)(2,1)}, u32[]{:S(2)}) copy-start(bf16[768,256]{1,0:T(8,128)(2,1)} %copy.297) | copy-start | bytes 1179652
  254.0 1.2 copy-start.4
  263.0 8.0 %copy-start.13 = (f32[256,768]{1,0:T(8,128)S(1)}, f32[256,768]{1,0:T(8,128)}, u32[]{:S(2)}) copy-start(f32[256,768]{1,0:T(8,128)} %copy-done.11) | copy-start | bytes 2359300
  263.0 8.0 %copy-start.40 = (f32[256]{0:T(256)S(1)}, f32[256]{0:T(256)}, u32[]{:S(2)}) copy-start(f32[256]{0:T(256)} %copy-done.39) | copy-start | bytes 3076
  263.0 8.0 %copy-start.45 = (f32[256]{0:T(256)S(1)}, f32[256]{0:T(256)}, u32[]{:S(2)}) copy-start(f32[256]{0:T(256)} %copy-done.44) | copy-start | bytes 3076
  269.1 1.9 copy-start.32
  271.0 3.7 copy-start.23
  271.0 3.7 copy-start.25
  274.7 3.6 copy-start.5
  354.2 5.5 %copy-start.27 = (bf16[4,192,256]{2,1,0:T(8,128)(2,1)S(1)}, bf16[4,192,256]{2,1,0:T(8,128)(2,1)}, u32[]{:S(2)}) copy-start(bf16[4,192,256]{2,1,0:T(8,128)(2,1)} %get-tuple-element.46) | copy-start | bytes 1179652
  362.6 6.1 %copy-start.14 = (bf16[4,192,4,192]{3,1,2,0:T(8,128)(2,1)S(1)}, bf16[4,192,4,192]{3,1,2,0:T(8,128)(2,1)}, u32[]{:S(2)}) copy-start(bf16[4,192,4,192]{3,1,2,0:T(8,128)(2,1)} %convolution_convert_fusion.2) | copy-start | bytes 3538948
  415.9 1.4 copy-start.35
  415.9 2.2 copy-start.1
